TPU v7x, 32 devices: a whole 2x2x4 slice. The times are simulated.
32 devices in a mesh: dp: 2 (over x), expert: 16 (over z, y, core).
Axes of the slice: x: 2, y: 2, z: 4, core: 2. Of those that a mesh axis runs over, the one named last changes fastest.
Arguments:
- inputs: bfloat16 [4, 1024, 2048], P('dp', 'expert'), may hold values from -6 to 6
- segments: int32 [4, 1024], P('dp'), may hold values from 0 to 2, never falling along the last dimension, each value on 1 to 800 neighbouring positions
- expert_picks: int32 [4, 1024, 6], P('dp', 'expert'), may hold values from 0 to 15, all different within a row
- priority: int32 [4, 1024], P('dp', 'expert'), may hold values from 0 to 1023, each once within a row
- cotangent: bfloat16 [4, 1024, 2048], P('dp', 'expert'), may hold values from -6 to 6
- query_weight: bfloat16 [2048, 3072], P(('dp', 'expert')), may hold values from -0.125 to 0.125
- latent_down: bfloat16 [2048, 576], P(('dp', 'expert')), may hold values from -0.125 to 0.125
- latent_up: bfloat16 [512, 4096], P(('dp', 'expert')), may hold values from -0.25 to 0.25
- output_weight: bfloat16 [2048, 2048], P(None, ('dp', 'expert')), may hold values from -0.75 to 0.75
- attn_gain: bfloat16 [2048], P(('dp', 'expert')), may hold values from 0.25 to 1.75
- latent_gain: bfloat16 [512], P(('dp', 'expert')), may hold values from 0.25 to 1.75
- router_weight: bfloat16 [2048, 16], P(('dp', 'expert')), may hold values from -0.25 to 0.25
- shared_gate: bfloat16 [2048, 2816], P(('dp', 'expert')), may hold values from -0.125 to 0.125
- shared_up: bfloat16 [2048, 2816], P(('dp', 'expert')), may hold values from -0.125 to 0.125
- shared_down: bfloat16 [2816, 2048], P(('dp', 'expert')), may hold values from -0.21875 to 0.21875
- moe_gain: bfloat16 [2048], P(('dp', 'expert')), may hold values from 0.25 to 1.75
- expert_gate: bfloat16 [16, 2048, 1408], P('expert', 'dp'), may hold values from -0.125 to 0.125
- expert_up: bfloat16 [16, 2048, 1408], P('expert', 'dp'), may hold values from -0.125 to 0.125
- expert_down: bfloat16 [16, 1408, 2048], P('expert', 'dp'), may hold values from -0.625 to 0.625
Outputs:
- outputs: bfloat16 [4, 1024, 2048], P('dp', 'expert')
- input_grad: bfloat16 [4, 1024, 2048], P('dp', 'expert')
- query_weight_grad: float32 [2048, 3072], P(('dp', 'expert'))
- latent_down_grad: float32 [2048, 576], P(('dp', 'expert'))
- latent_up_grad: float32 [512, 4096], P(('dp', 'expert'))
- output_weight_grad: float32 [2048, 2048], P(None, ('dp', 'expert'))
- attn_gain_grad: float32 [2048], P(('dp', 'expert'))
- latent_gain_grad: float32 [512], P(('dp', 'expert'))
- router_weight_grad: float32 [2048, 16], P(('dp', 'expert'))
- shared_gate_grad: float32 [2048, 2816], P(('dp', 'expert'))
- shared_up_grad: float32 [2048, 2816], P(('dp', 'expert'))
- shared_down_grad: float32 [2816, 2048], P(('dp', 'expert'))
- moe_gain_grad: float32 [2048], P(('dp', 'expert'))
- expert_gate_grad: float32 [16, 2048, 1408], P('expert', 'dp')
- expert_up_grad: float32 [16, 2048, 1408], P('expert', 'dp')
- expert_down_grad: float32 [16, 1408, 2048], P('expert', 'dp')
Inputs may be any that keep to these rules, and one draw needn't show every extreme that they name: `segments`: along each sequence the segment numbers never fall; a document has 1 to 800 tokens and some document has exactly 800. `expert_picks`: each token names 6 different experts; every expert is named by some token. `priority`: in each sequence every number of 0 to 1023 appears once.
All inputs are finite; a program needn't handle non-finite values.
Results may differ from a plain program's by a relative error of at most 0.024.
Values may be sent and summed in bfloat16 or wider, within the bound.
A program may use at most 448 MiB of HBM per device.

v0:
```python
import math

import jax
import jax.numpy as jnp
from jax import lax
from jax.sharding import PartitionSpec as P

D = 2048
HEADS = 16
HD = 128
RD = 64
VD = 128
RANK = 512
TOP = 6
EXP_DEV = 1
MICRO = 2


epsilon = 1e-06
highest = lax.Precision.HIGHEST
masked_score = -1e30


def product(left, right):
    return jnp.dot(left, right, preferred_element_type=jnp.float32)


def left_product(left, right):
    return lax.dot_general(
        left, right, (((0,), (0,)), ((), ())), preferred_element_type=jnp.float32
    )


def right_product(left, right):
    return lax.dot_general(
        left, right, (((1,), (1,)), ((), ())), preferred_element_type=jnp.float32
    )


def exact_left(left, right):
    return lax.dot_general(
        left, right, (((0,), (0,)), ((), ())), precision=highest, preferred_element_type=jnp.float32
    )


def norm_parts(values):
    factor = lax.rsqrt(jnp.mean(values * values, axis=-1, keepdims=True) + epsilon)
    return (values * factor, factor)


def norm_back(grad_normed, normed, factor):
    return factor * (grad_normed - normed * jnp.mean(grad_normed * normed, axis=-1, keepdims=True))


def angle_tables(positions, width, depth):
    half_width = width // 2
    freqs = jnp.power(10000.0, -2.0 * jnp.arange(half_width, dtype=jnp.float32) / width)
    angles = positions.astype(jnp.float32)[:, None] * freqs[None, :]
    cosine = jnp.cos(angles)
    sine = jnp.sin(angles)
    if depth == 3:
        cosine = cosine[:, None, :]
        sine = sine[:, None, :]
    return (cosine, sine)


def rotate(values, positions):
    half_width = values.shape[-1] // 2
    cosine, sine = angle_tables(positions, values.shape[-1], values.ndim)
    first = values[..., :half_width]
    second = values[..., half_width:]
    return jnp.concatenate(
        [first * cosine - second * sine, second * cosine + first * sine], axis=-1
    )


def unrotate(grads, positions):
    half_width = grads.shape[-1] // 2
    cosine, sine = angle_tables(positions, grads.shape[-1], grads.ndim)
    first = grads[..., :half_width]
    second = grads[..., half_width:]
    return jnp.concatenate(
        [first * cosine + second * sine, second * cosine - first * sine], axis=-1
    )


def silu_slope(pre):
    sigma = jax.nn.sigmoid(pre)
    return sigma * (1.0 + pre * (1.0 - sigma))


def slot_table(picks_rows, order_rows, experts, capacity):
    hit = jnp.sum(
        (picks_rows[:, :, None] == jnp.arange(experts, dtype=jnp.int32)[None, None, :]).astype(
            jnp.float32
        ),
        axis=1,
    )
    earlier = (order_rows[None, :] < order_rows[:, None]).astype(jnp.bfloat16)
    ranks = product(earlier, hit.astype(jnp.bfloat16))
    kept = hit * (ranks < capacity).astype(jnp.float32)
    table = kept[:, :, None] * (
        ranks[:, :, None] == jnp.arange(capacity, dtype=jnp.float32)[None, None, :]
    ).astype(jnp.float32)
    return table.reshape(picks_rows.shape[0], experts * capacity)


def per_device(
    inputs,
    segments,
    expert_picks,
    priority,
    cotangent,
    query_weight,
    latent_down,
    latent_up,
    output_weight,
    attn_gain,
    latent_gain,
    router_weight,
    shared_gate,
    shared_up,
    shared_down,
    moe_gain,
    expert_gate,
    expert_up,
    expert_down,
):
    groups = lax.axis_size("expert")
    place = lax.axis_index("expert")
    span = inputs.shape[1]
    length = span * groups
    experts = EXP_DEV * groups
    capacity = (9 * span * TOP + 8 * experts - 1) // (8 * experts)
    scale = 1.0 / math.sqrt(HD + RD)
    query_pos = place * span + jnp.arange(span, dtype=jnp.int32)
    key_pos = jnp.arange(length, dtype=jnp.int32)

    def to_owners(slot_rows):
        return slot_rows.reshape(groups, EXP_DEV * capacity, D)

    def owner_rows(received):
        return (
            received.reshape(groups, EXP_DEV, capacity, D)
            .transpose(1, 0, 2, 3)
            .reshape(EXP_DEV, groups * capacity, D)
        )

    def from_owner(local_rows):
        return (
            local_rows.reshape(EXP_DEV, groups, capacity, D)
            .transpose(1, 0, 2, 3)
            .reshape(groups, EXP_DEV * capacity, D)
        )

    def score_block(query, key_nope, key_rope, key_mask):
        both = jnp.einsum(
            "chd,lhd->hcl", query[..., :HD], key_nope, preferred_element_type=jnp.float32
        )
        both = both + jnp.einsum(
            "chr,lr->hcl", query[..., HD:], key_rope, preferred_element_type=jnp.float32
        )
        return jnp.where(key_mask[None], both * scale, masked_score)

    result_list = []
    grad_list = []
    owned_total = None
    expert_grand_sum = None
    for micro_index in range(MICRO):
        attn_set = (
            lax.all_gather(query_weight, ("dp", "expert"), axis=0, tiled=True),
            lax.all_gather(latent_down, ("dp", "expert"), axis=0, tiled=True),
            lax.all_gather(latent_up, ("dp", "expert"), axis=0, tiled=True),
            lax.all_gather(output_weight, ("dp", "expert"), axis=1, tiled=True),
            lax.all_gather(attn_gain, ("dp", "expert"), axis=0, tiled=True),
            lax.all_gather(latent_gain, ("dp", "expert"), axis=0, tiled=True),
        )
        moe_set = (
            lax.all_gather(router_weight, ("dp", "expert"), axis=0, tiled=True),
            lax.all_gather(shared_gate, ("dp", "expert"), axis=0, tiled=True),
            lax.all_gather(shared_up, ("dp", "expert"), axis=0, tiled=True),
            lax.all_gather(shared_down, ("dp", "expert"), axis=0, tiled=True),
            lax.all_gather(moe_gain, ("dp", "expert"), axis=0, tiled=True),
        )
        expert_set = (
            lax.all_gather(expert_gate, "dp", axis=1, tiled=True),
            lax.all_gather(expert_up, "dp", axis=1, tiled=True),
            lax.all_gather(expert_down, "dp", axis=1, tiled=True),
        )
        (
            forward_q_all,
            forward_down_all,
            forward_up_all,
            forward_out_all,
            forward_gain_attn,
            forward_latent_norm_scale,
        ) = attn_set
        (
            forward_router_all,
            forward_sgate_all,
            forward_shared_up_gathered,
            forward_sdown_all,
            forward_gain_moe,
        ) = moe_set
        forward_gate_local, forward_up_local, forward_down_local = expert_set
        x_first = inputs[micro_index].astype(jnp.float32)
        seg_row = segments[micro_index]
        own_seg = lax.dynamic_slice_in_dim(seg_row, place * span, span, 0)
        forward_key_mask = (key_pos[None, :] <= query_pos[:, None]) & (
            seg_row[None, :] == own_seg[:, None]
        )
        forward_normed_one, forward_factor_one = norm_parts(x_first)
        forward_h_one = (forward_normed_one * forward_gain_attn.astype(jnp.float32)).astype(
            jnp.bfloat16
        )
        query_raw = product(forward_h_one, forward_q_all).reshape(span, HEADS, HD + RD)
        forward_query = jnp.concatenate(
            [query_raw[..., :HD], rotate(query_raw[..., HD:], query_pos)], axis=-1
        ).astype(jnp.bfloat16)
        down = product(forward_h_one, forward_down_all)
        forward_normed_lat, forward_factor_lat = norm_parts(down[:, :RANK])
        latent_own = jnp.concatenate(
            [
                forward_normed_lat * forward_latent_norm_scale.astype(jnp.float32),
                rotate(down[:, RANK:], query_pos),
            ],
            axis=-1,
        ).astype(jnp.bfloat16)
        forward_latent = lax.all_gather(latent_own, "expert", axis=0, tiled=True)
        expanded = (
            product(forward_latent[:, :RANK], forward_up_all)
            .astype(jnp.bfloat16)
            .reshape(length, HEADS, HD + VD)
        )
        forward_key_nope = expanded[..., :HD]
        forward_values = expanded[..., HD:]
        forward_key_rope = forward_latent[:, RANK:]
        forward_scores = score_block(
            forward_query, forward_key_nope, forward_key_rope, forward_key_mask
        )
        top_score = jnp.max(forward_scores, axis=-1, keepdims=True)
        weights_exp = jnp.exp(forward_scores - top_score)
        totals = jnp.sum(weights_exp, axis=-1, keepdims=True)
        forward_probs = weights_exp / totals
        forward_log_total = top_score + jnp.log(totals)
        forward_heads_out = jnp.einsum(
            "hcl,lhd->chd",
            forward_probs.astype(jnp.bfloat16),
            forward_values,
            preferred_element_type=jnp.float32,
        )
        forward_heads_out = forward_heads_out.reshape(span, HEADS * VD).astype(jnp.bfloat16)
        x_second = x_first + product(forward_heads_out, forward_out_all)
        forward_normed_two, forward_factor_two = norm_parts(x_second)
        forward_h_two = (forward_normed_two * forward_gain_moe.astype(jnp.float32)).astype(
            jnp.bfloat16
        )
        forward_gate_probs = jax.nn.softmax(product(forward_h_two, forward_router_all), axis=-1)
        forward_table = slot_table(
            expert_picks[micro_index], priority[micro_index], experts, capacity
        )
        forward_slot_weights = forward_table * jnp.repeat(forward_gate_probs, capacity, axis=1)
        sent = left_product(forward_table.astype(jnp.bfloat16), forward_h_two).astype(jnp.bfloat16)
        forward_expert_in = owner_rows(
            lax.all_to_all(to_owners(sent), "expert", split_axis=0, concat_axis=0, tiled=True)
        )
        forward_gate_pre = jnp.einsum(
            "erd,edf->erf",
            forward_expert_in,
            forward_gate_local,
            preferred_element_type=jnp.float32,
        )
        forward_up_pre = jnp.einsum(
            "erd,edf->erf", forward_expert_in, forward_up_local, preferred_element_type=jnp.float32
        )
        forward_expert_hidden = (jax.nn.silu(forward_gate_pre) * forward_up_pre).astype(
            jnp.bfloat16
        )
        expert_out = jnp.einsum(
            "erf,efd->erd",
            forward_expert_hidden,
            forward_down_local,
            preferred_element_type=jnp.float32,
        ).astype(jnp.bfloat16)
        forward_returned = lax.all_to_all(
            from_owner(expert_out), "expert", split_axis=0, concat_axis=0, tiled=True
        ).reshape(experts * capacity, D)
        routed = jnp.dot(
            forward_slot_weights, forward_returned.astype(jnp.float32), precision=highest
        )
        forward_shared_a = product(forward_h_two, forward_sgate_all)
        forward_shared_b = product(forward_h_two, forward_shared_up_gathered)
        forward_shared_hidden = (jax.nn.silu(forward_shared_a) * forward_shared_b).astype(
            jnp.bfloat16
        )
        result = (x_second + product(forward_shared_hidden, forward_sdown_all) + routed).astype(
            jnp.bfloat16
        )
        forward_kept = (
            forward_normed_one,
            forward_factor_one,
            forward_h_one,
            forward_query,
            forward_normed_lat,
            forward_factor_lat,
            forward_latent,
            forward_key_nope,
            forward_values,
            forward_key_mask,
            forward_log_total,
            forward_heads_out,
            forward_normed_two,
            forward_factor_two,
            forward_h_two,
            forward_gate_probs,
            forward_table,
            forward_slot_weights,
            forward_returned,
            forward_expert_in,
            forward_gate_pre,
            forward_up_pre,
            forward_expert_hidden,
            forward_shared_a,
            forward_shared_b,
            forward_shared_hidden,
        )
        result, kept = (result, forward_kept)
        attn_set = (
            lax.all_gather(query_weight, ("dp", "expert"), axis=0, tiled=True),
            lax.all_gather(latent_down, ("dp", "expert"), axis=0, tiled=True),
            lax.all_gather(latent_up, ("dp", "expert"), axis=0, tiled=True),
            lax.all_gather(output_weight, ("dp", "expert"), axis=1, tiled=True),
            lax.all_gather(attn_gain, ("dp", "expert"), axis=0, tiled=True),
            lax.all_gather(latent_gain, ("dp", "expert"), axis=0, tiled=True),
        )
        moe_set = (
            lax.all_gather(router_weight, ("dp", "expert"), axis=0, tiled=True),
            lax.all_gather(shared_gate, ("dp", "expert"), axis=0, tiled=True),
            lax.all_gather(shared_up, ("dp", "expert"), axis=0, tiled=True),
            lax.all_gather(shared_down, ("dp", "expert"), axis=0, tiled=True),
            lax.all_gather(moe_gain, ("dp", "expert"), axis=0, tiled=True),
        )
        expert_set = (
            lax.all_gather(expert_gate, "dp", axis=1, tiled=True),
            lax.all_gather(expert_up, "dp", axis=1, tiled=True),
            lax.all_gather(expert_down, "dp", axis=1, tiled=True),
        )
        q_all, down_all, up_all, out_all, gain_attn, latent_norm_scale = attn_set
        router_all, sgate_all, shared_up_gathered, sdown_all, gain_moe = moe_set
        gate_local, up_local, down_local = expert_set
        (
            normed_one,
            factor_one,
            h_one,
            backward_query,
            normed_lat,
            factor_lat,
            latent,
            backward_key_nope,
            values,
            backward_key_mask,
            log_total,
            heads_out,
            normed_two,
            factor_two,
            h_two,
            gate_probs,
            table,
            slot_weights,
            returned,
            expert_in,
            gate_pre,
            up_pre,
            expert_hidden,
            shared_a,
            shared_b,
            shared_hidden,
        ) = kept
        grad_out = cotangent[micro_index].astype(jnp.float32)
        shared_low = grad_out.astype(jnp.bfloat16)
        sdown_grad = left_product(shared_hidden, shared_low)
        shared_hidden_grad = right_product(shared_low, sdown_all)
        shared_a_grad = (shared_hidden_grad * shared_b * silu_slope(shared_a)).astype(jnp.bfloat16)
        shared_b_grad = (shared_hidden_grad * jax.nn.silu(shared_a)).astype(jnp.bfloat16)
        sgate_grad = left_product(h_two, shared_a_grad)
        sup_grad = left_product(h_two, shared_b_grad)
        h_two_grad = right_product(shared_a_grad, sgate_all) + right_product(
            shared_b_grad, shared_up_gathered
        )
        slot_grad = exact_left(slot_weights, grad_out).astype(jnp.bfloat16)
        match = jnp.dot(grad_out, returned.astype(jnp.float32).T, precision=highest)
        prob_grad = jnp.sum((match * table).reshape(span, experts, capacity), axis=2)
        logit_grad = (
            gate_probs * (prob_grad - jnp.sum(gate_probs * prob_grad, axis=-1, keepdims=True))
        ).astype(jnp.bfloat16)
        router_grad = left_product(h_two, logit_grad)
        h_two_grad = h_two_grad + right_product(logit_grad, router_all)
        out_grad_local = owner_rows(
            lax.all_to_all(to_owners(slot_grad), "expert", split_axis=0, concat_axis=0, tiled=True)
        )
        hidden_grad = jnp.einsum(
            "erd,efd->erf", out_grad_local, down_local, preferred_element_type=jnp.float32
        )
        backward_routed_down_gradient = jnp.einsum(
            "erf,erd->efd", expert_hidden, out_grad_local, preferred_element_type=jnp.float32
        )
        expert_a_grad = (hidden_grad * up_pre * silu_slope(gate_pre)).astype(jnp.bfloat16)
        expert_b_grad = (hidden_grad * jax.nn.silu(gate_pre)).astype(jnp.bfloat16)
        backward_routed_gate_gradient = jnp.einsum(
            "erd,erf->edf", expert_in, expert_a_grad, preferred_element_type=jnp.float32
        )
        backward_routed_up_gradient = jnp.einsum(
            "erd,erf->edf", expert_in, expert_b_grad, preferred_element_type=jnp.float32
        )
        in_grad = jnp.einsum(
            "erf,edf->erd", expert_a_grad, gate_local, preferred_element_type=jnp.float32
        )
        in_grad = (
            in_grad
            + jnp.einsum(
                "erf,edf->erd", expert_b_grad, up_local, preferred_element_type=jnp.float32
            )
        ).astype(jnp.bfloat16)
        in_grad_back = lax.all_to_all(
            from_owner(in_grad), "expert", split_axis=0, concat_axis=0, tiled=True
        ).reshape(experts * capacity, D)
        h_two_grad = h_two_grad + product(table.astype(jnp.bfloat16), in_grad_back)
        gmoe_grad = jnp.sum(h_two_grad * normed_two, axis=0)
        moe_owned = (
            lax.psum_scatter(router_grad, ("dp", "expert"), scatter_dimension=0, tiled=True),
            lax.psum_scatter(sgate_grad, ("dp", "expert"), scatter_dimension=0, tiled=True),
            lax.psum_scatter(sup_grad, ("dp", "expert"), scatter_dimension=0, tiled=True),
            lax.psum_scatter(sdown_grad, ("dp", "expert"), scatter_dimension=0, tiled=True),
            lax.psum_scatter(gmoe_grad, ("dp", "expert"), scatter_dimension=0, tiled=True),
        )
        x_second_grad = grad_out + norm_back(
            h_two_grad * gain_moe.astype(jnp.float32), normed_two, factor_two
        )
        attn_low = x_second_grad.astype(jnp.bfloat16)
        out_grad = left_product(heads_out, attn_low)
        heads_grad = right_product(attn_low, out_all).astype(jnp.bfloat16).reshape(span, HEADS, VD)
        backward_key_rope = latent[:, RANK:]
        scores = score_block(
            backward_query, backward_key_nope, backward_key_rope, backward_key_mask
        )
        probs = jnp.exp(scores - log_total)
        probs_grad = jnp.einsum(
            "chd,lhd->hcl", heads_grad, values, preferred_element_type=jnp.float32
        )
        spread = jnp.sum(probs * probs_grad, axis=-1, keepdims=True)
        score_grad = (probs * (probs_grad - spread) * scale).astype(jnp.bfloat16)
        value_grad = jnp.einsum(
            "hcl,chd->lhd",
            probs.astype(jnp.bfloat16),
            heads_grad,
            preferred_element_type=jnp.float32,
        )
        key_grad = jnp.einsum(
            "hcl,chd->lhd", score_grad, backward_query[..., :HD], preferred_element_type=jnp.float32
        )
        rope_key_grad = jnp.einsum(
            "hcl,chr->lr", score_grad, backward_query[..., HD:], preferred_element_type=jnp.float32
        )
        query_nope_grad = jnp.einsum(
            "hcl,lhd->chd", score_grad, backward_key_nope, preferred_element_type=jnp.float32
        )
        query_rope_grad = jnp.einsum(
            "hcl,lr->chr", score_grad, backward_key_rope, preferred_element_type=jnp.float32
        )
        expanded_grad = (
            jnp.concatenate([key_grad, value_grad], axis=-1)
            .reshape(length, HEADS * (HD + VD))
            .astype(jnp.bfloat16)
        )
        lup_grad = left_product(latent[:, :RANK], expanded_grad)
        latent_grad = jnp.concatenate(
            [right_product(expanded_grad, up_all), rope_key_grad], axis=-1
        )
        own_grad = lax.psum_scatter(
            latent_grad.astype(jnp.bfloat16), "expert", scatter_dimension=0, tiled=True
        ).astype(jnp.float32)
        glat_grad = jnp.sum(own_grad[:, :RANK] * normed_lat, axis=0)
        lat_part = norm_back(
            own_grad[:, :RANK] * latent_norm_scale.astype(jnp.float32), normed_lat, factor_lat
        )
        down_grad = jnp.concatenate(
            [lat_part, unrotate(own_grad[:, RANK:], query_pos)], axis=-1
        ).astype(jnp.bfloat16)
        query_gradient = jnp.concatenate(
            [query_nope_grad, unrotate(query_rope_grad, query_pos)], axis=-1
        )
        query_gradient = query_gradient.reshape(span, HEADS * (HD + RD)).astype(jnp.bfloat16)
        q_grad = left_product(h_one, query_gradient)
        ldown_grad = left_product(h_one, down_grad)
        h_one_grad = right_product(query_gradient, q_all) + right_product(down_grad, down_all)
        gattn_grad = jnp.sum(h_one_grad * normed_one, axis=0)
        input_grad = x_second_grad + norm_back(
            h_one_grad * gain_attn.astype(jnp.float32), normed_one, factor_one
        )
        attn_owned = (
            lax.psum_scatter(q_grad, ("dp", "expert"), scatter_dimension=0, tiled=True),
            lax.psum_scatter(ldown_grad, ("dp", "expert"), scatter_dimension=0, tiled=True),
            lax.psum_scatter(lup_grad, ("dp", "expert"), scatter_dimension=0, tiled=True),
            lax.psum_scatter(out_grad, ("dp", "expert"), scatter_dimension=1, tiled=True),
            lax.psum_scatter(gattn_grad, ("dp", "expert"), scatter_dimension=0, tiled=True),
            lax.psum_scatter(glat_grad, ("dp", "expert"), scatter_dimension=0, tiled=True),
        )
        expert_portion = (
            backward_routed_gate_gradient,
            backward_routed_up_gradient,
            backward_routed_down_gradient,
        )
        input_grad, owned_part, expert_portion = (
            input_grad.astype(jnp.bfloat16),
            tuple(attn_owned) + tuple(moe_owned),
            expert_portion,
        )
        result_list.append(result)
        grad_list.append(input_grad)
        owned_total = (
            owned_part if owned_total is None else jax.tree.map(jnp.add, owned_total, owned_part)
        )
        expert_grand_sum = (
            expert_portion
            if expert_grand_sum is None
            else jax.tree.map(jnp.add, expert_grand_sum, expert_portion)
        )
    (
        q_owned,
        ldown_owned,
        lup_owned,
        out_owned,
        gattn_owned,
        glat_owned,
        router_owned,
        sgate_owned,
        sup_owned,
        sdown_owned,
        gmoe_owned,
    ) = owned_total
    routed_gate_gradient, routed_up_gradient, routed_down_gradient = expert_grand_sum
    expert_owned = (
        lax.psum_scatter(
            routed_gate_gradient.astype(jnp.bfloat16), "dp", scatter_dimension=1, tiled=True
        ).astype(jnp.float32),
        lax.psum_scatter(
            routed_up_gradient.astype(jnp.bfloat16), "dp", scatter_dimension=1, tiled=True
        ).astype(jnp.float32),
        lax.psum_scatter(
            routed_down_gradient.astype(jnp.bfloat16), "dp", scatter_dimension=1, tiled=True
        ).astype(jnp.float32),
    )
    return (
        jnp.stack(result_list),
        jnp.stack(grad_list),
        q_owned,
        ldown_owned,
        lup_owned,
        out_owned,
        gattn_owned,
        glat_owned,
        router_owned,
        sgate_owned,
        sup_owned,
        sdown_owned,
        gmoe_owned,
        expert_owned[0],
        expert_owned[1],
        expert_owned[2],
    )


def solution(mesh):
    return jax.shard_map(
        per_device,
        mesh=mesh,
        in_specs=(
            P("dp", "expert", None),
            P("dp", None),
            P("dp", "expert", None),
            P("dp", "expert"),
            P("dp", "expert", None),
            P(("dp", "expert"), None),
            P(("dp", "expert"), None),
            P(("dp", "expert"), None),
            P(None, ("dp", "expert")),
            P(("dp", "expert")),
            P(("dp", "expert")),
            P(("dp", "expert"), None),
            P(("dp", "expert"), None),
            P(("dp", "expert"), None),
            P(("dp", "expert"), None),
            P(("dp", "expert")),
            P("expert", "dp", None),
            P("expert", "dp", None),
            P("expert", "dp", None),
        ),
        out_specs=(
            P("dp", "expert", None),
            P("dp", "expert", None),
            P(("dp", "expert"), None),
            P(("dp", "expert"), None),
            P(("dp", "expert"), None),
            P(None, ("dp", "expert")),
            P(("dp", "expert")),
            P(("dp", "expert")),
            P(("dp", "expert"), None),
            P(("dp", "expert"), None),
            P(("dp", "expert"), None),
            P(("dp", "expert"), None),
            P(("dp", "expert")),
            P("expert", "dp", None),
            P("expert", "dp", None),
            P("expert", "dp", None),
        ),
        check_vma=False,
    )
```

profile of v0, /device:TPU:0, one launch (start us, length us, event | category | flops | bytes accessed | tf_op | source)
XLA Modules:
  0.0 3334.5 jit_solution(17593700352784996804)
XLA Ops:
  10.5 42.3 %all-reduce.7 = (bf16[2048]{0:T(1024)(128)(2,1)S(1)}, bf16[512]{0:T(512)(128)(2,1)S(1)}, bf16[2048]{0:T(1024)(128)(2,1)S(1)}) all-reduce(bf16[2048]{0:T(1024)(128)(2,1)S(1)} %dynamic-update-slice, bf16[512]{0:T(512)(128)(2,1)S(1)} %dynamic-update-slice.1, ...), channel_id=1, replica_groups=mesh['dp'=2,'expert'=16] {'dp','expert'}, use_global_device_ids=true, to_apply=%add | all-reduce | flops 4608 | bytes 18432
  54.1 17.2 all-gather.14.cloned.1.call-done
  87.1 28.4 all-gather.16.cloned.1.call-done
  115.6 63.4 %all-gather.18.cloned.1.call-done = bf16[512,4096]{1,0:T(8,128)(2,1)} async-done(((bf16[16,4096]{1,0:T(8,128)(2,1)}), bf16[512,4096]{1,0:T(8,128)(2,1)}) %all-gather.18.cloned.1.call-update) | async-done | bytes 4194320 | tf_op jit(solution)/shard_map/all_gather | solution.py:173
  179.0 10.3 convolution_convert_fusion.1
  189.3 9.9 copy.228
  205.7 70.0 %all-gather.20.cloned.1.call-done = bf16[2048,3072]{1,0:T(8,128)(2,1)} async-done(((bf16[64,3072]{1,0:T(8,128)(2,1)}), bf16[2048,3072]{1,0:T(8,128)(2,1)}) %all-gather.20.cloned.1.call-update) | async-done | bytes 12582928 | tf_op jit(solution)/shard_map/all_gather | solution.py:171
  275.7 16.8 copy.169
  321.2 32.9 all-gather.22.cloned.1.call-done
  364.4 51.2 %all_to_all.40 = bf16[16,27,2048]{2,1,0:T(8,128)(2,1)} all-to-all(bf16[16,27,2048]{2,1,0:T(8,128)(2,1)S(1)} %reshape.675), channel_id=1, replica_groups=mesh['dp'=2,'expert'=16] {'expert'}, dimensions={0} | all-to-all | bytes 3538944 | tf_op jit(solution)/shard_map/all_to_all | solution.py:265
  417.5 11.1 all-gather.30.cloned.1.call-done
  435.6 69.1 %all-gather.32.cloned.1.call-done = bf16[1,2048,1408]{2,1,0:T(8,128)(2,1)} async-done(((bf16[1,1024,1408]{2,1,0:T(8,128)(2,1)}), bf16[1,2048,1408]{2,1,0:T(8,128)(2,1)}) %all-gather.32.cloned.1.call-update) | async-done | bytes 5767184 | tf_op jit(solution)/shard_map/all_gather | solution.py:187
  512.1 68.6 %all-gather.34.cloned.1.call-done = bf16[1,1408,2048]{2,1,0:T(8,128)(2,1)} async-done(((bf16[1,704,2048]{2,1,0:T(8,128)(2,1)}), bf16[1,1408,2048]{2,1,0:T(8,128)(2,1)}) %all-gather.34.cloned.1.call-update) | async-done | bytes 5767184 | tf_op jit(solution)/shard_map/all_gather | solution.py:188
  593.9 82.8 %all-gather = bf16[32,64,16]{1,2,0:T(8,128)(2,1)S(1)} all-gather(bf16[1,64,16]{1,2,0:T(8,128)(2,1)S(1)} %bitcast.444), channel_id=1, replica_groups=mesh['dp'=2,'expert'=16] {'dp','expert'}, dimensions={0}, use_global_device_ids=true | all-gather | bytes 67584 | tf_op jit(solution)/shard_map/all_gather | solution.py:179
  690.2 10.4 convolution_convert_fusion
  700.6 9.9 copy.229
  767.8 40.2 %all-to-all-done.4 = bf16[16,27,2048]{2,1,0:T(8,128)(2,1)} async-done(((bf16[16,27,2048]{2,1,0:T(8,128)(2,1)}), bf16[16,27,2048]{2,1,0:T(8,128)(2,1)}, u32[]{:S(2)}, u32[]{:S(2)}) %all-to-all-start.4) | async-done | bytes 1769504 | tf_op jit(solution)/shard_map/all_to_all | solution.py:399
  835.2 13.5 all-to-all-start.5
  861.9 101.2 %all-gather.28.cloned.1.call-done = bf16[2816,2048]{1,0:T(8,128)(2,1)} async-done(((bf16[88,2048]{1,0:T(8,128)(2,1)}), bf16[2816,2048]{1,0:T(8,128)(2,1)}) %all-gather.28.cloned.1.call-update) | async-done | bytes 11534352 | tf_op jit(solution)/shard_map/all_gather | solution.py:182
  991.4 51.5 %all_to_all.41 = bf16[16,27,2048]{2,1,0:T(8,128)(2,1)} all-to-all(bf16[16,27,2048]{2,1,0:T(8,128)(2,1)S(1)} %reshape.681), channel_id=1, replica_groups=mesh['dp'=2,'expert'=16] {'expert'}, dimensions={0} | all-to-all | bytes 3538944 | tf_op jit(solution)/shard_map/all_to_all | solution.py:265
  1069.7 40.7 %all-to-all-done.3 = bf16[16,27,2048]{2,1,0:T(8,128)(2,1)S(1)} async-done(((bf16[16,27,2048]{2,1,0:T(8,128)(2,1)}), bf16[16,27,2048]{2,1,0:T(8,128)(2,1)S(1)}, u32[]{:S(2)}, u32[]{:S(2)}) %all-to-all-start.3) | async-done | bytes 1769504 | tf_op jit(solution)/shard_map/all_to_all | solution.py:285
  1129.0 11.4 all-to-all-start.6
  1148.5 33.0 all-to-all-done.6
  1204.3 11.3 all-to-all-start.7
  1244.1 12.5 all-to-all-done.7
  1270.8 9.9 fusion.143
  1280.7 13.9 convert_bitcast_fusion.3
  1309.9 9.9 fusion.146
  1319.9 13.9 convert_bitcast_fusion.1
  1386.9 11.1 fusion.4
  1423.5 60.2 %reduce-scatter.18.cloned.1.call-done = bf16[64,576]{1,0:T(8,128)(2,1)} async-done(((bf16[1024,576]{1,0:T(8,128)(2,1)}), bf16[64,576]{1,0:T(8,128)(2,1)}) %reduce-scatter.18.cloned.1.call-update) | async-done | bytes 73744 | tf_op jit(solution)/shard_map/reduce_scatter | solution.py:479
  1499.4 10.4 convolution_add_fusion.5
  1520.2 15.1 convolution_add_fusion
  1545.6 14.9 convolution_add_fusion.1
  1570.9 15.0 convolution_add_fusion.2
  1614.7 13.4 fusion.113
  1629.2 13.6 fusion.118
  1643.9 10.8 fusion.217
  1654.7 17.1 convolution_add_fusion.3
  1715.1 42.4 %all-reduce.6 = (f32[2048]{0:T(1024)S(1)}, f32[512]{0:T(512)S(1)}, f32[2048]{0:T(1024)S(1)}) all-reduce(f32[2048]{0:T(1024)S(1)} %add.379, f32[512]{0:T(512)S(1)} %add.380, f32[2048]{0:T(1024)S(1)} %copy-done.124), channel_id=19, replica_groups=mesh['dp'=2,'expert'=16] {'dp','expert'}, use_global_device_ids=true, to_apply=%region_39.40.clone | all-reduce | flops 4608 | bytes 36864
  1772.4 68.9 %reduce-scatter.22.cloned.1.call-done = bf16[1,1024,1408]{2,1,0:T(8,128)(2,1)} async-done(((bf16[1,2048,1408]{2,1,0:T(8,128)(2,1)}), bf16[1,1024,1408]{2,1,0:T(8,128)(2,1)}) %reduce-scatter.22.cloned.1.call-update) | async-done | bytes 2883600 | tf_op jit(solution)/shard_map/reduce_scatter | solution.py:546
  1846.1 142.8 %reduce-scatter.28.cloned.1.call-done = f32[64,576]{1,0:T(8,128)} async-done(((f32[2048,576]{1,0:T(8,128)}), f32[64,576]{1,0:T(8,128)}) %reduce-scatter.28.cloned.1.call-update) | async-done | bytes 147472 | tf_op jit(solution)/shard_map/reduce_scatter | solution.py:502
  1988.9 149.0 %reduce-scatter.30.cloned.1.call-done = f32[16,4096]{1,0:T(8,128)} async-done(((f32[512,4096]{1,0:T(8,128)}), f32[16,4096]{1,0:T(8,128)}) %reduce-scatter.30.cloned.1.call-update) | async-done | bytes 262160 | tf_op jit(solution)/shard_map/reduce_scatter | solution.py:503
  2137.8 245.8 %reduce-scatter.38.cloned.1.call-done = f32[88,2048]{1,0:T(8,128)} async-done(((f32[2816,2048]{1,0:T(8,128)}), f32[88,2048]{1,0:T(8,128)}) %reduce-scatter.38.cloned.1.call-update) | async-done | bytes 720912 | tf_op jit(solution)/shard_map/reduce_scatter | solution.py:433
  2383.6 251.8 %reduce-scatter.36.cloned.1.call-done = f32[64,2816]{1,0:T(8,128)} async-done(((f32[2048,2816]{1,0:T(8,128)}), f32[64,2816]{1,0:T(8,128)}) %reduce-scatter.36.cloned.1.call-update) | async-done | bytes 720912 | tf_op jit(solution)/shard_map/reduce_scatter | solution.py:432
  2635.5 251.9 %reduce-scatter.34.cloned.1.call-done = f32[64,2816]{1,0:T(8,128)} async-done(((f32[2048,2816]{1,0:T(8,128)}), f32[64,2816]{1,0:T(8,128)}) %reduce-scatter.34.cloned.1.call-update) | async-done | bytes 720912 | tf_op jit(solution)/shard_map/reduce_scatter | solution.py:431
  2887.3 188.6 %reduce-scatter.32.cloned.1.call-done = f32[2048,64]{0,1:T(8,128)} async-done(((f32[2048,2048]{0,1:T(8,128)}), f32[2048,64]{0,1:T(8,128)}) %reduce-scatter.32.cloned.1.call-update) | async-done | bytes 524304 | tf_op jit(solution)/shard_map/reduce_scatter | solution.py:504
  3076.0 251.5 %reduce-scatter.26.cloned.1.call-done = f32[64,3072]{1,0:T(8,128)} async-done(((f32[2048,3072]{1,0:T(8,128)}), f32[64,3072]{1,0:T(8,128)}) %reduce-scatter.26.cloned.1.call-update) | async-done | bytes 786448 | tf_op jit(solution)/shard_map/reduce_scatter | solution.py:501
  (617 shorter events, 585.8 us)
Async XLA Ops:
  7.2 64.2 %all-gather.14.cloned.1.call-start = ((), (), s32[]{:S(2)}) async-start(), calls=%async_computation.21 | async-start | bytes 2703360 | tf_op jit(solution)/shard_map/all_gather | solution.py:172
  7.9 107.6 %all-gather.16.cloned.1.call-start = ((), (), s32[]{:S(2)}) async-start(), calls=%async_computation.22 | async-start | bytes 1392640 | tf_op jit(solution)/shard_map/all_gather | solution.py:229
  52.8 248.6 %copy-start.62 = (f32[2048]{0:T(1024)}, f32[2048]{0:T(1024)S(1)}, u32[]{:S(2)}) copy-start(f32[2048]{0:T(1024)S(1)} %convert_element_type.339) | copy-start | bytes 24580
  54.1 238.4 %copy-start.125 = (f32[64]{0:T(128)}, f32[64]{0:T(128)S(1)}, u32[]{:S(2)}) copy-start(f32[64]{0:T(128)S(1)} %get-tuple-element.121) | copy-start | bytes 772
  54.1 247.3 %copy-start.129 = (f32[64]{0:T(128)}, f32[64]{0:T(128)S(1)}, u32[]{:S(2)}) copy-start(f32[64]{0:T(128)S(1)} %get-tuple-element.122) | copy-start | bytes 772
  76.8 228.8 %copy-start.81 = (f32[64,32]{1,0:T(8,128)}, f32[64,32]{1,0:T(8,128)S(1)}, u32[]{:S(2)}) copy-start(f32[64,32]{1,0:T(8,128)S(1)} %get-tuple-element.92) | copy-start | bytes 24580
  76.8 228.8 %copy-start.83 = (f32[64,32]{1,0:T(8,128)}, f32[64,32]{1,0:T(8,128)S(1)}, u32[]{:S(2)}) copy-start(f32[64,32]{1,0:T(8,128)S(1)} %get-tuple-element.95) | copy-start | bytes 24580
  77.8 101.2 %all-gather.18.cloned.1.call-start = ((), (), s32[]{:S(2)}) async-start(), calls=%async_computation.23 | async-start | bytes 4325376 | tf_op jit(solution)/shard_map/all_gather | solution.py:173
  78.6 197.2 %all-gather.20.cloned.1.call-start = ((), (), s32[]{:S(2)}) async-start(), calls=%async_computation.24 | async-start | bytes 12976128 | tf_op jit(solution)/shard_map/all_gather | solution.py:171
  79.1 275.0 %all-gather.22.cloned.1.call-start = ((), (), s32[]{:S(2)}) async-start(), calls=%async_computation.25 | async-start | bytes 8650752 | tf_op jit(solution)/shard_map/all_gather | solution.py:174
  79.8 348.9 %all-gather.30.cloned.1.call-start = ((), (), s32[]{:S(2)}) async-start(), calls=%async_computation.29 | async-start | bytes 8650752 | tf_op jit(solution)/shard_map/all_gather | solution.py:186
  80.4 424.3 %all-gather.32.cloned.1.call-start = ((), (), s32[]{:S(2)}) async-start(), calls=%async_computation.30 | async-start | bytes 8650752 | tf_op jit(solution)/shard_map/all_gather | solution.py:187
  81.1 499.6 %all-gather.34.cloned.1.call-start = ((), (), s32[]{:S(2)}) async-start(), calls=%async_computation.31 | async-start | bytes 8650752 | tf_op jit(solution)/shard_map/all_gather | solution.py:188
  81.9 608.3 %all-gather.36.cloned.1.call-start = ((), (), s32[]{:S(2)}) async-start(), calls=%async_computation.32 | async-start | bytes 1392640 | tf_op jit(solution)/shard_map/all_gather | solution.py:229
  82.7 678.6 %all-gather.26.cloned.1.call-start = ((), (), s32[]{:S(2)}) async-start(), calls=%async_computation.27 | async-start | bytes 11894784 | tf_op jit(solution)/shard_map/all_gather | solution.py:181
  83.3 771.5 %all-gather.24.cloned.1.call-start = ((), (), s32[]{:S(2)}) async-start(), calls=%async_computation.26 | async-start | bytes 11894784 | tf_op jit(solution)/shard_map/all_gather | solution.py:180
  84.0 879.2 %all-gather.28.cloned.1.call-start = ((), (), s32[]{:S(2)}) async-start(), calls=%async_computation.28 | async-start | bytes 11894784 | tf_op jit(solution)/shard_map/all_gather | solution.py:182
  85.9 274.6 %copy-start.114 = (f32[432]{0:T(512)}, f32[432]{0:T(512)S(1)}, u32[]{:S(2)}) copy-start(f32[432]{0:T(512)S(1)} %eq.147) | copy-start | bytes 5188
  86.1 898.1 %copy-start.89 = (f32[64,16]{0,1:T(8,128)}, f32[64,16]{0,1:T(8,128)S(1)}, u32[]{:S(2)}) copy-start(f32[64,16]{0,1:T(8,128)S(1)} %get-tuple-element.104) | copy-start | bytes 12292
  86.3 274.2 %copy-start.67 = (f32[64,432]{1,0:T(8,128)}, f32[64,432]{1,0:T(8,128)S(1)}, u32[]{:S(2)}) copy-start(f32[64,432]{1,0:T(8,128)S(1)} %copy.176) | copy-start | bytes 331780
  86.8 273.7 %copy-start.68 = (f32[64,432]{1,0:T(8,128)}, f32[64,432]{1,0:T(8,128)S(1)}, u32[]{:S(2)}) copy-start(f32[64,432]{1,0:T(8,128)S(1)} %copy.175) | copy-start | bytes 331780
  360.3 899.1 %copy-start.17 = (f32[64,2048]{1,0:T(8,128)}, f32[64,2048]{1,0:T(8,128)S(1)}, u32[]{:S(2)}) copy-start(f32[64,2048]{1,0:T(8,128)S(1)} %get-tuple-element.103) | copy-start | bytes 1572868
  360.5 494.2 %copy-start.7 = (bf16[64,2048]{1,0:T(8,128)(2,1)}, bf16[64,2048]{1,0:T(8,128)(2,1)S(1)}, u32[]{:S(2)}) copy-start(bf16[64,2048]{1,0:T(8,128)(2,1)S(1)} %multiply_convert_fusion.15) | copy-start | bytes 786436
  588.3 129.8 %all-to-all-start.1 = ((bf16[16,27,2048]{2,1,0:T(8,128)(2,1)}), bf16[16,27,2048]{2,1,0:T(8,128)(2,1)S(1)}, u32[]{:S(2)}, u32[]{:S(2)}) async-start(bf16[16,27,2048]{2,1,0:T(8,128)(2,1)} %reshape_transpose_reshape.16), calls=%async_computation.1 | async-start | bytes 4194304 | tf_op jit(solution)/shard_map/all_to_all | solution.py:285
  739.6 68.4 %all-to-all-start.4 = ((bf16[16,27,2048]{2,1,0:T(8,128)(2,1)}), bf16[16,27,2048]{2,1,0:T(8,128)(2,1)}, u32[]{:S(2)}, u32[]{:S(2)}) async-start(bf16[16,27,2048]{2,1,0:T(8,128)(2,1)} %reshape.685), calls=%async_computation.4 | async-start | bytes 4194304 | tf_op jit(solution)/shard_map/all_to_all | solution.py:399
  761.2 223.0 %copy-start.19 = (f32[64,2048]{1,0:T(8,128)}, f32[64,2048]{1,0:T(8,128)S(1)}, u32[]{:S(2)}) copy-start(f32[64,2048]{1,0:T(8,128)S(1)} %get-tuple-element.111) | copy-start | bytes 1572868
  761.2 223.0 %copy-start.140 = (f32[64]{0:T(128)}, f32[64]{0:T(128)S(1)}, u32[]{:S(2)}) copy-start(f32[64]{0:T(128)S(1)} %add_rsqrt_fusion) | copy-start | bytes 772
  835.2 149.0 %all-to-all-start.5 = ((bf16[16,27,2048]{2,1,0:T(8,128)(2,1)}), bf16[16,27,2048]{2,1,0:T(8,128)(2,1)}, u32[]{:S(2)}, u32[]{:S(2)}) async-start(bf16[16,27,2048]{2,1,0:T(8,128)(2,1)} %reshape_transpose_reshape.18), calls=%async_computation.5 | async-start | bytes 4194304 | tf_op jit(solution)/shard_map/all_to_all | solution.py:424
  848.7 114.5 %copy-start.22 = (bf16[2,64,2048]{2,1,0:T(8,128)(2,1)S(1)}, bf16[2,64,2048]{2,1,0:T(8,128)(2,1)}, u32[]{:S(2)}) copy-start(bf16[2,64,2048]{2,1,0:T(8,128)(2,1)} %param.23) | copy-start | bytes 1572868
  1064.3 46.1 %all-to-all-start.3 = ((bf16[16,27,2048]{2,1,0:T(8,128)(2,1)}), bf16[16,27,2048]{2,1,0:T(8,128)(2,1)S(1)}, u32[]{:S(2)}, u32[]{:S(2)}) async-start(bf16[16,27,2048]{2,1,0:T(8,128)(2,1)} %reshape_transpose_reshape.17), calls=%async_computation.3 | async-start | bytes 4194304 | tf_op jit(solution)/shard_map/all_to_all | solution.py:285
  1120.1 122.9 %copy-start.102 = (f32[64,16]{0,1:T(8,128)}, f32[64,16]{0,1:T(8,128)S(1)}, u32[]{:S(2)}) copy-start(f32[64,16]{0,1:T(8,128)S(1)} %get-tuple-element.41) | copy-start | bytes 12292
  1129.0 52.4 %all-to-all-start.6 = ((bf16[16,27,2048]{2,1,0:T(8,128)(2,1)}), bf16[16,27,2048]{2,1,0:T(8,128)(2,1)S(1)}, u32[]{:S(2)}, u32[]{:S(2)}) async-start(bf16[16,27,2048]{2,1,0:T(8,128)(2,1)} %reshape.690), calls=%async_computation.7 | async-start | bytes 4194304 | tf_op jit(solution)/shard_map/all_to_all | solution.py:399
  1140.5 154.1 %copy-start.119 = (f32[16,64]{1,0:T(8,128)}, f32[16,64]{1,0:T(8,128)S(1)}, u32[]{:S(2)}) copy-start(f32[16,64]{1,0:T(8,128)S(1)} %log_add_fusion.1) | copy-start | bytes 12292
  1141.2 192.6 %copy-start.117 = (f32[16,64]{1,0:T(8,128)}, f32[16,64]{1,0:T(8,128)S(1)}, u32[]{:S(2)}) copy-start(f32[16,64]{1,0:T(8,128)S(1)} %log_add_fusion) | copy-start | bytes 12292
  1204.3 52.3 %all-to-all-start.7 = ((bf16[16,27,2048]{2,1,0:T(8,128)(2,1)}), bf16[16,27,2048]{2,1,0:T(8,128)(2,1)}, u32[]{:S(2)}, u32[]{:S(2)}) async-start(bf16[16,27,2048]{2,1,0:T(8,128)(2,1)} %reshape_transpose_reshape.19), calls=%async_computation.8 | async-start | bytes 4194304 | tf_op jit(solution)/shard_map/all_to_all | solution.py:424
  1215.5 207.0 %reduce-scatter.16.cloned.1.call-start = ((), (), s32[]{:S(2)}) async-start(), calls=%async_computation.33 | async-start | bytes 1392640 | tf_op jit(solution)/shard_map/reduce_scatter | solution.py:479
  1358.2 125.5 %reduce-scatter.18.cloned.1.call-start = ((), (), s32[]{:S(2)}) async-start(), calls=%async_computation.34 | async-start | bytes 1392640 | tf_op jit(solution)/shard_map/reduce_scatter | solution.py:479
  1377.3 312.4 %reduce-scatter.40.cloned.1.call-start = ((), (), s32[]{:S(2)}) async-start(), calls=%async_computation.45 | async-start | bytes 1081344
  1386.9 373.6 %reduce-scatter.24.cloned.1.call-start = ((), (), s32[]{:S(2)}) async-start(), calls=%async_computation.37 | async-start | bytes 8650752 | tf_op jit(solution)/shard_map/reduce_scatter | solution.py:549
  1398.0 369.7 %reduce-scatter.20.cloned.1.call-start = ((), (), s32[]{:S(2)}) async-start(), calls=%async_computation.35 | async-start | bytes 8650752 | tf_op jit(solution)/shard_map/reduce_scatter | solution.py:543
  1410.0 431.3 %reduce-scatter.22.cloned.1.call-start = ((), (), s32[]{:S(2)}) async-start(), calls=%async_computation.36 | async-start | bytes 8650752 | tf_op jit(solution)/shard_map/reduce_scatter | solution.py:546
  1420.6 568.2 %reduce-scatter.28.cloned.1.call-start = ((), (), s32[]{:S(2)}) async-start(), calls=%async_computation.39 | async-start | bytes 5406720 | tf_op jit(solution)/shard_map/reduce_scatter | solution.py:502
  1491.0 646.9 %reduce-scatter.30.cloned.1.call-start = ((), (), s32[]{:S(2)}) async-start(), calls=%async_computation.40 | async-start | bytes 8650752 | tf_op jit(solution)/shard_map/reduce_scatter | solution.py:503
  1509.8 873.8 %reduce-scatter.38.cloned.1.call-start = ((), (), s32[]{:S(2)}) async-start(), calls=%async_computation.44 | async-start | bytes 23789568 | tf_op jit(solution)/shard_map/reduce_scatter | solution.py:433
  1535.3 1100.2 %reduce-scatter.36.cloned.1.call-start = ((), (), s32[]{:S(2)}) async-start(), calls=%async_computation.43 | async-start | bytes 23789568 | tf_op jit(solution)/shard_map/reduce_scatter | solution.py:432
  1560.5 1326.8 %reduce-scatter.34.cloned.1.call-start = ((), (), s32[]{:S(2)}) async-start(), calls=%async_computation.42 | async-start | bytes 23789568 | tf_op jit(solution)/shard_map/reduce_scatter | solution.py:431
  1585.9 1490.0 %reduce-scatter.32.cloned.1.call-start = ((), (), s32[]{:S(2)}) async-start(), calls=%async_computation.41 | async-start | bytes 17301504 | tf_op jit(solution)/shard_map/reduce_scatter | solution.py:504
  1597.6 1730.0 %reduce-scatter.26.cloned.1.call-start = ((), (), s32[]{:S(2)}) async-start(), calls=%async_computation.38 | async-start | bytes 25952256 | tf_op jit(solution)/shard_map/reduce_scatter | solution.py:501
  (155 other events, 2135.8 us)
Sparse Core Ops, SparseCore 0:
  10.9 60.4 all-gather.13
  77.9 37.5 all-gather.15
  118.4 60.4 all-gather.17
  181.7 93.9 all-gather.19
  278.4 75.6 all-gather.21
  355.5 73.0 all-gather.29
  430.2 74.4 all-gather.31
  506.2 74.4 all-gather.33
  583.6 60.9 all-gather.35
  647.3 87.2 all-gather.25
  737.5 117.2 all-gather.23
  857.4 105.7 all-gather.27
  1358.3 64.2 reduce-scatter.15
  1426.0 57.5 reduce-scatter.17
  1485.7 135.8 reduce-scatter.39
  1624.3 67.7 reduce-scatter.23
  1694.8 72.8 reduce-scatter.19
  1769.9 71.4 reduce-scatter.21
  1844.2 144.6 reduce-scatter.27
  1991.6 146.2 reduce-scatter.29
  2140.7 242.8 reduce-scatter.37
  2386.5 248.9 reduce-scatter.35
  2638.3 248.9 reduce-scatter.33
  2890.0 185.8 reduce-scatter.31
  3083.0 244.5 reduce-scatter.25
where the time goes:
time: 3350 us; the launch traced here: 3330 us
  waiting for transfers between devices  2220 us (66%)
  matrix products  592 us (18%)
  blocking collectives  270 us (8%)
  local copies, waits for them, and re-layouts  128 us (4%)
  other arithmetic  57.9 us (2%)
  starting transfers between devices  54.3 us (2%)
    reduce_scatter x1, waiting for transfers between devices, per_device(): lax.psum_scatter(sgate_grad, ('dp', 'expert'), scatter_dimension=0, tiled...  252 us
    reduce_scatter x1, waiting for transfers between devices, per_device(): lax.psum_scatter(sup_grad, ('dp', 'expert'), scatter_dimension=0, tiled=T...  252 us
    reduce_scatter x1, waiting for transfers between devices, per_device(): lax.psum_scatter(q_grad, ('dp', 'expert'), scatter_dimension=0, tiled=True)  252 us
    reduce_scatter x1, waiting for transfers between devices, per_device(): lax.psum_scatter(sdown_grad, ('dp', 'expert'), scatter_dimension=0, tiled...  246 us
    reduce_scatter x1, waiting for transfers between devices, per_device(): lax.psum_scatter(out_grad, ('dp', 'expert'), scatter_dimension=1, tiled=T...  189 us
    reduce_scatter x1, waiting for transfers between devices, per_device(): lax.psum_scatter(lup_grad, ('dp', 'expert'), scatter_dimension=0, tiled=T...  149 us
    reduce_scatter x1, waiting for transfers between devices, per_device(): lax.psum_scatter(ldown_grad, ('dp', 'expert'), scatter_dimension=0, tiled...  143 us
    dot_general x18, matrix products, left_product(): lax.dot_general(left, right, (((0,), (0,)), ((), ())), preferred_element_...  137 us
  transfers between devices with their start and end apart: 31, of which 25 were waited for; matrix products, arithmetic and copies ran while one was open for 17% of the time, Pallas kernels for 0%

commit v1 on v0

v1 whole, which is shorter than its diff:
```python
import functools
import math

import jax
import jax.numpy as jnp
from jax import lax
from jax.experimental import pallas as pl
from jax.experimental.pallas import tpu as pltpu
from jax.sharding import PartitionSpec as P

HEADS = 16
HD = 128
RD = 64
VD = 128
RANK = 512
TOP = 6

epsilon = 1e-06
masked_score = -1e30
DP = "dp"
EXPERT = "expert"
BOTH = (DP, EXPERT)
TOKENS = P(DP, EXPERT, None)
ROWS = P(BOTH, None)
ROUTED = P(EXPERT, DP, None)
f32 = jnp.float32
bf16 = jnp.bfloat16


def product(left, right):
    return jnp.dot(left, right, preferred_element_type=f32)


def left_product(left, right):
    return lax.dot_general(left, right, (((0,), (0,)), ((), ())), preferred_element_type=f32)


def right_product(left, right):
    return lax.dot_general(left, right, (((1,), (1,)), ((), ())), preferred_element_type=f32)


def einsum(spec, left, right):
    return jnp.einsum(spec, left, right, preferred_element_type=f32)


def norm_parts(values):
    factor = lax.rsqrt(jnp.mean(values * values, axis=-1, keepdims=True) + epsilon)
    return (values * factor, factor)


def norm_back(grad_normed, normed, factor):
    return factor * (grad_normed - normed * jnp.mean(grad_normed * normed, axis=-1, keepdims=True))


def angle_tables(positions, width):
    half = width // 2
    freqs = jnp.power(10000.0, -2.0 * jnp.arange(half, dtype=f32) / width)
    angles = positions.astype(f32)[:, None] * freqs[None, :]
    return (jnp.cos(angles), jnp.sin(angles))


def rotate(values, tables):
    half = values.shape[-1] // 2
    cosine, sine = tables
    first = values[..., :half]
    second = values[..., half:]
    return jnp.concatenate(
        [first * cosine - second * sine, second * cosine + first * sine], axis=-1
    )


def unrotate(grads, tables):
    half = grads.shape[-1] // 2
    cosine, sine = tables
    first = grads[..., :half]
    second = grads[..., half:]
    return jnp.concatenate(
        [first * cosine + second * sine, second * cosine - first * sine], axis=-1
    )


def silu_slope(pre):
    sigma = jax.nn.sigmoid(pre)
    return sigma * (1.0 + pre * (1.0 - sigma))


def dp_swap(value):
    return lax.ppermute(value, DP, [(0, 1), (1, 0)])


def dp_gather(value):
    if lax.axis_size(DP) == 2:
        other = dp_swap(value)
        first = lax.axis_index(DP) == 0
        return jnp.concatenate(
            [jnp.where(first, value, other), jnp.where(first, other, value)], axis=0
        )
    return lax.all_gather(value, DP, axis=0, tiled=True)


def dp_scatter_product(left, right):
    if lax.axis_size(DP) == 2:
        first = lax.axis_index(DP) == 0
        half = left.shape[1] // 2
        low, high = left[:, :half], left[:, half:]
        sent = left_product(jnp.where(first, high, low), right).astype(bf16)
        other = dp_swap(sent)
        return left_product(jnp.where(first, low, high), right) + other.astype(f32)
    return dp_scatter(left_product(left, right))


def dp_scatter(value):
    if lax.axis_size(DP) == 2:
        rows = value.shape[0] // 2
        at = lax.axis_index(DP)
        sent = lax.dynamic_slice_in_dim(value, (1 - at) * rows, rows, 0)
        kept = lax.dynamic_slice_in_dim(value, at * rows, rows, 0)
        return kept + dp_swap(sent.astype(bf16)).astype(f32)
    return lax.psum_scatter(
        value.astype(bf16), DP, scatter_dimension=0, tiled=True
    ).astype(f32)


def expert_swap(value):
    return lax.all_to_all(value, EXPERT, split_axis=0, concat_axis=0, tiled=True)


def gather_rows(value, axes):
    return lax.all_gather(value, axes, axis=0, tiled=True)


def scatter_rows(value, axes):
    return lax.psum_scatter(value, axes, scatter_dimension=0, tiled=True)


MESH = pl.DeviceIdType.MESH


def at_expert(index):
    return {EXPERT: index}


def grid_place():
    me = lax.axis_index(EXPERT)
    return me, me // 4, (me // 2) % 2, me % 2


def greet_neighbours(me, line, pair, core):
    partner = me + 1 - 2 * core
    mate = me + 2 - 4 * pair
    barrier = pltpu.get_barrier_semaphore()
    for other in (partner, mate):
        pl.semaphore_signal(barrier, inc=1, device_id=at_expert(other), device_id_type=MESH)

    @pl.when(line < 3)
    def _():
        pl.semaphore_signal(barrier, inc=1, device_id=at_expert(me + 4), device_id_type=MESH)

    @pl.when(line > 0)
    def _():
        pl.semaphore_signal(barrier, inc=1, device_id=at_expert(me - 4), device_id_type=MESH)

    pl.semaphore_wait(barrier, 3 + jnp.where((line > 0) & (line < 3), 1, 0))
    return partner, mate


def gather_kernel(x_ref, out_ref, own_sem, send_sem, recv_sem):
    me, line, pair, core = grid_place()
    partner, mate = greet_neighbours(me, line, pair, core)
    own = pltpu.make_async_copy(x_ref, out_ref.at[me], own_sem)
    own.start()

    def copy(source, origin, way, to):
        return pltpu.make_async_remote_copy(
            src_ref=source,
            dst_ref=out_ref.at[origin],
            send_sem=send_sem.at[origin, way],
            recv_sem=recv_sem.at[origin],
            device_id=at_expert(to),
            device_id_type=MESH,
        )

    def arrived(origin):
        copy(out_ref.at[origin], origin, 0, partner).wait_recv()

    def along(origin, source, upward, downward, act):
        if upward:

            @pl.when(line < 3)
            def _():
                act(copy(source, origin, 0, me + 4))

        if downward:

            @pl.when(line > 0)
            def _():
                act(copy(source, origin, 1, me - 4))

        act(copy(source, origin, 2, mate))
        act(copy(source, origin, 3, partner))

    def walk(act, wait):
        along(me, x_ref, True, True, act)
        for far in range(1, 5):
            if far < 4:

                @pl.when(line >= far)
                def _():
                    origin = me - 4 * far
                    wait(origin)
                    along(origin, out_ref.at[origin], True, False, act)

                @pl.when(line + far <= 3)
                def _():
                    origin = me + 4 * far
                    wait(origin)
                    along(origin, out_ref.at[origin], False, True, act)

            for sign in (-1, 1) if far > 1 else (1,):
                step = sign * (far - 1)

                @pl.when((line + step >= 0) & (line + step <= 3))
                def _():
                    origin = mate + 4 * step
                    wait(origin)
                    act(copy(out_ref.at[origin], origin, 3, partner))

    walk(lambda c: c.start(), arrived)
    for index in range(8):
        arrived(2 * index + 1 - core)
    walk(lambda c: c.wait_send(), lambda origin: None)
    own.wait()


def ring_gather(value, collective):
    rows, columns = value.shape
    sent = 15 * rows * columns * 2
    out = pl.pallas_call(
        gather_kernel,
        out_shape=jax.ShapeDtypeStruct((16, rows, columns), value.dtype),
        in_specs=[pl.BlockSpec(memory_space=pltpu.VMEM)],
        out_specs=pl.BlockSpec(memory_space=pl.ANY),
        scratch_shapes=[
            pltpu.SemaphoreType.DMA,
            pltpu.SemaphoreType.DMA((16, 4)),
            pltpu.SemaphoreType.DMA((16,)),
        ],
        compiler_params=pltpu.CompilerParams(collective_id=collective, has_side_effects=True),
        cost_estimate=pl.CostEstimate(flops=0, bytes_accessed=16 * sent, transcendentals=0),
    )(value)
    return out.reshape(16 * rows, columns)


def scatter_kernel(
    p_ref, out_ref, chip, mate_in, up_in, down_in, total,
    core_send, core_recv, mate_send, mate_recv, up_send, up_recv, down_send, down_recv,
):
    me, line, pair, core = grid_place()
    partner, mate = greet_neighbours(me, line, pair, core)
    rows = p_ref.shape[1]
    tile = 16

    def remote(source, target, send, recv, to):
        return pltpu.make_async_remote_copy(
            src_ref=source, dst_ref=target, send_sem=send, recv_sem=recv,
            device_id=at_expert(to), device_id_type=MESH,
        )

    def core_copy(index):
        return remote(
            p_ref.at[2 * index + 1 - core], chip.at[index],
            core_send.at[index], core_recv.at[index], partner,
        )

    def mate_copy(dest):
        return remote(
            total.at[2 * dest + 1 - pair], mate_in.at[dest],
            mate_send.at[dest], mate_recv.at[dest], mate,
        )

    def up_copy(dest):
        return remote(
            total.at[2 * dest + pair], up_in.at[dest], up_send.at[dest], up_recv.at[dest], me + 4
        )

    def down_copy(dest):
        return remote(
            total.at[2 * dest + pair], down_in.at[dest],
            down_send.at[dest], down_recv.at[dest], me - 4,
        )

    def add(target, left, right):
        @pl.loop(0, rows // tile)
        def _(i):
            at = pl.ds(pl.multiple_of(i * tile, tile), tile)
            target[at, :] = (left[at, :].astype(f32) + right[at, :].astype(f32)).astype(
                target.dtype
            )

    def farthest(act):
        for far in (3, 2, 1, 0):
            for step in (-far, far) if far else (0,):

                @pl.when((line + step >= 0) & (line + step <= 3))
                def _():
                    act(line + step, step)

    def send_core(dest, step):
        core_copy(2 * dest + 1 - pair).start()

    def send_core_own(dest, step):
        core_copy(2 * dest + pair).start()

    def chip_sum(index):
        core_copy(index).wait_recv()
        add(total.at[index], p_ref.at[2 * index + core], chip.at[index])

    def to_mate(dest, step):
        chip_sum(2 * dest + 1 - pair)
        mate_copy(dest).start()

    def keep(dest, step):
        chip_sum(2 * dest + pair)

    def along(dest, step):
        mine = total.at[2 * dest + pair]
        mate_copy(dest).wait_recv()
        if step == 0:
            mine, kept = out_ref, mine
            add(mine, kept, mate_in.at[dest])
        else:
            add(mine, mine, mate_in.at[dest])
        if step > 0:

            @pl.when(line > 0)
            def _():
                up_copy(dest).wait_recv()
                add(mine, mine, up_in.at[dest])

            up_copy(dest).start()
        elif step < 0:

            @pl.when(line < 3)
            def _():
                down_copy(dest).wait_recv()
                add(mine, mine, down_in.at[dest])

            down_copy(dest).start()
        else:

            @pl.when(line > 0)
            def _():
                up_copy(dest).wait_recv()
                add(mine, mine, up_in.at[dest])

            @pl.when(line < 3)
            def _():
                down_copy(dest).wait_recv()
                add(mine, mine, down_in.at[dest])

    def finish(dest, step):
        mate_copy(dest).wait_send()
        core_copy(2 * dest + 1 - pair).wait_send()
        core_copy(2 * dest + pair).wait_send()
        if step > 0:
            up_copy(dest).wait_send()
        elif step < 0:
            down_copy(dest).wait_send()

    farthest(send_core)
    farthest(send_core_own)
    farthest(to_mate)
    farthest(keep)
    farthest(along)
    farthest(finish)


def ring_scatter(value, collective):
    rows, columns = value.shape[0] // 16, value.shape[1]
    block = lambda n: pltpu.VMEM((n, rows, columns), bf16)
    sems = lambda n: pltpu.SemaphoreType.DMA((n,))
    sent = 15 * rows * columns * 2
    return pl.pallas_call(
        scatter_kernel,
        out_shape=jax.ShapeDtypeStruct((rows, columns), f32),
        in_specs=[pl.BlockSpec(memory_space=pltpu.VMEM)],
        out_specs=pl.BlockSpec(memory_space=pltpu.VMEM),
        scratch_shapes=[block(8), block(4), block(4), block(4), block(8)]
        + [sems(8), sems(8), sems(4), sems(4), sems(4), sems(4), sems(4), sems(4)],
        compiler_params=pltpu.CompilerParams(collective_id=collective, has_side_effects=True),
        cost_estimate=pl.CostEstimate(flops=0, bytes_accessed=16 * sent, transcendentals=0),
    )(value.reshape(16, rows, columns))


def swap_kernel(source, target, x_ref, out_ref, own_sem, send_sem, recv_sem):
    me = lax.axis_index(EXPERT)
    barrier = pltpu.get_barrier_semaphore()
    for step in range(1, 16):
        pl.semaphore_signal(
            barrier, inc=1, device_id=at_expert((me + step) % 16), device_id_type=MESH
        )
    pl.semaphore_wait(barrier, 15)

    def copy(step):
        to = (me + step) % 16
        return pltpu.make_async_remote_copy(
            src_ref=source(x_ref, to),
            dst_ref=target(out_ref, me),
            send_sem=send_sem.at[step],
            recv_sem=recv_sem.at[step],
            device_id=at_expert(to),
            device_id_type=MESH,
        )

    for step in range(1, 16):
        copy(step).start()
    own = pltpu.make_async_copy(source(x_ref, me), target(out_ref, me), own_sem)
    own.start()
    for step in range(1, 16):
        copy(step).wait()
    own.wait()


def swap_call(source, target, value, shape, collective):
    sent = value.size * 2
    return pl.pallas_call(
        functools.partial(swap_kernel, source, target),
        out_shape=jax.ShapeDtypeStruct(shape, value.dtype),
        in_specs=[pl.BlockSpec(memory_space=pltpu.VMEM)],
        out_specs=pl.BlockSpec(memory_space=pltpu.VMEM),
        scratch_shapes=[
            pltpu.SemaphoreType.DMA,
            pltpu.SemaphoreType.DMA((16,)),
            pltpu.SemaphoreType.DMA((16,)),
        ],
        compiler_params=pltpu.CompilerParams(collective_id=collective, has_side_effects=True),
        cost_estimate=pl.CostEstimate(flops=0, bytes_accessed=64 * sent, transcendentals=0),
    )(value)


def block_rows(span):
    return lambda ref, at: ref.at[:, pl.ds(pl.multiple_of(at * span, span), span), :]


def head_columns(columns):
    return lambda ref, at: ref.at[:, :, pl.ds(pl.multiple_of(at * columns, columns), columns)]


def heads_to_tokens(value, span, collective):
    seqs = value.shape[0]
    return swap_call(
        block_rows(span), head_columns(VD), value, (seqs, span, HEADS * VD), collective
    )


def tokens_to_heads(value, collective):
    seqs, span, _ = value.shape
    return swap_call(
        head_columns(VD), block_rows(span), value, (seqs, span * HEADS, VD), collective
    )


def per_device(
    inputs,
    segments,
    expert_picks,
    priority,
    cotangent,
    query_weight,
    latent_down,
    latent_up,
    output_weight,
    attn_gain,
    latent_gain,
    router_weight,
    shared_gate,
    shared_up,
    shared_down,
    moe_gain,
    expert_gate,
    expert_up,
    expert_down,
):
    groups = lax.axis_size(EXPERT)
    replicas = lax.axis_size(DP)
    place = lax.axis_index(EXPERT)
    seqs, span, width = inputs.shape
    length = span * groups
    own = seqs * span
    tokens = own * groups
    experts = groups
    capacity = (9 * span * TOP + 8 * experts - 1) // (8 * experts)
    scale = 1.0 / math.sqrt(HD + RD)
    rows = query_weight.shape[0]
    part = shared_down.shape[0]
    hidden_own = part * replicas
    QD = HD + RD

    def by_sequence(value):
        return value.reshape(groups, seqs, span, -1).transpose(1, 0, 2, 3).reshape(
            seqs, length, -1
        )

    def by_block(value):
        return value.reshape(seqs, groups, span, -1).transpose(1, 0, 2, 3).reshape(tokens, -1)

    x_low = inputs.reshape(own, width)
    x_all = gather_rows(x_low, EXPERT)
    cot_own = cotangent.reshape(own, width)

    order = priority[:, None, :] < priority[:, :, None]
    hit = jnp.sum(
        (expert_picks[..., None] == jnp.arange(experts, dtype=jnp.int32)).astype(f32), axis=2
    )
    ranks = einsum("stu,sue->ste", order.astype(bf16), hit.astype(bf16))
    codes = jnp.where((hit > 0) & (ranks < capacity), ranks, -1.0).astype(bf16)

    pad = rows - latent_gain.shape[0]
    small = jnp.concatenate(
        [
            latent_down,
            router_weight,
            attn_gain[:, None],
            moe_gain[:, None],
            jnp.pad(latent_gain, (0, pad))[:, None],
            jnp.zeros((rows, 45), bf16),
        ],
        axis=1,
    )
    small_all = dp_gather(small)
    small_all = ring_gather(small_all, 1)
    small_all = (
        small_all.reshape(groups, replicas, rows, -1).transpose(1, 0, 2, 3).reshape(width, -1)
    )
    ldown_all = small_all[:, : RANK + RD]
    router_all = small_all[:, RANK + RD : RANK + RD + experts]
    gains = small_all[:, RANK + RD + experts :].astype(f32)
    gain_attn = gains[:, 0]
    gain_moe = gains[:, 1]
    gain_lat = gains[:, 2].reshape(-1, rows)[:, : latent_gain.shape[0]].reshape(-1)

    query_swap = expert_swap(query_weight.reshape(rows, HEADS, QD).transpose(1, 0, 2))
    lup_rows = latent_up.shape[0]
    code_row = jnp.pad(
        codes.reshape(own, experts).T, ((0, 0), (0, HD + VD - own))
    )[:, None, :]
    lup_swap = expert_swap(
        jnp.concatenate(
            [latent_up.reshape(lup_rows, HEADS, HD + VD).transpose(1, 0, 2), code_row], axis=1
        )
    )
    wq = dp_gather(query_swap.reshape(groups * rows, QD))
    lup = dp_gather(lup_swap[:, :lup_rows].reshape(groups * lup_rows, HD + VD))
    code = lup_swap[:, lup_rows, :own].astype(f32).reshape(tokens)

    def columns_of(weight):
        return (
            weight.reshape(rows, replicas, groups, part)
            .transpose(2, 0, 1, 3)
            .reshape(groups, rows, hidden_own)
        )

    gate_up_swap = expert_swap(
        jnp.concatenate([columns_of(shared_gate), columns_of(shared_up)], axis=2)
    )
    gate_up = dp_gather(gate_up_swap.reshape(groups * rows, 2 * hidden_own))
    gate_up_router = jnp.concatenate([gate_up, router_all], axis=1)
    sdown = dp_gather(shared_down)
    gate_w = dp_gather(expert_gate[0])
    up_w = dp_gather(expert_up[0])
    down_w = dp_gather(expert_down[0])
    out_t = gather_rows(output_weight.T, BOTH)
    cot_all = gather_rows(cot_own, EXPERT)

    at_block = jnp.arange(groups, dtype=jnp.int32)[:, None, None] * span
    positions = jnp.broadcast_to(
        at_block + jnp.arange(span, dtype=jnp.int32), (groups, seqs, span)
    ).reshape(tokens)
    tables = lax.optimization_barrier(angle_tables(positions, RD))
    normed_one, _ = norm_parts(x_all.astype(f32))
    h_one = (normed_one * gain_attn).astype(bf16)
    query_raw = product(h_one, wq)
    query = jnp.concatenate(
        [query_raw[:, :HD], rotate(query_raw[:, HD:], tables)], axis=-1
    ).astype(bf16)
    down = product(h_one, ldown_all)
    normed_lat, factor_lat = norm_parts(down[:, :RANK])
    latent = (normed_lat * gain_lat).astype(bf16)
    key_rope = rotate(down[:, RANK:], tables).astype(bf16)
    expanded = product(latent, lup).astype(bf16)
    query_s = by_sequence(query)
    key_s = by_sequence(jnp.concatenate([expanded[:, :HD], key_rope], axis=-1))
    value_s = by_sequence(expanded[:, HD:])
    at = jnp.arange(length, dtype=jnp.int32)
    mask = (at[None, None, :] <= at[None, :, None]) & (
        segments[:, None, :] == segments[:, :, None]
    )
    scores = jnp.where(mask, einsum("sqd,skd->sqk", query_s, key_s) * scale, masked_score)
    top_score = jnp.max(scores, axis=-1, keepdims=True)
    weights_exp = jnp.exp(scores - top_score)
    probs_attn = (weights_exp / jnp.sum(weights_exp, axis=-1, keepdims=True)).astype(bf16)
    heads_s = einsum("sqk,skd->sqd", probs_attn, value_s).astype(bf16)
    heads_own = heads_to_tokens(heads_s, span, 3).reshape(own, HEADS * VD)

    x_second = x_low.astype(f32) + right_product(heads_own, out_t)
    normed_two, factor_two = norm_parts(x_second)
    h_two = ring_gather((normed_two * gain_moe).astype(bf16), 2)

    chunk = tokens // 2
    blocks = chunk // span
    slots = blocks * capacity
    slot_at = jnp.arange(slots, dtype=jnp.int32)
    token_at = jnp.arange(chunk, dtype=jnp.int32)
    select = (
        (slot_at[:, None] // capacity == token_at[None, :] // span)[None]
        & (
            (slot_at % capacity).astype(f32)[None, :, None]
            == code.reshape(2, chunk)[:, None, :]
        )
    ).astype(bf16)
    select = lax.optimization_barrier(select)

    def to_slots(values):
        return einsum("cst,ctd->csd", select, values.reshape(2, chunk, -1)).astype(bf16).reshape(
            2 * slots, -1
        )

    def to_tokens(values):
        return einsum("cst,csd->ctd", select, values.reshape(2, slots, -1)).reshape(tokens, -1)

    pre = product(h_two, gate_up_router)
    shared_a = pre[:, :hidden_own]
    shared_b = pre[:, hidden_own : 2 * hidden_own]
    gate_probs = jax.nn.softmax(pre[:, 2 * hidden_own :], axis=-1)
    shared_hidden = (jax.nn.silu(shared_a) * shared_b).astype(bf16)
    mine = (jnp.arange(experts, dtype=jnp.int32) == place).astype(f32)
    own_prob = jnp.sum(gate_probs * mine, axis=-1)
    slot_prob = jnp.sum(
        select.astype(f32) * own_prob.reshape(2, 1, chunk), axis=-1
    ).reshape(2 * slots, 1)
    expert_in = to_slots(h_two)
    gate_pre = product(expert_in, gate_w)
    up_pre = product(expert_in, up_w)
    expert_hidden = (jax.nn.silu(gate_pre) * up_pre).astype(bf16)
    expert_out = product(expert_hidden, down_w).astype(bf16).astype(f32)
    partial = product(shared_hidden, sdown) + to_tokens((slot_prob * expert_out).astype(bf16))
    partial, cot_all = lax.optimization_barrier((partial.astype(bf16), cot_all))
    result = x_second + scatter_rows(partial, EXPERT).astype(f32)
    result = result.astype(bf16).reshape(seqs, span, width)

    grad_slots = to_slots(cot_all)
    hidden_grad = right_product(cot_all, sdown)
    sdown_grad = left_product(shared_hidden, cot_all)
    shared_a_grad = (hidden_grad * shared_b * silu_slope(shared_a)).astype(bf16)
    shared_b_grad = (hidden_grad * jax.nn.silu(shared_a)).astype(bf16)
    grad_wide = grad_slots.astype(f32)
    slot_grad = (slot_prob * grad_wide).astype(bf16)
    match = jnp.sum(grad_wide * expert_out, axis=-1).reshape(2, slots, 1)
    prob_grad = jnp.sum(select.astype(f32) * match, axis=1).reshape(tokens, 1)
    logit_grad = (gate_probs * prob_grad * (mine - own_prob[:, None])).astype(bf16)
    pre_grad = jnp.concatenate([shared_a_grad, shared_b_grad, logit_grad], axis=1)
    expert_hidden_grad = right_product(slot_grad, down_w)
    expert_a_grad = (expert_hidden_grad * up_pre * silu_slope(gate_pre)).astype(bf16)
    expert_b_grad = (expert_hidden_grad * jax.nn.silu(gate_pre)).astype(bf16)
    in_grad = (right_product(expert_a_grad, gate_w) + right_product(expert_b_grad, up_w)).astype(
        bf16
    )
    h_two_partial = right_product(pre_grad, gate_up_router) + to_tokens(in_grad)
    routed_down_grad = dp_scatter_product(expert_hidden, slot_grad)
    routed_gate_grad = dp_scatter_product(expert_in, expert_a_grad)
    routed_up_grad = dp_scatter_product(expert_in, expert_b_grad)
    h_two_grad = ring_scatter(h_two_partial.astype(bf16), 4)
    pre_weight_grad = left_product(h_two, pre_grad)
    sdown_owned = dp_scatter(sdown_grad)
    gate_up_owned = dp_scatter(pre_weight_grad[:, : 2 * hidden_own]).astype(bf16)
    gate_up_owned = expert_swap(
        gate_up_owned.reshape(groups, rows, 2 * hidden_own)
    ).astype(f32)

    def owned_columns(value):
        return (
            value.reshape(groups, rows, replicas, part)
            .transpose(1, 2, 0, 3)
            .reshape(rows, replicas * groups * part)
        )

    sgate_owned = owned_columns(gate_up_owned[:, :, :hidden_own])
    sup_owned = owned_columns(gate_up_owned[:, :, hidden_own:])
    router_grad = pre_weight_grad[:, 2 * hidden_own :]

    gmoe_grad = jnp.sum(h_two_grad * normed_two, axis=0)
    x_second_grad = cot_own.astype(f32) + norm_back(h_two_grad * gain_moe, normed_two, factor_two)
    attn_low = x_second_grad.astype(bf16)
    heads_grad = product(attn_low, out_t).astype(bf16)
    grad_s = tokens_to_heads(heads_grad.reshape(seqs, span, HEADS * VD), 5)
    out_owned = (
        scatter_rows(left_product(attn_low, heads_own).astype(bf16), BOTH).astype(f32).T
    )
    probs_grad = einsum("sqd,skd->sqk", grad_s, value_s)
    spread = jnp.sum(grad_s.astype(f32) * heads_s.astype(f32), axis=-1, keepdims=True)
    score_grad = (probs_attn.astype(f32) * (probs_grad - spread) * scale).astype(bf16)
    value_grad = einsum("sqk,sqd->skd", probs_attn, grad_s)
    key_grad = einsum("sqk,sqd->skd", score_grad, query_s)
    query_grad = by_block(einsum("sqk,skd->sqd", score_grad, key_s))
    expanded_grad = by_block(
        jnp.concatenate([key_grad[..., :HD], value_grad], axis=-1).astype(bf16)
    )
    rope_grad = by_block(key_grad[..., HD:])
    lup_grad = left_product(latent, expanded_grad)
    latent_grad = right_product(expanded_grad, lup)
    glat_grad = jnp.sum(latent_grad * normed_lat, axis=0)
    joint_grad = jnp.concatenate(
        [
            query_grad[:, :HD],
            unrotate(query_grad[:, HD:], tables),
            norm_back(latent_grad * gain_lat, normed_lat, factor_lat),
            unrotate(rope_grad, tables),
        ],
        axis=-1,
    ).astype(bf16)
    joint_weight = jnp.concatenate([wq, ldown_all], axis=1)
    h_one_partial = right_product(joint_grad, joint_weight)
    gattn_grad = jnp.sum(h_one_partial * normed_one, axis=0)
    h_one_grad = ring_scatter(h_one_partial.astype(bf16), 6)
    normed_own, factor_own = norm_parts(x_low.astype(f32))
    input_grad = x_second_grad + norm_back(h_one_grad * gain_attn, normed_own, factor_own)
    input_grad = input_grad.astype(bf16).reshape(seqs, span, width)
    joint_weight_grad = left_product(h_one, joint_grad)
    q_owned = expert_swap(
        dp_scatter(joint_weight_grad[:, :QD]).astype(bf16).reshape(groups, rows, QD)
    ).astype(f32)
    q_owned = q_owned.transpose(1, 0, 2).reshape(rows, HEADS * QD)
    lup_owned = expert_swap(
        dp_scatter(lup_grad).astype(bf16).reshape(groups, lup_rows, HD + VD)
    ).astype(f32)
    lup_owned = lup_owned.transpose(1, 0, 2).reshape(lup_rows, HEADS * (HD + VD))
    glat_column = jnp.pad(
        glat_grad.reshape(-1, latent_gain.shape[0]), ((0, 0), (0, pad))
    ).reshape(-1, 1)
    small_grad = jnp.concatenate(
        [
            joint_weight_grad[:, QD:],
            router_grad,
            gattn_grad[:, None],
            gmoe_grad[:, None],
            glat_column,
            jnp.zeros((width, 45), f32),
        ],
        axis=1,
    )
    small_grad = (
        small_grad.astype(bf16)
        .reshape(replicas, groups, rows, -1)
        .transpose(1, 0, 2, 3)
        .reshape(width, -1)
    )
    small_owned = ring_scatter(small_grad, 7)
    small_owned = dp_scatter(small_owned)
    ldown_owned = small_owned[:, : RANK + RD]
    router_owned = small_owned[:, RANK + RD : RANK + RD + experts]
    gain_owned = small_owned[:, RANK + RD + experts :]
    return (
        result,
        input_grad,
        q_owned,
        ldown_owned,
        lup_owned,
        out_owned,
        gain_owned[:, 0],
        gain_owned[: latent_gain.shape[0], 2],
        router_owned,
        sgate_owned,
        sup_owned,
        sdown_owned,
        gain_owned[:, 1],
        routed_gate_grad[None],
        routed_up_grad[None],
        routed_down_grad[None],
    )


def solution(mesh):
    return jax.shard_map(
        per_device,
        mesh=mesh,
        in_specs=(
            TOKENS, P(DP, None), TOKENS, P(DP, EXPERT), TOKENS,
            ROWS, ROWS, ROWS, P(None, BOTH), P(BOTH), P(BOTH),
            ROWS, ROWS, ROWS, ROWS, P(BOTH), ROUTED, ROUTED, ROUTED,
        ),
        out_specs=(
            TOKENS, TOKENS, ROWS, ROWS, ROWS, P(None, BOTH), P(BOTH), P(BOTH),
            ROWS, ROWS, ROWS, ROWS, P(BOTH), ROUTED, ROUTED, ROUTED,
        ),
        check_vma=False,
    )
```

time: 3350 us -> 1180 us (0.35)
  waiting for transfers between devices: 2220 us -> 311 us
  Pallas kernels: 0 us -> 356 us
  matrix products: 592 us -> 261 us
  blocking collectives: 270 us -> 0 us
    reduce_scatter x12 -> x2, waiting for transfers between devices: 1610 us -> 0.02 us  [scatter_rows(): return lax.psum_scatter(value, axes, scatter_dimension=0, tiled=True)]
    all_gather x12 -> x3, waiting for transfers between devices: 468 us -> 0.02 us  [gather_rows(): return lax.all_gather(value, axes, axis=0, tiled=True)]
    pallas_call x0 -> x7, Pallas kernels: none -> 356 us  [the longest x3 159 us: ring_scatter(): pl.pallas_call(scatter_kernel, out_shape=jax.ShapeDtypeStruct((rows, colu...]
    ppermute x0 -> x16, waiting for transfers between devices: none -> 299 us  [dp_swap(): return lax.ppermute(value, DP, [(0, 1), (1, 0)])]
    dot_general x62 -> x19, matrix products: 362 us -> 103 us  [the longest x9 57 us: product(): return jnp.dot(left, right, preferred_element_type=f32)]
    all_to_all x6, waiting for transfers between devices: 126 us -> 10.4 us  [expert_swap(): lax.all_to_all(value, EXPERT, split_axis=0, concat_axis=0, tiled=True)]
    all_to_all x2 -> x0, blocking collectives: 103 us -> none  [per_device(): lax.all_to_all(to_owners(sent), 'expert', split_axis=0, concat_axis=0, ti...]
    unnamed x2 -> x0, blocking collectives: 84.7 us -> none
  transfers between devices with their start and end apart: 31 -> 27, of which waited for: 25 -> 7; matrix products, arithmetic and copies ran while one was open for 17% -> 35% of each run, Pallas kernels for 0% -> 30%
where the time goes in v1:
time: 1180 us; the launch traced here: 1170 us
  Pallas kernels  356 us (30%)
  waiting for transfers between devices  311 us (26%)
  matrix products  261 us (22%)
  local copies, waits for them, and re-layouts  109 us (9%)
  other arithmetic  69.8 us (6%)
  starting transfers between devices  51.8 us (4%)
  between operations  15.6 us (1%)
    ppermute x16, waiting for transfers between devices, dp_swap(): return lax.ppermute(value, DP, [(0, 1), (1, 0)])  299 us
    pallas_call x3, Pallas kernels, ring_scatter(): pl.pallas_call(scatter_kernel, out_shape=jax.ShapeDtypeStruct((rows, colu...  159 us
    pallas_call x2, Pallas kernels, ring_gather(): pl.pallas_call(gather_kernel, out_shape=jax.ShapeDtypeStruct((16, rows, c...  124 us
    dot_general x8, matrix products, right_product(): lax.dot_general(left, right, (((1,), (1,)), ((), ())), preferred_element_...  85.3 us
    pallas_call x2, Pallas kernels, swap_call(): pl.pallas_call(functools.partial(swap_kernel, source, target), out_shape=...  72.5 us
    dot_general x11, matrix products, left_product(): lax.dot_general(left, right, (((0,), (0,)), ((), ())), preferred_element_...  64.2 us
    dot_general x9, matrix products, product(): return jnp.dot(left, right, preferred_element_type=f32)  57 us
    dot_general x10, matrix products, einsum(): return jnp.einsum(spec, left, right, preferred_element_type=f32)  46.3 us
  transfers between devices with their start and end apart: 27, of which 7 were waited for; matrix products, arithmetic and copies ran while one was open for 35% of the time, Pallas kernels for 30%

profile of v1, /device:TPU:0, one launch (start us, length us, event | category | flops | bytes accessed | tf_op | source)
XLA Modules:
  0.0 1172.8 jit_solution(6255929293664734363)
XLA Ops:
  12.1 7.4 all-to-all-start.1
  36.4 6.0 all-to-all-start.2
  49.9 64.7 %shard_map.306 = bf16[16,128,640]{2,1,0:T(8,128)(2,1)} custom-call(bf16[128,640]{1,0:T(8,128)(2,1)} %pad_maximum_fusion.27.x_ref), custom_call_target="tpu_custom_call" | custom-call | bytes 39321600 | tf_op jit(solution)/shard_map/pallas_call | solution.py:238
  132.1 115.3 %collective-permute-done.4 = bf16[88,2048]{1,0:T(8,128)(2,1)} collective-permute-done((bf16[88,2048]{1,0:T(8,128)(2,1)}, bf16[88,2048]{1,0:T(8,128)(2,1)}, u32[]{:S(2)}, u32[]{:S(2)}) %collective-permute-start.4) | collective-permute-done | bytes 360480 | tf_op jit(solution)/shard_map/ppermute | solution.py:88
  255.1 7.2 collective-permute-done.1
  264.4 11.8 %collective-permute-done.3 = bf16[1024,352]{0,1:T(8,128)(2,1)S(1)} collective-permute-done((bf16[1024,352]{0,1:T(8,128)(2,1)}, bf16[1024,352]{0,1:T(8,128)(2,1)S(1)}, u32[]{:S(2)}, u32[]{:S(2)}) %collective-permute-start.3) | collective-permute-done | bytes 720928 | tf_op jit(solution)/shard_map/ppermute | solution.py:88
  277.4 5.0 broadcast_select_fusion.5
  282.4 5.1 broadcast_select_fusion.3
  287.5 4.8 broadcast_select_fusion.1
  292.3 5.2 fusion.5
  298.1 7.4 fusion.109
  322.4 7.7 fusion.119
  330.1 4.6 divide_convert_fusion
  339.3 15.3 %shard_map.307 = bf16[2,64,2048]{2,1,0:T(8,128)(2,1)} custom-call(bf16[2,1024,128]{2,1,0:T(8,128)(2,1)} %convolution_convert_fusion.9.x_ref), custom_call_target="tpu_custom_call" | custom-call | bytes 33554432 | tf_op jit(solution)/shard_map/pallas_call | solution.py:426
  354.7 6.6 multiply_reduce_fusion.7
  363.2 59.6 %shard_map.308 = bf16[16,128,2048]{2,1,0:T(8,128)(2,1)} custom-call(bf16[128,2048]{1,0:T(8,128)(2,1)} %multiply_convert_fusion.9.x_ref), custom_call_target="tpu_custom_call" | custom-call | bytes 125829120 | tf_op jit(solution)/shard_map/pallas_call | solution.py:238
  422.9 5.9 fusion.60
  433.3 7.6 convolution_convert_fusion.4
  440.9 7.3 fusion.23
  448.2 9.7 multiply_convert_fusion.3
  457.9 7.0 fusion.8
  465.0 8.7 fusion.120
  473.7 11.5 fusion.7
  485.2 7.6 convolution_convert_fusion.3
  498.2 9.6 multiply_convert_fusion.7
  507.8 16.3 %multiply_convert_fusion.2 = (bf16[864,1408]{1,0:T(8,128)(2,1)}, bf16[864,1408]{1,0:T(8,128)(2,1)}) fusion(f32[864,1408]{1,0:T(8,128)} %fusion.23, f32[864,1408]{1,0:T(8,128)} %get-tuple-element.156, bf16[864,2048]{1,0:T(8,128)(2,1)S(1)} %copy-done.4, bf16[704,2048]{1,0:T(8,128)(2,1)} %get-tuple-element.118, bf16[704,2048]{1,0:T(8,128)(2,1)} %get-tuple-element.117), kind=kOutput, calls=%fused_computation.31 | convolution fusion | flops 5010182144 | bytes 23904256 | tf_op jit(solution)/shard_map/dot_general | solution.py:39
  524.2 11.4 fusion.20
  535.6 10.3 add_convert_fusion
  545.9 8.3 fusion.121
  554.2 10.8 fusion.6
  565.0 68.3 %shard_map.309 = f32[128,2048]{1,0:T(8,128)} custom-call(bf16[16,128,2048]{2,1,0:T(8,128)(2,1)} %bitcast.186), custom_call_target="tpu_custom_call" | custom-call | bytes 125829120 | tf_op jit(solution)/shard_map/pallas_call | solution.py:383
  633.4 5.7 fusion.59
  642.9 4.8 convolution_convert_fusion.2
  649.9 4.9 convolution_convert_fusion.1
  654.9 5.2 convolution_convert_fusion.5
  666.6 5.5 all-to-all-start.5
  675.0 5.7 convolution_convert_fusion
  686.6 163.5 %collective-permute-done.12 = bf16[88,2048]{1,0:T(8,128)(2,1)S(1)} collective-permute-done((bf16[88,2048]{1,0:T(8,128)(2,1)S(1)}, bf16[88,2048]{1,0:T(8,128)(2,1)S(1)}, u32[]{:S(2)}, u32[]{:S(2)}) %collective-permute-start.12) | collective-permute-done | bytes 360480 | tf_op jit(solution)/shard_map/ppermute | solution.py:88
  866.1 9.7 add_bitcast_fusion.2
  875.9 6.9 add_bitcast_fusion.1
  882.8 7.2 add_bitcast_fusion
  892.0 57.2 %shard_map.310 = bf16[2,1024,128]{2,1,0:T(8,128)(2,1)} custom-call(bf16[2,64,2048]{2,1,0:T(8,128)(2,1)} %bitcast.232), custom_call_target="tpu_custom_call" | custom-call | bytes 33554432 | tf_op jit(solution)/shard_map/pallas_call | solution.py:426
  986.9 16.4 %fusion.4 = (bf16[2048]{0:T(1024)(128)(2,1)S(1)}, bf16[2048,2048]{1,0:T(8,128)(2,1)}) fusion(bf16[2048,2048]{1,0:T(8,128)(2,1)S(1)} %bitcast.202, f32[2048]{0:T(1024)S(1)} %copy-done.84, bf16[2048,768]{0,1:T(8,128)(2,1)} %copy-done.76, bf16[2048,576]{1,0:T(8,128)(2,1)S(1)} %bitcast.210, bf16[1024,192]{1,0:T(8,128)(2,1)S(1)} %copy-done.67, ...), kind=kOutput, calls=%fused_computation.6 | convolution fusion | flops 6472857600 | bytes 23080960 | tf_op jit(solution)/shard_map/dot_general | solution.py:39
  1003.3 61.1 %shard_map.311 = f32[128,2048]{1,0:T(8,128)} custom-call(bf16[16,128,2048]{2,1,0:T(8,128)(2,1)} %bitcast.203), custom_call_target="tpu_custom_call" | custom-call | bytes 125829120 | tf_op jit(solution)/shard_map/pallas_call | solution.py:383
  1064.4 10.6 fusion.112
  1091.8 6.8 concatenate.115
  1102.1 29.4 %shard_map.312 = f32[128,640]{1,0:T(8,128)} custom-call(bf16[16,128,640]{2,1,0:T(8,128)(2,1)} %bitcast.197), custom_call_target="tpu_custom_call" | custom-call | bytes 39321600 | tf_op jit(solution)/shard_map/pallas_call | solution.py:383
  1154.6 7.7 all-to-all-done.3
  (437 shorter events, 214.8 us)
Async XLA Ops:
  7.2 25.8 %copy-start.70 = (bf16[64,2816]{1,0:T(8,128)(2,1)S(1)}, bf16[64,2816]{1,0:T(8,128)(2,1)}, u32[]{:S(2)}) copy-start(bf16[64,2816]{1,0:T(8,128)(2,1)} %param.31) | copy-start | bytes 1081348
  7.2 285.1 %all-gather.4.cloned.1.call-start = ((), (), s32[]{:S(2)}) async-start(), calls=%async_computation.8 | async-start | bytes 8912896 | tf_op jit(solution)/shard_map/all_gather | solution.py:129
  7.9 346.7 %all-gather.6.cloned.1.call-start = ((), (), s32[]{:S(2)}) async-start(), calls=%async_computation.9 | async-start | bytes 8650752 | tf_op jit(solution)/shard_map/all_gather | solution.py:129
  12.1 24.3 %all-to-all-start.1 = ((bf16[16,17,256]{2,1,0:T(8,128)(2,1)}), bf16[16,17,256]{2,1,0:T(8,128)(2,1)S(1)}, u32[]{:S(2)}, u32[]{:S(2)}) async-start(bf16[16,17,256]{2,1,0:T(8,128)(2,1)} %copy.226), calls=%async_computation.1 | async-start | bytes 393216 | tf_op jit(solution)/shard_map/all_to_all | solution.py:125
  19.6 465.6 %all-gather.8.cloned.1.call-start = ((), (), s32[]{:S(2)}) async-start(), calls=%async_computation.10 | async-start | bytes 8912896 | tf_op jit(solution)/shard_map/all_gather | solution.py:129
  24.3 23.9 %collective-permute-start = (bf16[64,640]{1,0:T(8,128)(2,1)}, bf16[64,640]{1,0:T(8,128)(2,1)}, u32[]{:S(2)}, u32[]{:S(2)}) collective-permute-start(bf16[64,640]{1,0:T(8,128)(2,1)} %concatenate.87), channel_id=1, source_target_pairs={{0,16},{16,0},{1,17},{17,1},{2,18},{18,2},{3,19},{19,3},{4,20},{20... | collective-permute-start | bytes 245768 | tf_op jit(solution)/shard_map/ppermute | solution.py:88
  25.8 251.5 %collective-permute-start.5 = (bf16[1024,1408]{1,0:T(8,128)(2,1)}, bf16[1024,1408]{1,0:T(8,128)(2,1)}, u32[]{:S(2)}, u32[]{:S(2)}) collective-permute-start(bf16[1024,1408]{1,0:T(8,128)(2,1)} %bitcast.224), channel_id=1, source_target_pairs={{0,16},{16,0},{1,17},{17,1},{2,18},{18,2},{3,19},{19,3},{4,20},{20... | collective-permute-start | bytes 8650760 | tf_op jit(solution)/shard_map/ppermute | solution.py:88
  26.4 256.1 %collective-permute-start.6 = (bf16[1024,1408]{1,0:T(8,128)(2,1)}, bf16[1024,1408]{1,0:T(8,128)(2,1)}, u32[]{:S(2)}, u32[]{:S(2)}) collective-permute-start(bf16[1024,1408]{1,0:T(8,128)(2,1)} %bitcast.225), channel_id=1, source_target_pairs={{0,16},{16,0},{1,17},{17,1},{2,18},{18,2},{3,19},{19,3},{4,20},{20... | collective-permute-start | bytes 8650760 | tf_op jit(solution)/shard_map/ppermute | solution.py:88
  27.9 259.7 %collective-permute-start.7 = (bf16[704,2048]{1,0:T(8,128)(2,1)}, bf16[704,2048]{1,0:T(8,128)(2,1)}, u32[]{:S(2)}, u32[]{:S(2)}) collective-permute-start(bf16[704,2048]{1,0:T(8,128)(2,1)} %bitcast.226), channel_id=1, source_target_pairs={{0,16},{16,0},{1,17},{17,1},{2,18},{18,2},{3,19},{19,3},{4,20},{20... | collective-permute-start | bytes 8650760 | tf_op jit(solution)/shard_map/ppermute | solution.py:88
  28.4 218.9 %collective-permute-start.4 = (bf16[88,2048]{1,0:T(8,128)(2,1)}, bf16[88,2048]{1,0:T(8,128)(2,1)}, u32[]{:S(2)}, u32[]{:S(2)}) collective-permute-start(bf16[88,2048]{1,0:T(8,128)(2,1)} %param.33), channel_id=1, source_target_pairs={{0,16},{16,0},{1,17},{17,1},{2,18},{18,2},{3,19},{19,3},{4,20},{20... | collective-permute-start | bytes 1081352 | tf_op jit(solution)/shard_map/ppermute | solution.py:88
  36.4 81.8 %all-to-all-start.2 = ((bf16[16,64,352]{2,1,0:T(8,128)(2,1)}), bf16[16,64,352]{2,1,0:T(8,128)(2,1)S(1)}, u32[]{:S(2)}, u32[]{:S(2)}) async-start(bf16[16,64,352]{2,1,0:T(8,128)(2,1)} %pad_maximum_fusion.16), calls=%async_computation.2 | async-start | bytes 1572864 | tf_op jit(solution)/shard_map/all_to_all | solution.py:125
  43.9 265.6 %copy-start.12 = (f32[2048,32]{0,1:T(8,128)}, f32[2048,32]{0,1:T(8,128)S(1)}, u32[]{:S(2)}) copy-start(f32[2048,32]{0,1:T(8,128)S(1)} %get-tuple-element.21) | copy-start | bytes 786436
  43.9 265.5 %copy-start.14 = (f32[2048,32]{0,1:T(8,128)}, f32[2048,32]{0,1:T(8,128)S(1)}, u32[]{:S(2)}) copy-start(f32[2048,32]{0,1:T(8,128)S(1)} %get-tuple-element.20) | copy-start | bytes 786436
  118.2 129.1 %all-to-all-start = ((bf16[16,64,192]{2,1,0:T(8,128)(2,1)}), bf16[16,64,192]{2,1,0:T(8,128)(2,1)}, u32[]{:S(2)}, u32[]{:S(2)}) async-start(bf16[16,64,192]{2,1,0:T(8,128)(2,1)} %bitcast.179), calls=%async_computation | async-start | bytes 1048576 | tf_op jit(solution)/shard_map/all_to_all | solution.py:125
  122.5 549.8 %reduce-scatter.3.cloned.1.call-start = ((), (), s32[]{:S(2)}) async-start(), calls=%async_computation.11 | async-start | bytes 8912896 | tf_op jit(solution)/shard_map/reduce_scatter | solution.py:133
  127.0 178.5 %copy-start.77 = (f32[2048]{0:T(1024)}, f32[2048]{0:T(1024)S(1)}, u32[]{:S(2)}) copy-start(f32[2048]{0:T(1024)S(1)} %get-tuple-element.110) | copy-start | bytes 24580
  127.0 234.3 %copy-start.74 = (f32[2048]{0:T(1024)}, f32[2048]{0:T(1024)S(1)}, u32[]{:S(2)}) copy-start(f32[2048]{0:T(1024)S(1)} %get-tuple-element.108) | copy-start | bytes 24580
  127.2 191.4 %copy-start.81 = (f32[512]{0:T(512)}, f32[512]{0:T(512)S(1)}, u32[]{:S(2)}) copy-start(f32[512]{0:T(512)S(1)} %mul.396) | copy-start | bytes 6148
  128.7 121.2 %collective-permute-start.2 = (bf16[256,256]{1,0:T(8,128)(2,1)}, bf16[256,256]{1,0:T(8,128)(2,1)}, u32[]{:S(2)}, u32[]{:S(2)}) collective-permute-start(bf16[256,256]{1,0:T(8,128)(2,1)} %bitcast.18), channel_id=1, source_target_pairs={{0,16},{16,0},{1,17},{17,1},{2,18},{18,2},{3,19},{19,3},{4,20},{20... | collective-permute-start | bytes 393224 | tf_op jit(solution)/shard_map/ppermute | solution.py:88
  132.1 144.1 %copy-start.29 = (bf16[1024,352]{0,1:T(8,128)(2,1)S(1)}, bf16[1024,352]{0,1:T(8,128)(2,1)}, u32[]{:S(2)}) copy-start(bf16[1024,352]{0,1:T(8,128)(2,1)} %copy.239) | copy-start | bytes 2162692
  247.3 30.0 %copy-start.30 = (bf16[1,1024,1408]{2,1,0:T(8,128)(2,1)S(1)}, bf16[1,1024,1408]{2,1,0:T(8,128)(2,1)}, u32[]{:S(2)}) copy-start(bf16[1,1024,1408]{2,1,0:T(8,128)(2,1)} %param.35) | copy-start | bytes 8650756
  247.3 15.0 %collective-permute-start.1 = (bf16[1024,192]{1,0:T(8,128)(2,1)}, bf16[1024,192]{1,0:T(8,128)(2,1)S(1)}, u32[]{:S(2)}, u32[]{:S(2)}) collective-permute-start(bf16[1024,192]{1,0:T(8,128)(2,1)} %bitcast.8), channel_id=1, source_target_pairs={{0,16},{16,0},{1,17},{17,1},{2,18},{18,2},{3,19},{19,3},{4,20},{20... | collective-permute-start | bytes 1179656 | tf_op jit(solution)/shard_map/ppermute | solution.py:88
  249.9 26.3 %collective-permute-start.3 = (bf16[1024,352]{0,1:T(8,128)(2,1)}, bf16[1024,352]{0,1:T(8,128)(2,1)S(1)}, u32[]{:S(2)}, u32[]{:S(2)}) collective-permute-start(bf16[1024,352]{0,1:T(8,128)(2,1)} %copy.239), channel_id=1, source_target_pairs={{0,16},{16,0},{1,17},{17,1},{2,18},{18,2},{3,19},{19,3},{4,20},{20... | collective-permute-start | bytes 2162696 | tf_op jit(solution)/shard_map/ppermute | solution.py:88
  255.1 63.5 %copy-start.61 = (bf16[256,256]{1,0:T(8,128)(2,1)}, bf16[256,256]{1,0:T(8,128)(2,1)S(1)}, u32[]{:S(2)}) copy-start(bf16[256,256]{1,0:T(8,128)(2,1)S(1)} %get-tuple-element.145) | copy-start | bytes 393220
  334.8 19.9 %copy-start.7 = (bf16[2,64,2048]{2,1,0:T(8,128)(2,1)S(1)}, bf16[2,64,2048]{2,1,0:T(8,128)(2,1)}, u32[]{:S(2)}) copy-start(bf16[2,64,2048]{2,1,0:T(8,128)(2,1)} %param.19) | copy-start | bytes 1572868
  363.2 59.6 %copy-start.43 = (bf16[1024,352]{0,1:T(8,128)(2,1)S(1)}, bf16[1024,352]{0,1:T(8,128)(2,1)}, u32[]{:S(2)}) copy-start(bf16[1024,352]{0,1:T(8,128)(2,1)} %get-tuple-element.131) | copy-start | bytes 2162692
  363.2 59.6 %copy-start.44 = (bf16[1024,352]{0,1:T(8,128)(2,1)S(1)}, bf16[1024,352]{0,1:T(8,128)(2,1)}, u32[]{:S(2)}) copy-start(bf16[1024,352]{0,1:T(8,128)(2,1)} %get-tuple-element.132) | copy-start | bytes 2162692
  363.2 59.6 %copy-start.73 = (bf16[2048,16]{0,1:T(8,128)(2,1)S(1)}, bf16[2048,16]{0,1:T(8,128)(2,1)}, u32[]{:S(2)}) copy-start(bf16[2048,16]{0,1:T(8,128)(2,1)} %copy.241) | copy-start | bytes 196612
  565.0 68.3 %copy-start.59 = (bf16[2048,176]{0,1:T(8,128)(2,1)S(1)}, bf16[2048,176]{0,1:T(8,128)(2,1)}, u32[]{:S(2)}) copy-start(bf16[2048,176]{0,1:T(8,128)(2,1)} %get-tuple-element.125) | copy-start | bytes 2162692
  565.0 68.4 %copy-start.60 = (bf16[2048,176]{0,1:T(8,128)(2,1)S(1)}, bf16[2048,176]{0,1:T(8,128)(2,1)}, u32[]{:S(2)}) copy-start(bf16[2048,176]{0,1:T(8,128)(2,1)} %get-tuple-element.126) | copy-start | bytes 2162692
  640.7 24.5 %collective-permute-start.11 = (bf16[1024,352]{0,1:T(8,128)(2,1)S(1)}, bf16[1024,352]{0,1:T(8,128)(2,1)S(1)}, u32[]{:S(2)}, u32[]{:S(2)}) collective-permute-start(bf16[1024,352]{0,1:T(8,128)(2,1)S(1)} %dynamic-slice_convert_fusion), channel_id=1, source_target_pairs={{0,16},{16,0},{1,17},{17,1},{2,18},{18,2},{3,19},{19,3},{4,20},{20... | collective-permute-start | bytes 2162696 | tf_op jit(solution)/shard_map/ppermute | solution.py:88
  647.7 218.4 %collective-permute-start.13 = (bf16[1024,1408]{1,0:T(8,128)(2,1)}, bf16[1024,1408]{1,0:T(8,128)(2,1)}, u32[]{:S(2)}, u32[]{:S(2)}) collective-permute-start(bf16[1024,1408]{1,0:T(8,128)(2,1)} %convolution_convert_fusion.2), channel_id=1, source_target_pairs={{0,16},{16,0},{1,17},{17,1},{2,18},{18,2},{3,19},{19,3},{4,20},{20... | collective-permute-start | bytes 8650760 | tf_op jit(solution)/shard_map/ppermute | solution.py:88
  654.7 221.1 %collective-permute-start.14 = (bf16[1024,1408]{1,0:T(8,128)(2,1)}, bf16[1024,1408]{1,0:T(8,128)(2,1)}, u32[]{:S(2)}, u32[]{:S(2)}) collective-permute-start(bf16[1024,1408]{1,0:T(8,128)(2,1)} %convolution_convert_fusion.1), channel_id=1, source_target_pairs={{0,16},{16,0},{1,17},{17,1},{2,18},{18,2},{3,19},{19,3},{4,20},{20... | collective-permute-start | bytes 8650760 | tf_op jit(solution)/shard_map/ppermute | solution.py:88
  660.1 222.7 %collective-permute-start.15 = (bf16[704,2048]{1,0:T(8,128)(2,1)}, bf16[704,2048]{1,0:T(8,128)(2,1)}, u32[]{:S(2)}, u32[]{:S(2)}) collective-permute-start(bf16[704,2048]{1,0:T(8,128)(2,1)} %convolution_convert_fusion.5), channel_id=1, source_target_pairs={{0,16},{16,0},{1,17},{17,1},{2,18},{18,2},{3,19},{19,3},{4,20},{20... | collective-permute-start | bytes 8650760 | tf_op jit(solution)/shard_map/ppermute | solution.py:88
  666.6 185.6 %all-to-all-start.5 = ((bf16[16,64,352]{2,1,0:T(8,128)(2,1)}), bf16[16,64,352]{2,1,0:T(8,128)(2,1)S(1)}, u32[]{:S(2)}, u32[]{:S(2)}) async-start(bf16[16,64,352]{2,1,0:T(8,128)(2,1)} %bitcast.69), calls=%async_computation.7 | async-start | bytes 1572864 | tf_op jit(solution)/shard_map/all_to_all | solution.py:125
  672.1 492.2 %reduce-scatter.5.cloned.1.call-start = ((), (), s32[]{:S(2)}) async-start(), calls=%async_computation.12 | async-start | bytes 8650752 | tf_op jit(solution)/shard_map/reduce_scatter | solution.py:133
  682.0 168.2 %collective-permute-start.12 = (bf16[88,2048]{1,0:T(8,128)(2,1)S(1)}, bf16[88,2048]{1,0:T(8,128)(2,1)S(1)}, u32[]{:S(2)}, u32[]{:S(2)}) collective-permute-start(bf16[88,2048]{1,0:T(8,128)(2,1)S(1)} %dynamic-slice_convert_fusion.2), channel_id=1, source_target_pairs={{0,16},{16,0},{1,17},{17,1},{2,18},{18,2},{3,19},{19,3},{4,20},{20... | collective-permute-start | bytes 1081352 | tf_op jit(solution)/shard_map/ppermute | solution.py:88
  866.1 23.8 %slice-start = ((s8[8388608]{0:T(1024)(128)(4,1)}), s8[4194304]{0:T(1024)(128)(4,1)S(1)}, s32[]{:S(2)}) async-start(s8[8388608]{0:T(1024)(128)(4,1)} %bitcast.184), calls=%async_computation.13 | async-start | bytes 8388608
  890.0 59.3 %copy-start.19 = (bf16[2,1024,128]{2,1,0:T(8,128)(2,1)S(1)}, bf16[2,1024,128]{2,1,0:T(8,128)(2,1)}, u32[]{:S(2)}) copy-start(bf16[2,1024,128]{2,1,0:T(8,128)(2,1)} %convolution_convert_fusion.9.x_ref) | copy-start | bytes 1572868
  890.0 60.7 %copy-start.48 = (bf16[16,2,64,128]{3,2,0,1:T(8,128)(2,1)S(1)}, bf16[16,2,64,128]{3,2,0,1:T(8,128)(2,1)}, u32[]{:S(2)}) copy-start(bf16[16,2,64,128]{3,2,0,1:T(8,128)(2,1)} %copy-done.47) | copy-start | bytes 1572868
  1003.3 61.1 %copy-start.78 = (f32[2048]{0:T(1024)S(1)}, f32[2048]{0:T(1024)}, u32[]{:S(2)}) copy-start(f32[2048]{0:T(1024)} %copy-done.77) | copy-start | bytes 24580
  1003.3 75.5 %slice-start.4 = ((s8[4718592]{0:T(1024)(128)(4,1)}), s8[524288]{0:T(1024)(128)(4,1)S(1)}, s32[]{:S(2)}) async-start(s8[4718592]{0:T(1024)(128)(4,1)} %bitcast.189), calls=%async_computation.17 | async-start | bytes 1048576
  1077.1 61.6 %collective-permute-start.8 = (bf16[1024,192]{0,1:T(8,128)(2,1)}, bf16[1024,192]{0,1:T(8,128)(2,1)}, u32[]{:S(2)}, u32[]{:S(2)}) collective-permute-start(bf16[1024,192]{0,1:T(8,128)(2,1)} %dynamic-slice_convert_fusion.1), channel_id=1, source_target_pairs={{0,16},{16,0},{1,17},{17,1},{2,18},{18,2},{3,19},{19,3},{4,20},{20... | collective-permute-start | bytes 1179656 | tf_op jit(solution)/shard_map/ppermute | solution.py:88
  1080.5 51.1 %collective-permute-start.10 = (bf16[256,256]{1,0:T(8,128)(2,1)S(1)}, bf16[256,256]{1,0:T(8,128)(2,1)S(1)}, u32[]{:S(2)}, u32[]{:S(2)}) collective-permute-start(bf16[256,256]{1,0:T(8,128)(2,1)S(1)} %dynamic-slice_convert_fusion.3), channel_id=1, source_target_pairs={{0,16},{16,0},{1,17},{17,1},{2,18},{18,2},{3,19},{19,3},{4,20},{20... | collective-permute-start | bytes 393224 | tf_op jit(solution)/shard_map/ppermute | solution.py:88
  1098.6 33.0 %copy-start.72 = (f32[512,256]{1,0:T(8,128)S(1)}, f32[512,256]{1,0:T(8,128)}, u32[]{:S(2)}) copy-start(f32[512,256]{1,0:T(8,128)} %copy-done.71) | copy-start | bytes 1572868
  1132.3 11.5 all-to-all-start.4
  1136.8 13.0 %collective-permute-start.9 = (bf16[64,640]{1,0:T(8,128)(2,1)S(1)}, bf16[64,640]{1,0:T(8,128)(2,1)}, u32[]{:S(2)}, u32[]{:S(2)}) collective-permute-start(bf16[64,640]{1,0:T(8,128)(2,1)S(1)} %dynamic-slice_convert_fusion.4), channel_id=1, source_target_pairs={{0,16},{16,0},{1,17},{17,1},{2,18},{18,2},{3,19},{19,3},{4,20},{20... | collective-permute-start | bytes 245768 | tf_op jit(solution)/shard_map/ppermute | solution.py:88
  1144.4 17.8 %all-to-all-start.3 = ((bf16[16,64,192]{2,1,0:T(8,128)(2,1)}), bf16[16,64,192]{2,1,0:T(8,128)(2,1)S(1)}, u32[]{:S(2)}, u32[]{:S(2)}) async-start(bf16[16,64,192]{2,1,0:T(8,128)(2,1)} %bitcast.233), calls=%async_computation.4 | async-start | bytes 1048576 | tf_op jit(solution)/shard_map/all_to_all | solution.py:125
  (85 other events, 566.9 us)
Sparse Core Ops, SparseCore 0:
  10.2 95.7 all-gather.3
  108.9 101.2 all-gather.5
  212.4 72.9 all-gather.7
  497.3 110.2 reduce-scatter.2
  680.9 152.2 reduce-scatter.4

commit v2 on v1

--- a/solution.py
+++ b/solution.py
@@ -164,57 +164,91 @@
     return partner, mate
 
 
-def gather_kernel(x_ref, out_ref, own_sem, send_sem, recv_sem):
+def greet_all(me):
+    barrier = pltpu.get_barrier_semaphore()
+    for step in range(1, 16):
+        pl.semaphore_signal(
+            barrier, inc=1, device_id=at_expert((me + step) % 16), device_id_type=MESH
+        )
+    pl.semaphore_wait(barrier, 15)
+
+
+def gather_kernel(n, m, *refs):
+    x_refs, swap_refs = refs[:n], refs[n : n + m]
+    outs, swap_outs = refs[n + m : 2 * n + m], refs[2 * n + m : 2 * (n + m)]
+    own_sem, send_sem, recv_sem, swap_send, swap_recv = refs[2 * (n + m) :]
     me, line, pair, core = grid_place()
-    partner, mate = greet_neighbours(me, line, pair, core)
-    own = pltpu.make_async_copy(x_ref, out_ref.at[me], own_sem)
-    own.start()
-
-    def copy(source, origin, way, to):
+    if m:
+        greet_all(me)
+        partner, mate = me + 1 - 2 * core, me + 2 - 4 * pair
+    else:
+        partner, mate = greet_neighbours(me, line, pair, core)
+
+    def own_copy(i):
+        if i < n:
+            return pltpu.make_async_copy(x_refs[i], outs[i].at[me], own_sem.at[i])
+        i -= n
+        return pltpu.make_async_copy(
+            swap_refs[i].at[me], swap_outs[i].at[me], own_sem.at[n + i]
+        )
+
+    def copy(i, source, origin, way, to):
         return pltpu.make_async_remote_copy(
             src_ref=source,
-            dst_ref=out_ref.at[origin],
-            send_sem=send_sem.at[origin, way],
-            recv_sem=recv_sem.at[origin],
+            dst_ref=outs[i].at[origin],
+            send_sem=send_sem.at[i, origin, way],
+            recv_sem=recv_sem.at[i, origin],
             device_id=at_expert(to),
             device_id_type=MESH,
         )
 
-    def arrived(origin):
-        copy(out_ref.at[origin], origin, 0, partner).wait_recv()
-
-    def along(origin, source, upward, downward, act):
+    def swap_copy(i, step):
+        to = (me + step) % 16
+        return pltpu.make_async_remote_copy(
+            src_ref=swap_refs[i].at[to],
+            dst_ref=swap_outs[i].at[me],
+            send_sem=swap_send.at[i, step],
+            recv_sem=swap_recv.at[i, step],
+            device_id=at_expert(to),
+            device_id_type=MESH,
+        )
+
+    def arrived(i, origin):
+        copy(i, outs[i].at[origin], origin, 0, partner).wait_recv()
+
+    def along(i, origin, source, upward, downward, act):
         if upward:
 
             @pl.when(line < 3)
             def _():
-                act(copy(source, origin, 0, me + 4))
+                act(copy(i, source, origin, 0, me + 4))
 
         if downward:
 
             @pl.when(line > 0)
             def _():
-                act(copy(source, origin, 1, me - 4))
-
-        act(copy(source, origin, 2, mate))
-        act(copy(source, origin, 3, partner))
+                act(copy(i, source, origin, 1, me - 4))
+
+        act(copy(i, source, origin, 2, mate))
+        act(copy(i, source, origin, 3, partner))
 
     def walk(act, wait):
-        along(me, x_ref, True, True, act)
         for far in range(1, 5):
             if far < 4:
 
                 @pl.when(line >= far)
                 def _():
                     origin = me - 4 * far
-                    wait(origin)
-                    along(origin, out_ref.at[origin], True, False, act)
+                    for i in range(n):
+                        wait(i, origin)
+                        along(i, origin, outs[i].at[origin], True, False, act)
 
                 @pl.when(line + far <= 3)
                 def _():
                     origin = me + 4 * far
-                    wait(origin)
-                    along(origin, out_ref.at[origin], False, True, act)
+                    for i in range(n):
+                        wait(i, origin)
+                        along(i, origin, outs[i].at[origin], False, True, act)
 
             for sign in (-1, 1) if far > 1 else (1,):
                 step = sign * (far - 1)
@@ -222,43 +256,68 @@
                 @pl.when((line + step >= 0) & (line + step <= 3))
                 def _():
                     origin = mate + 4 * step
-                    wait(origin)
-                    act(copy(out_ref.at[origin], origin, 3, partner))
-
-    walk(lambda c: c.start(), arrived)
-    for index in range(8):
-        arrived(2 * index + 1 - core)
-    walk(lambda c: c.wait_send(), lambda origin: None)
-    own.wait()
-
-
-def ring_gather(value, collective):
-    rows, columns = value.shape
-    sent = 15 * rows * columns * 2
-    out = pl.pallas_call(
-        gather_kernel,
-        out_shape=jax.ShapeDtypeStruct((16, rows, columns), value.dtype),
-        in_specs=[pl.BlockSpec(memory_space=pltpu.VMEM)],
-        out_specs=pl.BlockSpec(memory_space=pl.ANY),
+                    for i in range(n):
+                        wait(i, origin)
+                        act(copy(i, outs[i].at[origin], origin, 3, partner))
+
+    def start(c):
+        c.start()
+
+    def sent(c):
+        c.wait_send()
+
+    for i in range(n):
+        along(i, me, x_refs[i], True, True, start)
+    for i in range(m):
+        for step in range(1, 16):
+            swap_copy(i, step).start()
+    for i in range(n + m):
+        own_copy(i).start()
+    walk(start, arrived)
+    for i in range(n):
+        for index in range(8):
+            arrived(i, 2 * index + 1 - core)
+    for i in range(n):
+        along(i, me, x_refs[i], True, True, sent)
+    walk(sent, lambda i, origin: None)
+    for i in range(m):
+        for step in range(1, 16):
+            swap_copy(i, step).wait()
+    for i in range(n + m):
+        own_copy(i).wait()
+
+
+def ring_gather(values, swaps, collective):
+    n, m = len(values), len(swaps)
+    sent = 2 * (15 * sum(v.size for v in values) + sum(v.size for v in swaps))
+    sems = pltpu.SemaphoreType.DMA
+    anywhere = pl.BlockSpec(memory_space=pl.ANY)
+    outs = pl.pallas_call(
+        functools.partial(gather_kernel, n, m),
+        out_shape=[jax.ShapeDtypeStruct((16,) + v.shape, v.dtype) for v in values]
+        + [jax.ShapeDtypeStruct(v.shape, v.dtype) for v in swaps],
+        in_specs=[pl.BlockSpec(memory_space=pltpu.VMEM)] * (n + m),
+        out_specs=[anywhere] * (n + m),
         scratch_shapes=[
-            pltpu.SemaphoreType.DMA,
-            pltpu.SemaphoreType.DMA((16, 4)),
-            pltpu.SemaphoreType.DMA((16,)),
+            sems((n + m,)),
+            sems((n, 16, 4)),
+            sems((n, 16)),
+            sems((max(m, 1), 16)),
+            sems((max(m, 1), 16)),
         ],
         compiler_params=pltpu.CompilerParams(collective_id=collective, has_side_effects=True),
         cost_estimate=pl.CostEstimate(flops=0, bytes_accessed=16 * sent, transcendentals=0),
-    )(value)
-    return out.reshape(16 * rows, columns)
-
-
-def scatter_kernel(
-    p_ref, out_ref, chip, mate_in, up_in, down_in, total,
-    core_send, core_recv, mate_send, mate_recv, up_send, up_recv, down_send, down_recv,
-):
+    )(*values, *swaps)
+    return [o.reshape(-1, o.shape[-1]) for o in outs[:n]] + list(outs[n:])
+
+
+def scatter_kernel(n, *refs):
+    parts = [(refs[i], refs[n + i]) + refs[2 * n + 5 * i : 2 * n + 5 * i + 5] for i in range(n)]
+    (
+        core_send, core_recv, mate_send, mate_recv, up_send, up_recv, down_send, down_recv,
+    ) = refs[7 * n :]
     me, line, pair, core = grid_place()
     partner, mate = greet_neighbours(me, line, pair, core)
-    rows = p_ref.shape[1]
-    tile = 16
 
     def remote(source, target, send, recv, to):
         return pltpu.make_async_remote_copy(
@@ -266,31 +325,34 @@
             device_id=at_expert(to), device_id_type=MESH,
         )
 
-    def core_copy(index):
+    def core_copy(i, index):
         return remote(
-            p_ref.at[2 * index + 1 - core], chip.at[index],
-            core_send.at[index], core_recv.at[index], partner,
-        )
-
-    def mate_copy(dest):
+            parts[i][0].at[2 * index + 1 - core], parts[i][2].at[index],
+            core_send.at[i, index], core_recv.at[i, index], partner,
+        )
+
+    def mate_copy(i, dest):
         return remote(
-            total.at[2 * dest + 1 - pair], mate_in.at[dest],
-            mate_send.at[dest], mate_recv.at[dest], mate,
-        )
-
-    def up_copy(dest):
+            parts[i][6].at[2 * dest + 1 - pair], parts[i][3].at[dest],
+            mate_send.at[i, dest], mate_recv.at[i, dest], mate,
+        )
+
+    def up_copy(i, dest):
         return remote(
-            total.at[2 * dest + pair], up_in.at[dest], up_send.at[dest], up_recv.at[dest], me + 4
-        )
-
-    def down_copy(dest):
+            parts[i][6].at[2 * dest + pair], parts[i][4].at[dest],
+            up_send.at[i, dest], up_recv.at[i, dest], me + 4,
+        )
+
+    def down_copy(i, dest):
         return remote(
-            total.at[2 * dest + pair], down_in.at[dest],
-            down_send.at[dest], down_recv.at[dest], me - 4,
+            parts[i][6].at[2 * dest + pair], parts[i][5].at[dest],
+            down_send.at[i, dest], down_recv.at[i, dest], me - 4,
         )
 
     def add(target, left, right):
-        @pl.loop(0, rows // tile)
+        tile = 16
+
+        @pl.loop(0, left.shape[0] // tile)
         def _(i):
             at = pl.ds(pl.multiple_of(i * tile, tile), tile)
             target[at, :] = (left[at, :].astype(f32) + right[at, :].astype(f32)).astype(
@@ -303,103 +365,88 @@
 
                 @pl.when((line + step >= 0) & (line + step <= 3))
                 def _():
-                    act(line + step, step)
-
-    def send_core(dest, step):
-        core_copy(2 * dest + 1 - pair).start()
-
-    def send_core_own(dest, step):
-        core_copy(2 * dest + pair).start()
-
-    def chip_sum(index):
-        core_copy(index).wait_recv()
-        add(total.at[index], p_ref.at[2 * index + core], chip.at[index])
-
-    def to_mate(dest, step):
-        chip_sum(2 * dest + 1 - pair)
-        mate_copy(dest).start()
-
-    def keep(dest, step):
-        chip_sum(2 * dest + pair)
-
-    def along(dest, step):
+                    for i in range(n):
+                        act(i, line + step, step)
+
+    def send_core(i, dest, step):
+        core_copy(i, 2 * dest + 1 - pair).start()
+
+    def send_core_own(i, dest, step):
+        core_copy(i, 2 * dest + pair).start()
+
+    def chip_sum(i, index):
+        core_copy(i, index).wait_recv()
+        add(parts[i][6].at[index], parts[i][0].at[2 * index + core], parts[i][2].at[index])
+
+    def to_mate(i, dest, step):
+        chip_sum(i, 2 * dest + 1 - pair)
+        mate_copy(i, dest).start()
+
+    def keep(i, dest, step):
+        chip_sum(i, 2 * dest + pair)
+
+    def along(i, dest, step):
+        out, up_in, down_in, total = parts[i][1], parts[i][4], parts[i][5], parts[i][6]
         mine = total.at[2 * dest + pair]
-        mate_copy(dest).wait_recv()
+        mate_copy(i, dest).wait_recv()
         if step == 0:
-            mine, kept = out_ref, mine
-            add(mine, kept, mate_in.at[dest])
+            add(out, mine, parts[i][3].at[dest])
+            mine = out
         else:
-            add(mine, mine, mate_in.at[dest])
-        if step > 0:
+            add(mine, mine, parts[i][3].at[dest])
+        if step >= 0:
 
             @pl.when(line > 0)
             def _():
-                up_copy(dest).wait_recv()
+                up_copy(i, dest).wait_recv()
                 add(mine, mine, up_in.at[dest])
 
-            up_copy(dest).start()
-        elif step < 0:
+        if step <= 0:
 
             @pl.when(line < 3)
             def _():
-                down_copy(dest).wait_recv()
+                down_copy(i, dest).wait_recv()
                 add(mine, mine, down_in.at[dest])
 
-            down_copy(dest).start()
-        else:
-
-            @pl.when(line > 0)
-            def _():
-                up_copy(dest).wait_recv()
-                add(mine, mine, up_in.at[dest])
-
-            @pl.when(line < 3)
-            def _():
-                down_copy(dest).wait_recv()
-                add(mine, mine, down_in.at[dest])
-
-    def finish(dest, step):
-        mate_copy(dest).wait_send()
-        core_copy(2 * dest + 1 - pair).wait_send()
-        core_copy(2 * dest + pair).wait_send()
         if step > 0:
-            up_copy(dest).wait_send()
+            up_copy(i, dest).start()
         elif step < 0:
-            down_copy(dest).wait_send()
-
-    farthest(send_core)
-    farthest(send_core_own)
-    farthest(to_mate)
-    farthest(keep)
-    farthest(along)
-    farthest(finish)
-
-
-def ring_scatter(value, collective):
-    rows, columns = value.shape[0] // 16, value.shape[1]
-    block = lambda n: pltpu.VMEM((n, rows, columns), bf16)
-    sems = lambda n: pltpu.SemaphoreType.DMA((n,))
-    sent = 15 * rows * columns * 2
+            down_copy(i, dest).start()
+
+    def finish(i, dest, step):
+        mate_copy(i, dest).wait_send()
+        core_copy(i, 2 * dest + 1 - pair).wait_send()
+        core_copy(i, 2 * dest + pair).wait_send()
+        if step > 0:
+            up_copy(i, dest).wait_send()
+        elif step < 0:
+            down_copy(i, dest).wait_send()
+
+    for act in (send_core, send_core_own, to_mate, keep, along, finish):
+        farthest(act)
+
+
+def ring_scatter(values, collective):
+    n = len(values)
+    shapes = [(v.shape[0] // 16, v.shape[1]) for v in values]
+    buffers = [pltpu.VMEM((k,) + s, bf16) for s in shapes for k in (8, 4, 4, 4, 8)]
+    sent = 30 * sum(a * b for a, b in shapes)
+    vmem = pl.BlockSpec(memory_space=pltpu.VMEM)
     return pl.pallas_call(
-        scatter_kernel,
-        out_shape=jax.ShapeDtypeStruct((rows, columns), f32),
-        in_specs=[pl.BlockSpec(memory_space=pltpu.VMEM)],
-        out_specs=pl.BlockSpec(memory_space=pltpu.VMEM),
-        scratch_shapes=[block(8), block(4), block(4), block(4), block(8)]
-        + [sems(8), sems(8), sems(4), sems(4), sems(4), sems(4), sems(4), sems(4)],
+        functools.partial(scatter_kernel, n),
+        out_shape=[jax.ShapeDtypeStruct(s, f32) for s in shapes],
+        in_specs=[vmem] * n,
+        out_specs=[vmem] * n,
+        scratch_shapes=buffers
+        + [pltpu.SemaphoreType.DMA((n, k)) for k in (8, 8, 4, 4, 4, 4, 4, 4)],
         compiler_params=pltpu.CompilerParams(collective_id=collective, has_side_effects=True),
         cost_estimate=pl.CostEstimate(flops=0, bytes_accessed=16 * sent, transcendentals=0),
-    )(value.reshape(16, rows, columns))
+    )(*[v.reshape((16,) + s) for v, s in zip(values, shapes)])
 
 
 def swap_kernel(source, target, x_ref, out_ref, own_sem, send_sem, recv_sem):
     me = lax.axis_index(EXPERT)
-    barrier = pltpu.get_barrier_semaphore()
-    for step in range(1, 16):
-        pl.semaphore_signal(
-            barrier, inc=1, device_id=at_expert((me + step) % 16), device_id_type=MESH
-        )
-    pl.semaphore_wait(barrier, 15)
+    greet_all(me)
 
     def copy(step):
         to = (me + step) % 16
@@ -505,7 +552,6 @@
         return value.reshape(seqs, groups, span, -1).transpose(1, 0, 2, 3).reshape(tokens, -1)
 
     x_low = inputs.reshape(own, width)
-    x_all = gather_rows(x_low, EXPERT)
     cot_own = cotangent.reshape(own, width)
 
     order = priority[:, None, :] < priority[:, :, None]
@@ -527,8 +573,19 @@
         ],
         axis=1,
     )
-    small_all = dp_gather(small)
-    small_all = ring_gather(small_all, 1)
+    small = dp_gather(small)
+    query_parts = query_weight.reshape(rows, HEADS, QD).transpose(1, 0, 2)
+    lup_rows = latent_up.shape[0]
+    code_rows = -(lup_rows + 1) % 16 + 1
+    code_part = jnp.pad(
+        codes.reshape(own, 1, experts).T, ((0, 0), (0, code_rows - 1), (0, HD + VD - own))
+    )
+    lup_parts = jnp.concatenate(
+        [latent_up.reshape(lup_rows, HEADS, HD + VD).transpose(1, 0, 2), code_part], axis=1
+    )
+    small_all, x_all, query_swap, lup_swap = ring_gather(
+        [small, x_low], [query_parts, lup_parts], 1
+    )
     small_all = (
         small_all.reshape(groups, replicas, rows, -1).transpose(1, 0, 2, 3).reshape(width, -1)
     )
@@ -539,16 +596,6 @@
     gain_moe = gains[:, 1]
     gain_lat = gains[:, 2].reshape(-1, rows)[:, : latent_gain.shape[0]].reshape(-1)
 
-    query_swap = expert_swap(query_weight.reshape(rows, HEADS, QD).transpose(1, 0, 2))
-    lup_rows = latent_up.shape[0]
-    code_row = jnp.pad(
-        codes.reshape(own, experts).T, ((0, 0), (0, HD + VD - own))
-    )[:, None, :]
-    lup_swap = expert_swap(
-        jnp.concatenate(
-            [latent_up.reshape(lup_rows, HEADS, HD + VD).transpose(1, 0, 2), code_row], axis=1
-        )
-    )
     wq = dp_gather(query_swap.reshape(groups * rows, QD))
     lup = dp_gather(lup_swap[:, :lup_rows].reshape(groups * lup_rows, HD + VD))
     code = lup_swap[:, lup_rows, :own].astype(f32).reshape(tokens)
@@ -560,9 +607,10 @@
             .reshape(groups, rows, hidden_own)
         )
 
-    gate_up_swap = expert_swap(
-        jnp.concatenate([columns_of(shared_gate), columns_of(shared_up)], axis=2)
-    )
+    gate_up_parts, query_swap = lax.optimization_barrier(
+        (jnp.concatenate([columns_of(shared_gate), columns_of(shared_up)], axis=2), query_swap)
+    )
+    gate_up_swap = expert_swap(gate_up_parts)
     gate_up = dp_gather(gate_up_swap.reshape(groups * rows, 2 * hidden_own))
     gate_up_router = jnp.concatenate([gate_up, router_all], axis=1)
     sdown = dp_gather(shared_down)
@@ -604,7 +652,7 @@
 
     x_second = x_low.astype(f32) + right_product(heads_own, out_t)
     normed_two, factor_two = norm_parts(x_second)
-    h_two = ring_gather((normed_two * gain_moe).astype(bf16), 2)
+    (h_two,) = ring_gather([(normed_two * gain_moe).astype(bf16)], [], 2)
 
     chunk = tokens // 2
     blocks = chunk // span
@@ -669,10 +717,21 @@
     routed_down_grad = dp_scatter_product(expert_hidden, slot_grad)
     routed_gate_grad = dp_scatter_product(expert_in, expert_a_grad)
     routed_up_grad = dp_scatter_product(expert_in, expert_b_grad)
-    h_two_grad = ring_scatter(h_two_partial.astype(bf16), 4)
+    (h_two_grad,) = ring_scatter([h_two_partial.astype(bf16)], 4)
     pre_weight_grad = left_product(h_two, pre_grad)
     sdown_owned = dp_scatter(sdown_grad)
     gate_up_owned = dp_scatter(pre_weight_grad[:, : 2 * hidden_own]).astype(bf16)
+    router_grad = pre_weight_grad[:, 2 * hidden_own :]
+
+    gmoe_grad = jnp.sum(h_two_grad * normed_two, axis=0)
+    x_second_grad = cot_own.astype(f32) + norm_back(h_two_grad * gain_moe, normed_two, factor_two)
+    attn_low = x_second_grad.astype(bf16)
+    heads_grad = product(attn_low, out_t).astype(bf16)
+    grad_s = tokens_to_heads(heads_grad.reshape(seqs, span, HEADS * VD), 5)
+    attn_low, gate_up_owned, grad_s = lax.optimization_barrier((attn_low, gate_up_owned, grad_s))
+    out_owned = (
+        scatter_rows(left_product(attn_low, heads_own).astype(bf16), BOTH).astype(f32).T
+    )
     gate_up_owned = expert_swap(
         gate_up_owned.reshape(groups, rows, 2 * hidden_own)
     ).astype(f32)
@@ -686,16 +745,6 @@
 
     sgate_owned = owned_columns(gate_up_owned[:, :, :hidden_own])
     sup_owned = owned_columns(gate_up_owned[:, :, hidden_own:])
-    router_grad = pre_weight_grad[:, 2 * hidden_own :]
-
-    gmoe_grad = jnp.sum(h_two_grad * normed_two, axis=0)
-    x_second_grad = cot_own.astype(f32) + norm_back(h_two_grad * gain_moe, normed_two, factor_two)
-    attn_low = x_second_grad.astype(bf16)
-    heads_grad = product(attn_low, out_t).astype(bf16)
-    grad_s = tokens_to_heads(heads_grad.reshape(seqs, span, HEADS * VD), 5)
-    out_owned = (
-        scatter_rows(left_product(attn_low, heads_own).astype(bf16), BOTH).astype(f32).T
-    )
     probs_grad = einsum("sqd,skd->sqk", grad_s, value_s)
     spread = jnp.sum(grad_s.astype(f32) * heads_s.astype(f32), axis=-1, keepdims=True)
     score_grad = (probs_attn.astype(f32) * (probs_grad - spread) * scale).astype(bf16)
@@ -721,18 +770,12 @@
     joint_weight = jnp.concatenate([wq, ldown_all], axis=1)
     h_one_partial = right_product(joint_grad, joint_weight)
     gattn_grad = jnp.sum(h_one_partial * normed_one, axis=0)
-    h_one_grad = ring_scatter(h_one_partial.astype(bf16), 6)
-    normed_own, factor_own = norm_parts(x_low.astype(f32))
-    input_grad = x_second_grad + norm_back(h_one_grad * gain_attn, normed_own, factor_own)
-    input_grad = input_grad.astype(bf16).reshape(seqs, span, width)
     joint_weight_grad = left_product(h_one, joint_grad)
-    q_owned = expert_swap(
-        dp_scatter(joint_weight_grad[:, :QD]).astype(bf16).reshape(groups, rows, QD)
-    ).astype(f32)
-    q_owned = q_owned.transpose(1, 0, 2).reshape(rows, HEADS * QD)
-    lup_owned = expert_swap(
-        dp_scatter(lup_grad).astype(bf16).reshape(groups, lup_rows, HD + VD)
-    ).astype(f32)
+    back_grad = jnp.concatenate([joint_weight_grad[:, :QD], lup_grad.reshape(width, -1)], axis=1)
+    back_grad = dp_scatter(back_grad).astype(bf16)
+    back_owned = expert_swap(back_grad.reshape(groups, rows, -1)).astype(f32)
+    q_owned = back_owned[:, :, :QD].transpose(1, 0, 2).reshape(rows, HEADS * QD)
+    lup_owned = back_owned[:, :, QD:].reshape(groups, lup_rows, HD + VD)
     lup_owned = lup_owned.transpose(1, 0, 2).reshape(lup_rows, HEADS * (HD + VD))
     glat_column = jnp.pad(
         glat_grad.reshape(-1, latent_gain.shape[0]), ((0, 0), (0, pad))
@@ -754,7 +797,10 @@
         .transpose(1, 0, 2, 3)
         .reshape(width, -1)
     )
-    small_owned = ring_scatter(small_grad, 7)
+    small_owned, h_one_grad = ring_scatter([small_grad, h_one_partial.astype(bf16)], 6)
+    normed_own, factor_own = norm_parts(x_low.astype(f32))
+    input_grad = x_second_grad + norm_back(h_one_grad * gain_attn, normed_own, factor_own)
+    input_grad = input_grad.astype(bf16).reshape(seqs, span, width)
     small_owned = dp_scatter(small_owned)
     ldown_owned = small_owned[:, : RANK + RD]
     router_owned = small_owned[:, RANK + RD : RANK + RD + experts]

time: 1180 us -> 988 us (0.84)
  waiting for transfers between devices: 311 us -> 51.4 us
  starting transfers between devices: 51.8 us -> 78.7 us
  local copies, waits for them, and re-layouts: 109 us -> 133 us
    ppermute x16 -> x15, waiting for transfers between devices: 299 us -> 50.7 us  [dp_swap(): return lax.ppermute(value, DP, [(0, 1), (1, 0)])]
    pallas_call x5 -> x4, Pallas kernels: 283 us -> 332 us  [the longest x2 181 us: ring_gather(): pl.pallas_call(functools.partial(gather_kernel, n, m), out_shape=[jax.Sha...]
    pallas_call x2, Pallas kernels: 72.5 us -> 32.2 us  [swap_call(): pl.pallas_call(functools.partial(swap_kernel, source, target), out_shape=...]
    all_to_all x6 -> x3, starting transfers between devices: 30.4 us -> 59.4 us  [expert_swap(): lax.all_to_all(value, EXPERT, split_axis=0, concat_axis=0, tiled=True)]
    convert_element_type x3 -> x6, other arithmetic: 2.98 us -> 15.7 us  [the longest x1 8.66 us: per_device(): h_one = (normed_one * gain_attn).astype(bf16)]
    unnamed x221 -> x234, local copies, waits for them, and re-layouts: 20.4 us -> 27.6 us
  transfers between devices with their start and end apart: 27 -> 22, of which waited for: 7 -> 2; matrix products, arithmetic and copies ran while one was open for 35% -> 44% of each run, Pallas kernels for 30% -> 37%
where the time goes in v2:
time: 988 us; the launch traced here: 979 us
  Pallas kernels  364 us (37%)
  matrix products  261 us (26%)
  local copies, waits for them, and re-layouts  133 us (13%)
  starting transfers between devices  78.7 us (8%)
  other arithmetic  76 us (8%)
  waiting for transfers between devices  51.4 us (5%)
  between operations  15.6 us (2%)
    pallas_call x2, Pallas kernels, ring_gather(): pl.pallas_call(functools.partial(gather_kernel, n, m), out_shape=[jax.Sha...  181 us
    pallas_call x2, Pallas kernels, ring_scatter(): pl.pallas_call(functools.partial(scatter_kernel, n), out_shape=[jax.Shape...  151 us
    dot_general x8, matrix products, right_product(): lax.dot_general(left, right, (((1,), (1,)), ((), ())), preferred_element_...  80.6 us
    dot_general x11, matrix products, left_product(): lax.dot_general(left, right, (((0,), (0,)), ((), ())), preferred_element_...  67.1 us
    dot_general x9, matrix products, product(): return jnp.dot(left, right, preferred_element_type=f32)  65.7 us
    all_to_all x3, starting transfers between devices, expert_swap(): lax.all_to_all(value, EXPERT, split_axis=0, concat_axis=0, tiled=True)  59.4 us
    ppermute x15, waiting for transfers between devices, dp_swap(): return lax.ppermute(value, DP, [(0, 1), (1, 0)])  50.7 us
    dot_general x10, matrix products, einsum(): return jnp.einsum(spec, left, right, preferred_element_type=f32)  39.7 us
  transfers between devices with their start and end apart: 22, of which 2 were waited for; matrix products, arithmetic and copies ran while one was open for 44% of the time, Pallas kernels for 37%

profile of v2, /device:TPU:0, one launch (start us, length us, event | category | flops | bytes accessed | tf_op | source)
XLA Modules:
  0.0 979.5 jit_solution(2958996491237273943)
XLA Ops:
  33.4 121.1 %shard_map.306 = (bf16[16,128,640]{2,1,0:T(8,128)(2,1)}, bf16[16,128,2048]{2,1,0:T(8,128)(2,1)}, bf16[16,64,192]{2,1,0:T(8,128)(2,1)}, bf16[16,32,256]{2,1,0:T(8,128)(2,1)}) custom-call(bf16[128,640]{1,0:T(8,128)(2,1)} %pad_maximum_fusion.27.refs_0_, bf16[128,2048]{1,0:T(8,128)(2,1)} %bitcast.204, bf16[16,64,192]{2,1,0:T(8,128)(2,1)} %bitcast.244, ...), custom_call_target="tpu_custom_call" | custom-call | bytes 175636480 | tf_op jit(solution)/shard_map/pallas_call | solution.py:295
  163.1 8.7 multiply_convert_fusion
  171.8 9.0 fusion.108
  186.0 4.6 all-to-all-start
  190.9 46.9 %collective-permute-done.2 = bf16[256,256]{1,0:T(8,128)(2,1)S(1)} collective-permute-done((bf16[256,256]{1,0:T(8,128)(2,1)S(1)}, bf16[256,256]{1,0:T(8,128)(2,1)S(1)}, u32[]{:S(2)}, u32[]{:S(2)}) %collective-permute-start.2) | collective-permute-done | bytes 131104 | tf_op jit(solution)/shard_map/ppermute | solution.py:88
  250.9 6.7 fusion.53
  269.2 7.6 fusion.116
  280.0 4.7 divide_convert_fusion
  289.4 15.7 %shard_map.307 = bf16[2,64,2048]{2,1,0:T(8,128)(2,1)} custom-call(bf16[2,1024,128]{2,1,0:T(8,128)(2,1)} %convolution_convert_fusion.9.x_ref), custom_call_target="tpu_custom_call" | custom-call | bytes 33554432 | tf_op jit(solution)/shard_map/pallas_call | solution.py:473
  307.3 4.9 broadcast_select_fusion.1
  312.3 4.9 broadcast_select_fusion.5
  317.2 4.9 broadcast_select_fusion.3
  322.2 6.4 multiply_reduce_fusion.9
  330.5 59.9 %shard_map.308 = bf16[16,128,2048]{2,1,0:T(8,128)(2,1)} custom-call(bf16[128,2048]{1,0:T(8,128)(2,1)} %multiply_convert_fusion.10.refs_0_), custom_call_target="tpu_custom_call" | custom-call | bytes 125829120 | tf_op jit(solution)/shard_map/pallas_call | solution.py:295
  390.4 5.9 fusion.60
  400.9 7.6 convolution_convert_fusion.4
  408.6 7.3 fusion.18
  415.9 9.7 multiply_convert_fusion.4
  425.6 7.1 fusion.3
  432.7 8.7 fusion.117
  441.4 11.4 %fusion.2 = bf16[2048,2048]{1,0:T(8,128)(2,1)} fusion(f32[2,1024,2048]{2,1,0:T(8,128)} %fusion.117, bf16[2048,176]{0,1:T(8,128)(2,1)S(1)} %multiply_convert_fusion.9, bf16[88,2048]{1,0:T(8,128)(2,1)S(1)} %copy-done.59, bf16[88,2048]{1,0:T(8,128)(2,1)S(1)} %copy-done.58), kind=kOutput, calls=%fused_computation.4 | convolution fusion | flops 1486225408 | bytes 26607616 | tf_op jit(solution)/shard_map/dot_general | solution.py:31
  452.9 8.6 multiply_convert_fusion.8
  470.0 6.4 fusion.59
  484.3 13.0 %multiply_convert_fusion.3 = (bf16[864,1408]{1,0:T(8,128)(2,1)}, bf16[864,1408]{1,0:T(8,128)(2,1)}) fusion(f32[864,1408]{1,0:T(8,128)} %fusion.18, f32[864,1408]{1,0:T(8,128)} %get-tuple-element.176, bf16[864,2048]{1,0:T(8,128)(2,1)S(1)} %fusion.5, bf16[704,2048]{1,0:T(8,128)(2,1)S(1)} %copy-done.45, bf16[704,2048]{1,0:T(8,128)(2,1)S(1)} %copy-done.43), kind=kOutput, calls=%fused_computation.28 | convolution fusion | flops 5010182144 | bytes 23904256 | tf_op jit(solution)/shard_map/dot_general | solution.py:39
  497.3 11.3 %fusion.15 = f32[864,2048]{1,0:T(8,128)} fusion(bf16[864,1408]{1,0:T(8,128)(2,1)} %get-tuple-element.136, bf16[1024,1408]{1,0:T(8,128)(2,1)} %get-tuple-element.142, bf16[1024,1408]{1,0:T(8,128)(2,1)} %get-tuple-element.141), kind=kOutput, calls=%fused_computation.52 | convolution fusion | flops 4994367488 | bytes 15278080 | tf_op jit(solution)/shard_map/dot_general | solution.py:39
  508.6 9.4 add_convert_fusion
  518.1 8.3 fusion.118
  526.4 10.8 %fusion.1 = bf16[2048,2048]{1,0:T(8,128)(2,1)} fusion(f32[2,1024,2048]{2,1,0:T(8,128)} %fusion.118, bf16[2048,16]{0,1:T(8,128)(2,1)S(1)} %multiply_convert_fusion.11, bf16[2048,176]{0,1:T(8,128)(2,1)} %get-tuple-element.146, bf16[2048,176]{0,1:T(8,128)(2,1)S(1)} %copy-done.66, bf16[2048,16]{0,1:T(8,128)(2,1)S(1)} %copy-done.78, ...), kind=kOutput, calls=%fused_computation.2 | convolution fusion | flops 3104440320 | bytes 28180480 | tf_op jit(solution)/shard_map/dot_general | solution.py:39
  537.2 67.4 %shard_map.309 = f32[128,2048]{1,0:T(8,128)} custom-call(bf16[16,128,2048]{2,1,0:T(8,128)(2,1)} %bitcast.200), custom_call_target="tpu_custom_call" | custom-call | bytes 125829120 | tf_op jit(solution)/shard_map/pallas_call | solution.py:435
  610.3 5.4 convolution_convert_fusion.7
  615.7 16.5 %shard_map.310 = bf16[2,1024,128]{2,1,0:T(8,128)(2,1)} custom-call(bf16[2,64,2048]{2,1,0:T(8,128)(2,1)} %bitcast.246), custom_call_target="tpu_custom_call" | custom-call | bytes 33554432 | tf_op jit(solution)/shard_map/pallas_call | solution.py:473
  635.0 5.2 fusion.121
  644.5 5.7 convolution_convert_fusion
  650.3 8.0 convolution_convert_fusion.2
  659.5 4.9 convolution_convert_fusion.1
  665.3 5.3 convolution_convert_fusion.5
  701.5 4.5 multiply_reduce_fusion.2
  709.4 7.1 fusion.122
  727.5 8.1 all-to-all-start.2
  735.6 16.6 %fusion.112 = (bf16[2048,2048]{1,0:T(8,128)(2,1)}, bf16[2048]{0:T(1024)(128)(2,1)S(1)}) fusion(f32[2048]{0:T(1024)S(1)} %copy-done.88, bf16[16,128,2048]{2,1,0:T(8,128)(2,1)} %get-tuple-element.30, bf16[2048,768]{0,1:T(8,128)(2,1)} %copy-done.84, bf16[2048,576]{1,0:T(8,128)(2,1)} %bitcast.221, bf16[1024,192]{1,0:T(8,128)(2,1)} %copy-done.71, ...), kind=kOutput, calls=%fused_computation.262 | convolution fusion | flops 6472857600 | bytes 23080960 | tf_op jit(solution)/shard_map/dot_general | solution.py:39
  752.2 4.1 slice.341
  756.3 4.4 copy.261
  764.6 6.8 concatenate.118
  774.9 83.7 %shard_map.311 = (f32[128,640]{1,0:T(8,128)}, f32[128,2048]{1,0:T(8,128)}) custom-call(bf16[16,128,640]{2,1,0:T(8,128)(2,1)} %bitcast.210, bf16[16,128,2048]{2,1,0:T(8,128)(2,1)} %bitcast.217), custom_call_target="tpu_custom_call" | custom-call | bytes 165150720 | tf_op jit(solution)/shard_map/pallas_call | solution.py:435
  865.0 46.7 %all-to-all-start.1 = ((bf16[16,64,256]{2,1,0:T(8,128)(2,1)}), bf16[16,64,256]{2,1,0:T(8,128)(2,1)}, u32[]{:S(2)}, u32[]{:S(2)}) async-start(bf16[16,64,256]{2,1,0:T(8,128)(2,1)} %bitcast.247), calls=%async_computation.2 | async-start | bytes 1048576 | tf_op jit(solution)/shard_map/all_to_all | solution.py:125
  944.3 9.7 add_bitcast_fusion.2
  954.0 6.9 add_bitcast_fusion.1
  960.9 7.2 add_bitcast_fusion
  (437 shorter events, 208.1 us)
Async XLA Ops:
  7.2 17.3 %copy-start.94 = (s32[2,64,6]{1,0,2:T(2,128)S(1)}, s32[2,64,6]{1,0,2:T(2,128)}, u32[]{:S(2)}) copy-start(s32[2,64,6]{1,0,2:T(2,128)} %param.21) | copy-start | bytes 9220
  7.2 17.3 %copy-start.102 = (s32[2,64]{1,0:T(2,128)S(1)}, s32[2,64]{1,0:T(2,128)}, u32[]{:S(2)}) copy-start(s32[2,64]{1,0:T(2,128)} %param.22) | copy-start | bytes 1540
  7.2 17.6 %copy-start.83 = (bf16[16,4096]{1,0:T(8,128)(2,1)S(1)}, bf16[16,4096]{1,0:T(8,128)(2,1)}, u32[]{:S(2)}) copy-start(bf16[16,4096]{1,0:T(8,128)(2,1)} %param.26) | copy-start | bytes 393220
  7.2 17.7 %copy-start.74 = (bf16[64,2816]{1,0:T(8,128)(2,1)S(1)}, bf16[64,2816]{1,0:T(8,128)(2,1)}, u32[]{:S(2)}) copy-start(bf16[64,2816]{1,0:T(8,128)(2,1)} %param.32) | copy-start | bytes 1081348
  7.2 315.0 %all-gather.3.cloned.1.call-start = ((), (), s32[]{:S(2)}) async-start(), calls=%async_computation.5 | async-start | bytes 8650752 | tf_op jit(solution)/shard_map/all_gather | solution.py:129
  8.0 444.9 %all-gather.5.cloned.1.call-start = ((), (), s32[]{:S(2)}) async-start(), calls=%async_computation.6 | async-start | bytes 8912896 | tf_op jit(solution)/shard_map/all_gather | solution.py:129
  12.1 20.6 %collective-permute-start = (bf16[64,640]{1,0:T(8,128)(2,1)S(1)}, bf16[64,640]{1,0:T(8,128)(2,1)S(1)}, u32[]{:S(2)}, u32[]{:S(2)}) collective-permute-start(bf16[64,640]{1,0:T(8,128)(2,1)S(1)} %concatenate.90), channel_id=1, source_target_pairs={{0,16},{16,0},{1,17},{17,1},{2,18},{18,2},{3,19},{19,3},{4,20},{20... | collective-permute-start | bytes 245768 | tf_op jit(solution)/shard_map/ppermute | solution.py:88
  15.1 297.2 %collective-permute-start.5 = (bf16[1024,1408]{1,0:T(8,128)(2,1)}, bf16[1024,1408]{1,0:T(8,128)(2,1)}, u32[]{:S(2)}, u32[]{:S(2)}) collective-permute-start(bf16[1024,1408]{1,0:T(8,128)(2,1)} %bitcast.237), channel_id=1, source_target_pairs={{0,16},{16,0},{1,17},{17,1},{2,18},{18,2},{3,19},{19,3},{4,20},{20... | collective-permute-start | bytes 8650760 | tf_op jit(solution)/shard_map/ppermute | solution.py:88
  15.2 302.0 %collective-permute-start.6 = (bf16[1024,1408]{1,0:T(8,128)(2,1)}, bf16[1024,1408]{1,0:T(8,128)(2,1)}, u32[]{:S(2)}, u32[]{:S(2)}) collective-permute-start(bf16[1024,1408]{1,0:T(8,128)(2,1)} %bitcast.238), channel_id=1, source_target_pairs={{0,16},{16,0},{1,17},{17,1},{2,18},{18,2},{3,19},{19,3},{4,20},{20... | collective-permute-start | bytes 8650760 | tf_op jit(solution)/shard_map/ppermute | solution.py:88
  17.1 290.2 %collective-permute-start.7 = (bf16[704,2048]{1,0:T(8,128)(2,1)}, bf16[704,2048]{1,0:T(8,128)(2,1)}, u32[]{:S(2)}, u32[]{:S(2)}) collective-permute-start(bf16[704,2048]{1,0:T(8,128)(2,1)} %bitcast.236), channel_id=1, source_target_pairs={{0,16},{16,0},{1,17},{17,1},{2,18},{18,2},{3,19},{19,3},{4,20},{20... | collective-permute-start | bytes 8650760 | tf_op jit(solution)/shard_map/ppermute | solution.py:88
  17.2 227.9 %collective-permute-start.4 = (bf16[88,2048]{1,0:T(8,128)(2,1)}, bf16[88,2048]{1,0:T(8,128)(2,1)}, u32[]{:S(2)}, u32[]{:S(2)}) collective-permute-start(bf16[88,2048]{1,0:T(8,128)(2,1)} %param.33), channel_id=1, source_target_pairs={{0,16},{16,0},{1,17},{17,1},{2,18},{18,2},{3,19},{19,3},{4,20},{20... | collective-permute-start | bytes 1081352 | tf_op jit(solution)/shard_map/ppermute | solution.py:88
  21.7 235.9 %copy-start.15 = (f32[2048,32]{0,1:T(8,128)}, f32[2048,32]{0,1:T(8,128)S(1)}, u32[]{:S(2)}) copy-start(f32[2048,32]{0,1:T(8,128)S(1)} %get-tuple-element.34) | copy-start | bytes 786436
  21.7 235.9 %copy-start.17 = (f32[2048,32]{0,1:T(8,128)}, f32[2048,32]{0,1:T(8,128)S(1)}, u32[]{:S(2)}) copy-start(f32[2048,32]{0,1:T(8,128)S(1)} %get-tuple-element.33) | copy-start | bytes 786436
  158.4 13.4 %copy-start.20 = (bf16[16,2,64,640]{3,2,0,1:T(8,128)(2,1)}, bf16[16,2,64,640]{3,2,0,1:T(8,128)(2,1)S(1)}, u32[]{:S(2)}) copy-start(bf16[16,2,64,640]{3,2,0,1:T(8,128)(2,1)S(1)} %copy.228) | copy-start | bytes 7864324
  160.3 168.3 %copy-start.79 = (f32[2048]{0:T(1024)}, f32[2048]{0:T(1024)S(1)}, u32[]{:S(2)}) copy-start(f32[2048]{0:T(1024)S(1)} %get-tuple-element.128) | copy-start | bytes 24580
  180.8 57.0 %collective-permute-start.2 = (bf16[256,256]{1,0:T(8,128)(2,1)S(1)}, bf16[256,256]{1,0:T(8,128)(2,1)S(1)}, u32[]{:S(2)}, u32[]{:S(2)}) collective-permute-start(bf16[256,256]{1,0:T(8,128)(2,1)S(1)} %bitcast.256), channel_id=1, source_target_pairs={{0,16},{16,0},{1,17},{17,1},{2,18},{18,2},{3,19},{19,3},{4,20},{20... | collective-permute-start | bytes 393224 | tf_op jit(solution)/shard_map/ppermute | solution.py:88
  181.9 57.6 %copy-start.89 = (f32[512]{0:T(512)}, f32[512]{0:T(512)S(1)}, u32[]{:S(2)}) copy-start(f32[512]{0:T(512)S(1)} %mul.391) | copy-start | bytes 6148
  186.0 90.9 %all-to-all-start = ((bf16[16,64,352]{2,1,0:T(8,128)(2,1)}), bf16[16,64,352]{2,1,0:T(8,128)(2,1)}, u32[]{:S(2)}, u32[]{:S(2)}) async-start(bf16[16,64,352]{2,1,0:T(8,128)(2,1)} %pad_maximum_fusion.16), calls=%async_computation | async-start | bytes 1572864 | tf_op jit(solution)/shard_map/all_to_all | solution.py:125
  190.6 777.5 %reduce-scatter.3.cloned.1.call-start = ((), (), s32[]{:S(2)}) async-start(), calls=%async_computation.7 | async-start | bytes 8912896 | tf_op jit(solution)/shard_map/reduce_scatter | solution.py:133
  190.8 52.5 %copy-start.85 = (f32[2048]{0:T(1024)}, f32[2048]{0:T(1024)S(1)}, u32[]{:S(2)}) copy-start(f32[2048]{0:T(1024)S(1)} %add_rsqrt_fusion) | copy-start | bytes 24580
  237.8 13.0 %collective-permute-start.1 = (bf16[1024,192]{1,0:T(8,128)(2,1)}, bf16[1024,192]{1,0:T(8,128)(2,1)S(1)}, u32[]{:S(2)}, u32[]{:S(2)}) collective-permute-start(bf16[1024,192]{1,0:T(8,128)(2,1)} %bitcast.255), channel_id=1, source_target_pairs={{0,16},{16,0},{1,17},{17,1},{2,18},{18,2},{3,19},{19,3},{4,20},{20... | collective-permute-start | bytes 1179656 | tf_op jit(solution)/shard_map/ppermute | solution.py:88
  278.2 26.9 %collective-permute-start.3 = (bf16[1024,352]{0,1:T(8,128)(2,1)S(1)}, bf16[1024,352]{0,1:T(8,128)(2,1)}, u32[]{:S(2)}, u32[]{:S(2)}) collective-permute-start(bf16[1024,352]{0,1:T(8,128)(2,1)S(1)} %copy.245), channel_id=1, source_target_pairs={{0,16},{16,0},{1,17},{17,1},{2,18},{18,2},{3,19},{19,3},{4,20},{20... | collective-permute-start | bytes 2162696 | tf_op jit(solution)/shard_map/ppermute | solution.py:88
  307.3 83.1 %copy-start.48 = (bf16[1024,352]{0,1:T(8,128)(2,1)}, bf16[1024,352]{0,1:T(8,128)(2,1)S(1)}, u32[]{:S(2)}) copy-start(bf16[1024,352]{0,1:T(8,128)(2,1)S(1)} %get-tuple-element.151) | copy-start | bytes 2162692
  330.5 59.9 %copy-start.50 = (bf16[1024,352]{0,1:T(8,128)(2,1)S(1)}, bf16[1024,352]{0,1:T(8,128)(2,1)}, u32[]{:S(2)}) copy-start(bf16[1024,352]{0,1:T(8,128)(2,1)} %get-tuple-element.152) | copy-start | bytes 2162692
  330.5 59.9 %copy-start.77 = (bf16[2048,16]{0,1:T(8,128)(2,1)S(1)}, bf16[2048,16]{0,1:T(8,128)(2,1)}, u32[]{:S(2)}) copy-start(bf16[2048,16]{0,1:T(8,128)(2,1)} %copy.247) | copy-start | bytes 196612
  468.9 502.1 %reduce-scatter.5.cloned.1.call-start = ((), (), s32[]{:S(2)}) async-start(), calls=%async_computation.8 | async-start | bytes 8650752 | tf_op jit(solution)/shard_map/reduce_scatter | solution.py:133
  480.5 16.8 %copy-start.8 = (bf16[864,2048]{1,0:T(8,128)(2,1)}, bf16[864,2048]{1,0:T(8,128)(2,1)S(1)}, u32[]{:S(2)}) copy-start(bf16[864,2048]{1,0:T(8,128)(2,1)S(1)} %fusion.5) | copy-start | bytes 10616836
  497.3 11.3 %copy-start.39 = (bf16[1024,1408]{1,0:T(8,128)(2,1)S(1)}, bf16[1024,1408]{1,0:T(8,128)(2,1)}, u32[]{:S(2)}) copy-start(bf16[1024,1408]{1,0:T(8,128)(2,1)} %get-tuple-element.139) | copy-start | bytes 8650756
  497.3 11.3 %copy-start.41 = (bf16[1024,1408]{1,0:T(8,128)(2,1)S(1)}, bf16[1024,1408]{1,0:T(8,128)(2,1)}, u32[]{:S(2)}) copy-start(bf16[1024,1408]{1,0:T(8,128)(2,1)} %get-tuple-element.140) | copy-start | bytes 8650756
  497.3 11.3 %copy-start.108 = (bf16[864,1408]{1,0:T(8,128)(2,1)S(1)}, bf16[864,1408]{1,0:T(8,128)(2,1)}, u32[]{:S(2)}) copy-start(bf16[864,1408]{1,0:T(8,128)(2,1)} %get-tuple-element.135) | copy-start | bytes 7299076
  537.2 71.1 %copy-start.4 = (f32[128,2048]{1,0:T(8,128)S(1)}, f32[128,2048]{1,0:T(8,128)}, u32[]{:S(2)}) copy-start(f32[128,2048]{1,0:T(8,128)} %copy-done.3) | copy-start | bytes 3145732
  537.2 71.1 %copy-start.80 = (f32[2048]{0:T(1024)S(1)}, f32[2048]{0:T(1024)}, u32[]{:S(2)}) copy-start(f32[2048]{0:T(1024)} %copy-done.79) | copy-start | bytes 24580
  537.2 71.2 %copy-start.92 = (f32[128]{0:T(128)S(1)}, f32[128]{0:T(128)}, u32[]{:S(2)}) copy-start(f32[128]{0:T(128)} %copy-done.91) | copy-start | bytes 1540
  607.1 35.2 %collective-permute-start.8 = (bf16[1024,352]{0,1:T(8,128)(2,1)}, bf16[1024,352]{0,1:T(8,128)(2,1)}, u32[]{:S(2)}, u32[]{:S(2)}) collective-permute-start(bf16[1024,352]{0,1:T(8,128)(2,1)} %dynamic-slice_convert_fusion), channel_id=1, source_target_pairs={{0,16},{16,0},{1,17},{17,1},{2,18},{18,2},{3,19},{19,3},{4,20},{20... | collective-permute-start | bytes 2162696 | tf_op jit(solution)/shard_map/ppermute | solution.py:88
  641.4 30.5 %collective-permute-start.11 = (bf16[88,2048]{1,0:T(8,128)(2,1)S(1)}, bf16[88,2048]{1,0:T(8,128)(2,1)S(1)}, u32[]{:S(2)}, u32[]{:S(2)}) collective-permute-start(bf16[88,2048]{1,0:T(8,128)(2,1)S(1)} %dynamic-slice_convert_fusion.1), channel_id=1, source_target_pairs={{0,16},{16,0},{1,17},{17,1},{2,18},{18,2},{3,19},{19,3},{4,20},{20... | collective-permute-start | bytes 1081352 | tf_op jit(solution)/shard_map/ppermute | solution.py:88
  658.3 286.0 %collective-permute-start.12 = (bf16[1024,1408]{1,0:T(8,128)(2,1)}, bf16[1024,1408]{1,0:T(8,128)(2,1)}, u32[]{:S(2)}, u32[]{:S(2)}) collective-permute-start(bf16[1024,1408]{1,0:T(8,128)(2,1)} %convolution_convert_fusion.2), channel_id=1, source_target_pairs={{0,16},{16,0},{1,17},{17,1},{2,18},{18,2},{3,19},{19,3},{4,20},{20... | collective-permute-start | bytes 8650760 | tf_op jit(solution)/shard_map/ppermute | solution.py:88
  664.4 289.6 %collective-permute-start.13 = (bf16[1024,1408]{1,0:T(8,128)(2,1)}, bf16[1024,1408]{1,0:T(8,128)(2,1)}, u32[]{:S(2)}, u32[]{:S(2)}) collective-permute-start(bf16[1024,1408]{1,0:T(8,128)(2,1)} %convolution_convert_fusion.1), channel_id=1, source_target_pairs={{0,16},{16,0},{1,17},{17,1},{2,18},{18,2},{3,19},{19,3},{4,20},{20... | collective-permute-start | bytes 8650760 | tf_op jit(solution)/shard_map/ppermute | solution.py:88
  670.6 290.3 %collective-permute-start.14 = (bf16[704,2048]{1,0:T(8,128)(2,1)}, bf16[704,2048]{1,0:T(8,128)(2,1)}, u32[]{:S(2)}, u32[]{:S(2)}) collective-permute-start(bf16[704,2048]{1,0:T(8,128)(2,1)} %convolution_convert_fusion.5), channel_id=1, source_target_pairs={{0,16},{16,0},{1,17},{17,1},{2,18},{18,2},{3,19},{19,3},{4,20},{20... | collective-permute-start | bytes 8650760 | tf_op jit(solution)/shard_map/ppermute | solution.py:88
  709.4 10.2 %copy-start.31 = (bf16[16,2,64,256]{3,2,1,0:T(8,128)(2,1)S(1)}, bf16[16,2,64,256]{3,2,1,0:T(8,128)(2,1)}, u32[]{:S(2)}) copy-start(bf16[16,2,64,256]{3,2,1,0:T(8,128)(2,1)} %copy.259) | copy-start | bytes 3145732
  721.6 13.9 %copy-start.88 = (f32[2048]{0:T(1024)S(1)}, f32[2048]{0:T(1024)}, u32[]{:S(2)}) copy-start(f32[2048]{0:T(1024)} %copy-done.87) | copy-start | bytes 24580
  723.2 29.0 %copy-start.23 = (f32[2048,64]{0,1:T(8,128)}, f32[2048,64]{0,1:T(8,128)S(1)}, u32[]{:S(2)}) copy-start(f32[2048,64]{0,1:T(8,128)S(1)} %copy.267) | copy-start | bytes 1572868
  725.5 135.2 %collective-permute-start.9 = (bf16[1024,256]{0,1:T(8,128)(2,1)}, bf16[1024,256]{0,1:T(8,128)(2,1)}, u32[]{:S(2)}, u32[]{:S(2)}) collective-permute-start(bf16[1024,256]{0,1:T(8,128)(2,1)} %fusion.49), channel_id=1, source_target_pairs={{0,16},{16,0},{1,17},{17,1},{2,18},{18,2},{3,19},{19,3},{4,20},{20... | collective-permute-start | bytes 1572872 | tf_op jit(solution)/shard_map/ppermute | solution.py:88
  727.5 137.5 %all-to-all-start.2 = ((bf16[16,64,352]{2,1,0:T(8,128)(2,1)}), bf16[16,64,352]{2,1,0:T(8,128)(2,1)S(1)}, u32[]{:S(2)}, u32[]{:S(2)}) async-start(bf16[16,64,352]{2,1,0:T(8,128)(2,1)} %bitcast.235), calls=%async_computation.4 | async-start | bytes 1572864 | tf_op jit(solution)/shard_map/all_to_all | solution.py:125
  858.7 53.1 %copy-start.13 = (bf16[2,64,2048]{2,1,0:T(8,128)(2,1)S(1)}, bf16[2,64,2048]{2,1,0:T(8,128)(2,1)}, u32[]{:S(2)}) copy-start(bf16[2,64,2048]{2,1,0:T(8,128)(2,1)} %param.19) | copy-start | bytes 1572868
  858.7 53.1 %copy-start.82 = (f32[2048]{0:T(1024)S(1)}, f32[2048]{0:T(1024)}, u32[]{:S(2)}) copy-start(f32[2048]{0:T(1024)} %copy-done.81) | copy-start | bytes 24580
  858.7 53.1 %copy-start.97 = (f32[128]{0:T(128)S(1)}, f32[128]{0:T(128)}, u32[]{:S(2)}) copy-start(f32[128]{0:T(128)} %rsqrt.43) | copy-start | bytes 1540
  859.7 53.6 %collective-permute-start.10 = (bf16[64,640]{1,0:T(8,128)(2,1)S(1)}, bf16[64,640]{1,0:T(8,128)(2,1)}, u32[]{:S(2)}, u32[]{:S(2)}) collective-permute-start(bf16[64,640]{1,0:T(8,128)(2,1)S(1)} %dynamic-slice_convert_fusion.2), channel_id=1, source_target_pairs={{0,16},{16,0},{1,17},{17,1},{2,18},{18,2},{3,19},{19,3},{4,20},{20... | collective-permute-start | bytes 245768 | tf_op jit(solution)/shard_map/ppermute | solution.py:88
  865.0 71.9 %all-to-all-start.1 = ((bf16[16,64,256]{2,1,0:T(8,128)(2,1)}), bf16[16,64,256]{2,1,0:T(8,128)(2,1)}, u32[]{:S(2)}, u32[]{:S(2)}) async-start(bf16[16,64,256]{2,1,0:T(8,128)(2,1)} %bitcast.247), calls=%async_computation.2 | async-start | bytes 1048576 | tf_op jit(solution)/shard_map/all_to_all | solution.py:125
  (87 other events, 506.9 us)
Sparse Core Ops, SparseCore 0:
  10.9 112.1 all-gather.2
  125.3 89.3 all-gather.4
  469.0 110.2 reduce-scatter.2
  650.4 159.7 reduce-scatter.4

commit v3 on v2

--- a/solution.py
+++ b/solution.py
@@ -319,6 +319,10 @@
     me, line, pair, core = grid_place()
     partner, mate = greet_neighbours(me, line, pair, core)
 
+    def block(i, dest):
+        ref = parts[i][0]
+        return ref.at[dest] if len(ref.shape) == 3 else ref.at[:, dest]
+
     def remote(source, target, send, recv, to):
         return pltpu.make_async_remote_copy(
             src_ref=source, dst_ref=target, send_sem=send, recv_sem=recv,
@@ -327,7 +331,7 @@
 
     def core_copy(i, index):
         return remote(
-            parts[i][0].at[2 * index + 1 - core], parts[i][2].at[index],
+            block(i, 2 * index + 1 - core), parts[i][2].at[index],
             core_send.at[i, index], core_recv.at[i, index], partner,
         )
 
@@ -350,7 +354,11 @@
         )
 
     def add(target, left, right):
-        tile = 16
+        if len(left.shape) == 3:
+            for i in range(left.shape[0]):
+                add(target.at[i], left.at[i], right.at[i])
+            return
+        tile = min(16, left.shape[0])
 
         @pl.loop(0, left.shape[0] // tile)
         def _(i):
@@ -376,7 +384,7 @@
 
     def chip_sum(i, index):
         core_copy(i, index).wait_recv()
-        add(parts[i][6].at[index], parts[i][0].at[2 * index + core], parts[i][2].at[index])
+        add(parts[i][6].at[index], block(i, 2 * index + core), parts[i][2].at[index])
 
     def to_mate(i, dest, step):
         chip_sum(i, 2 * dest + 1 - pair)
@@ -428,9 +436,9 @@
 
 def ring_scatter(values, collective):
     n = len(values)
-    shapes = [(v.shape[0] // 16, v.shape[1]) for v in values]
+    shapes = [v.shape[1:] if len(v.shape) == 3 else v.shape[:1] + v.shape[2:] for v in values]
     buffers = [pltpu.VMEM((k,) + s, bf16) for s in shapes for k in (8, 4, 4, 4, 8)]
-    sent = 30 * sum(a * b for a, b in shapes)
+    sent = 30 * sum(math.prod(s) for s in shapes)
     vmem = pl.BlockSpec(memory_space=pltpu.VMEM)
     return pl.pallas_call(
         functools.partial(scatter_kernel, n),
@@ -441,7 +449,7 @@
         + [pltpu.SemaphoreType.DMA((n, k)) for k in (8, 8, 4, 4, 4, 4, 4, 4)],
         compiler_params=pltpu.CompilerParams(collective_id=collective, has_side_effects=True),
         cost_estimate=pl.CostEstimate(flops=0, bytes_accessed=16 * sent, transcendentals=0),
-    )(*[v.reshape((16,) + s) for v, s in zip(values, shapes)])
+    )(*values)
 
 
 def swap_kernel(source, target, x_ref, out_ref, own_sem, send_sem, recv_sem):
@@ -548,6 +556,9 @@
             seqs, length, -1
         )
 
+    def by_owner(value):
+        return value.astype(bf16).reshape(groups, own, -1)
+
     def by_block(value):
         return value.reshape(seqs, groups, span, -1).transpose(1, 0, 2, 3).reshape(tokens, -1)
 
@@ -607,9 +618,7 @@
             .reshape(groups, rows, hidden_own)
         )
 
-    gate_up_parts, query_swap = lax.optimization_barrier(
-        (jnp.concatenate([columns_of(shared_gate), columns_of(shared_up)], axis=2), query_swap)
-    )
+    gate_up_parts = jnp.concatenate([columns_of(shared_gate), columns_of(shared_up)], axis=2)
     gate_up_swap = expert_swap(gate_up_parts)
     gate_up = dp_gather(gate_up_swap.reshape(groups * rows, 2 * hidden_own))
     gate_up_router = jnp.concatenate([gate_up, router_all], axis=1)
@@ -618,7 +627,6 @@
     up_w = dp_gather(expert_up[0])
     down_w = dp_gather(expert_down[0])
     out_t = gather_rows(output_weight.T, BOTH)
-    cot_all = gather_rows(cot_own, EXPERT)
 
     at_block = jnp.arange(groups, dtype=jnp.int32)[:, None, None] * span
     positions = jnp.broadcast_to(
@@ -654,7 +662,10 @@
     normed_two, factor_two = norm_parts(x_second)
     (h_two,) = ring_gather([(normed_two * gain_moe).astype(bf16)], [], 2)
 
-    chunk = tokens // 2
+    cot_all = gather_rows(cot_own, EXPERT)
+
+    chunks = 4
+    chunk = tokens // chunks
     blocks = chunk // span
     slots = blocks * capacity
     slot_at = jnp.arange(slots, dtype=jnp.int32)
@@ -663,18 +674,18 @@
         (slot_at[:, None] // capacity == token_at[None, :] // span)[None]
         & (
             (slot_at % capacity).astype(f32)[None, :, None]
-            == code.reshape(2, chunk)[:, None, :]
+            == code.reshape(chunks, chunk)[:, None, :]
         )
     ).astype(bf16)
     select = lax.optimization_barrier(select)
 
     def to_slots(values):
-        return einsum("cst,ctd->csd", select, values.reshape(2, chunk, -1)).astype(bf16).reshape(
-            2 * slots, -1
+        return einsum("cst,ctd->csd", select, values.reshape(chunks, chunk, -1)).astype(bf16).reshape(
+            chunks * slots, -1
         )
 
     def to_tokens(values):
-        return einsum("cst,csd->ctd", select, values.reshape(2, slots, -1)).reshape(tokens, -1)
+        return einsum("cst,csd->ctd", select, values.reshape(chunks, slots, -1)).reshape(tokens, -1)
 
     pre = product(h_two, gate_up_router)
     shared_a = pre[:, :hidden_own]
@@ -684,15 +695,15 @@
     mine = (jnp.arange(experts, dtype=jnp.int32) == place).astype(f32)
     own_prob = jnp.sum(gate_probs * mine, axis=-1)
     slot_prob = jnp.sum(
-        select.astype(f32) * own_prob.reshape(2, 1, chunk), axis=-1
-    ).reshape(2 * slots, 1)
+        select.astype(f32) * own_prob.reshape(chunks, 1, chunk), axis=-1
+    ).reshape(chunks * slots, 1)
     expert_in = to_slots(h_two)
     gate_pre = product(expert_in, gate_w)
     up_pre = product(expert_in, up_w)
     expert_hidden = (jax.nn.silu(gate_pre) * up_pre).astype(bf16)
     expert_out = product(expert_hidden, down_w).astype(bf16).astype(f32)
     partial = product(shared_hidden, sdown) + to_tokens((slot_prob * expert_out).astype(bf16))
-    partial, cot_all = lax.optimization_barrier((partial.astype(bf16), cot_all))
+    partial = partial.astype(bf16)
     result = x_second + scatter_rows(partial, EXPERT).astype(f32)
     result = result.astype(bf16).reshape(seqs, span, width)
 
@@ -703,21 +714,20 @@
     shared_b_grad = (hidden_grad * jax.nn.silu(shared_a)).astype(bf16)
     grad_wide = grad_slots.astype(f32)
     slot_grad = (slot_prob * grad_wide).astype(bf16)
-    match = jnp.sum(grad_wide * expert_out, axis=-1).reshape(2, slots, 1)
+    match = jnp.sum(grad_wide * expert_out, axis=-1).reshape(chunks, slots, 1)
     prob_grad = jnp.sum(select.astype(f32) * match, axis=1).reshape(tokens, 1)
     logit_grad = (gate_probs * prob_grad * (mine - own_prob[:, None])).astype(bf16)
     pre_grad = jnp.concatenate([shared_a_grad, shared_b_grad, logit_grad], axis=1)
     expert_hidden_grad = right_product(slot_grad, down_w)
     expert_a_grad = (expert_hidden_grad * up_pre * silu_slope(gate_pre)).astype(bf16)
     expert_b_grad = (expert_hidden_grad * jax.nn.silu(gate_pre)).astype(bf16)
-    in_grad = (right_product(expert_a_grad, gate_w) + right_product(expert_b_grad, up_w)).astype(
-        bf16
-    )
+    in_grad = right_product(expert_a_grad, gate_w) + right_product(expert_b_grad, up_w)
+    in_grad = in_grad.astype(bf16)
     h_two_partial = right_product(pre_grad, gate_up_router) + to_tokens(in_grad)
     routed_down_grad = dp_scatter_product(expert_hidden, slot_grad)
     routed_gate_grad = dp_scatter_product(expert_in, expert_a_grad)
     routed_up_grad = dp_scatter_product(expert_in, expert_b_grad)
-    (h_two_grad,) = ring_scatter([h_two_partial.astype(bf16)], 4)
+    (h_two_grad,) = ring_scatter([by_owner(h_two_partial)], 4)
     pre_weight_grad = left_product(h_two, pre_grad)
     sdown_owned = dp_scatter(sdown_grad)
     gate_up_owned = dp_scatter(pre_weight_grad[:, : 2 * hidden_own]).astype(bf16)
@@ -728,10 +738,7 @@
     attn_low = x_second_grad.astype(bf16)
     heads_grad = product(attn_low, out_t).astype(bf16)
     grad_s = tokens_to_heads(heads_grad.reshape(seqs, span, HEADS * VD), 5)
-    attn_low, gate_up_owned, grad_s = lax.optimization_barrier((attn_low, gate_up_owned, grad_s))
-    out_owned = (
-        scatter_rows(left_product(attn_low, heads_own).astype(bf16), BOTH).astype(f32).T
-    )
+    low_all = gather_rows(attn_low, EXPERT)
     gate_up_owned = expert_swap(
         gate_up_owned.reshape(groups, rows, 2 * hidden_own)
     ).astype(f32)
@@ -760,51 +767,65 @@
     glat_grad = jnp.sum(latent_grad * normed_lat, axis=0)
     joint_grad = jnp.concatenate(
         [
-            query_grad[:, :HD],
-            unrotate(query_grad[:, HD:], tables),
             norm_back(latent_grad * gain_lat, normed_lat, factor_lat),
             unrotate(rope_grad, tables),
+            unrotate(query_grad[:, HD:], tables),
+            query_grad[:, :HD],
         ],
         axis=-1,
     ).astype(bf16)
-    joint_weight = jnp.concatenate([wq, ldown_all], axis=1)
+    joint_weight = jnp.concatenate([ldown_all, wq[:, HD:], wq[:, :HD]], axis=1)
     h_one_partial = right_product(joint_grad, joint_weight)
-    gattn_grad = jnp.sum(h_one_partial * normed_one, axis=0)
     joint_weight_grad = left_product(h_one, joint_grad)
-    back_grad = jnp.concatenate([joint_weight_grad[:, :QD], lup_grad.reshape(width, -1)], axis=1)
+    gattn_grad = jnp.sum(joint_weight_grad * joint_weight.astype(f32), axis=1) / gain_attn
+    out_grad = left_product(low_all, by_block(heads_s))
+    down_at = RANK + RD
+    back_grad = jnp.concatenate(
+        [
+            joint_weight_grad[:, down_at + RD :],
+            out_grad,
+            joint_weight_grad[:, down_at : down_at + RD],
+            lup_grad.reshape(width, -1),
+        ],
+        axis=1,
+    )
     back_grad = dp_scatter(back_grad).astype(bf16)
     back_owned = expert_swap(back_grad.reshape(groups, rows, -1)).astype(f32)
-    q_owned = back_owned[:, :, :QD].transpose(1, 0, 2).reshape(rows, HEADS * QD)
-    lup_owned = back_owned[:, :, QD:].reshape(groups, lup_rows, HD + VD)
+    q_owned = jnp.concatenate(
+        [back_owned[:, :, :HD], back_owned[:, :, HD + VD : HD + VD + RD]], axis=2
+    )
+    q_owned = q_owned.transpose(1, 0, 2).reshape(rows, HEADS * QD)
+    out_owned = back_owned[:, :, HD : HD + VD].transpose(0, 2, 1).reshape(HEADS * VD, rows)
+    lup_owned = back_owned[:, :, HD + VD + RD :].reshape(groups, lup_rows, HD + VD)
     lup_owned = lup_owned.transpose(1, 0, 2).reshape(lup_rows, HEADS * (HD + VD))
     glat_column = jnp.pad(
         glat_grad.reshape(-1, latent_gain.shape[0]), ((0, 0), (0, pad))
-    ).reshape(-1, 1)
-    small_grad = jnp.concatenate(
+    ).reshape(-1)
+    lane = jnp.arange(128, dtype=jnp.int32)
+    small_grad = jnp.pad(router_grad, ((0, 0), (0, 128 - experts)))
+    for at_lane, column in enumerate((gattn_grad, gmoe_grad, glat_column)):
+        small_grad = jnp.where(lane == experts + at_lane, column[:, None], small_grad)
+
+    def by_row_owner(value):
+        return value.astype(bf16).reshape(replicas, groups, rows, -1)
+
+    ldown_owned, small_owned, h_one_grad = ring_scatter(
         [
-            joint_weight_grad[:, QD:],
-            router_grad,
-            gattn_grad[:, None],
-            gmoe_grad[:, None],
-            glat_column,
-            jnp.zeros((width, 45), f32),
+            by_row_owner(joint_weight_grad[:, :down_at]),
+            by_row_owner(small_grad),
+            by_owner(h_one_partial),
         ],
-        axis=1,
-    )
-    small_grad = (
-        small_grad.astype(bf16)
-        .reshape(replicas, groups, rows, -1)
-        .transpose(1, 0, 2, 3)
-        .reshape(width, -1)
-    )
-    small_owned, h_one_grad = ring_scatter([small_grad, h_one_partial.astype(bf16)], 6)
+        6,
+    )
     normed_own, factor_own = norm_parts(x_low.astype(f32))
     input_grad = x_second_grad + norm_back(h_one_grad * gain_attn, normed_own, factor_own)
     input_grad = input_grad.astype(bf16).reshape(seqs, span, width)
-    small_owned = dp_scatter(small_owned)
-    ldown_owned = small_owned[:, : RANK + RD]
-    router_owned = small_owned[:, RANK + RD : RANK + RD + experts]
-    gain_owned = small_owned[:, RANK + RD + experts :]
+    small_owned = dp_scatter(
+        jnp.concatenate([ldown_owned, small_owned], axis=2).reshape(replicas * rows, -1)
+    )
+    ldown_owned = small_owned[:, :down_at]
+    router_owned = small_owned[:, down_at : down_at + experts]
+    gain_owned = small_owned[:, down_at + experts :]
     return (
         result,
         input_grad,

time: 988 us -> 975 us (0.987)
  starting transfers between devices: 78.7 us -> 40.3 us
  local copies, waits for them, and re-layouts: 133 us -> 99.6 us
  Pallas kernels: 364 us -> 389 us
  waiting for transfers between devices: 51.4 us -> 76.1 us
  other arithmetic: 76 us -> 87 us
    all_to_all x3, starting transfers between devices: 59.4 us -> 19.3 us  [expert_swap(): lax.all_to_all(value, EXPERT, split_axis=0, concat_axis=0, tiled=True)]
    pallas_call x2, Pallas kernels: 181 us -> 199 us  [ring_gather(): pl.pallas_call(functools.partial(gather_kernel, n, m), out_shape=[jax.Sha...]
    ppermute x15, waiting for transfers between devices: 50.7 us -> 67 us  [dp_swap(): return lax.ppermute(value, DP, [(0, 1), (1, 0)])]
    concatenate x5 -> x1, local copies, waits for them, and re-layouts: 12.5 us -> 0.83 us  [per_device(): jnp.concatenate([norm_back(latent_grad * gain_lat, normed_lat, factor_lat...]
    unnamed x234 -> x224, local copies, waits for them, and re-layouts: 27.6 us -> 21.1 us
  transfers between devices with their start and end apart: 22 -> 22, of which waited for: 2 -> 5; matrix products, arithmetic and copies ran while one was open for 44% -> 33% of each run, Pallas kernels for 37% -> 28%
where the time goes in v3:
time: 975 us; the launch traced here: 967 us
  Pallas kernels  389 us (40%)
  matrix products  259 us (27%)
  local copies, waits for them, and re-layouts  99.6 us (10%)
  other arithmetic  87 us (9%)
  waiting for transfers between devices  76.1 us (8%)
  starting transfers between devices  40.3 us (4%)
  between operations  16 us (2%)
    pallas_call x2, Pallas kernels, ring_gather(): pl.pallas_call(functools.partial(gather_kernel, n, m), out_shape=[jax.Sha...  199 us
    pallas_call x2, Pallas kernels, ring_scatter(): pl.pallas_call(functools.partial(scatter_kernel, n), out_shape=[jax.Shape...  160 us
    dot_general x8, matrix products, right_product(): lax.dot_general(left, right, (((1,), (1,)), ((), ())), preferred_element_...  75.8 us
    dot_general x11, matrix products, left_product(): lax.dot_general(left, right, (((0,), (0,)), ((), ())), preferred_element_...  73.8 us
    ppermute x15, waiting for transfers between devices, dp_swap(): return lax.ppermute(value, DP, [(0, 1), (1, 0)])  67 us
    dot_general x9, matrix products, product(): return jnp.dot(left, right, preferred_element_type=f32)  59.1 us
    dot_general x10, matrix products, einsum(): return jnp.einsum(spec, left, right, preferred_element_type=f32)  42.9 us
    pallas_call x2, Pallas kernels, swap_call(): pl.pallas_call(functools.partial(swap_kernel, source, target), out_shape=...  29.4 us
  transfers between devices with their start and end apart: 22, of which 5 were waited for; matrix products, arithmetic and copies ran while one was open for 33% of the time, Pallas kernels for 28%

profile of v3, /device:TPU:0, one launch (start us, length us, event | category | flops | bytes accessed | tf_op | source)
XLA Modules:
  0.0 966.9 jit_solution(3762852204645662583)
XLA Ops:
  21.6 6.4 all-to-all-start
  39.2 139.5 %shard_map.306 = (bf16[16,128,640]{2,1,0:T(8,128)(2,1)}, bf16[16,128,2048]{2,1,0:T(8,128)(2,1)}, bf16[16,64,192]{2,1,0:T(8,128)(2,1)}, bf16[16,32,256]{2,1,0:T(8,128)(2,1)}) custom-call(bf16[128,640]{1,0:T(8,128)(2,1)} %pad_maximum_fusion.30.refs_0_, bf16[128,2048]{1,0:T(8,128)(2,1)} %bitcast.220, bf16[16,64,192]{2,1,0:T(8,128)(2,1)} %bitcast.256, ...), custom_call_target="tpu_custom_call" | custom-call | bytes 175636480 | tf_op jit(solution)/shard_map/pallas_call | solution.py:295
  189.3 5.4 multiply_reduce_fusion
  194.8 8.7 fusion.4
  203.5 7.8 fusion.98
  211.7 32.2 %collective-permute-done.2 = bf16[256,256]{1,0:T(8,128)(2,1)} collective-permute-done((bf16[256,256]{1,0:T(8,128)(2,1)}, bf16[256,256]{1,0:T(8,128)(2,1)}, u32[]{:S(2)}, u32[]{:S(2)}) %collective-permute-start.2) | collective-permute-done | bytes 131104 | tf_op jit(solution)/shard_map/ppermute | solution.py:88
  266.4 7.8 fusion.107
  286.5 15.2 %shard_map.307 = bf16[2,64,2048]{2,1,0:T(8,128)(2,1)} custom-call(bf16[2,1024,128]{2,1,0:T(8,128)(2,1)} %convolution_convert_fusion.9.x_ref), custom_call_target="tpu_custom_call" | custom-call | bytes 33554432 | tf_op jit(solution)/shard_map/pallas_call | solution.py:481
  302.7 5.5 broadcast_select_fusion.1
  308.2 5.7 broadcast_select_fusion.3
  313.9 5.8 broadcast_select_fusion.5
  319.7 7.3 convolution_convert_fusion.3
  327.0 6.6 multiply_reduce_fusion.9
  334.7 59.8 %shard_map.308 = bf16[16,128,2048]{2,1,0:T(8,128)(2,1)} custom-call(bf16[128,2048]{1,0:T(8,128)(2,1)} %multiply_convert_fusion.9.refs_0_), custom_call_target="tpu_custom_call" | custom-call | bytes 125829120 | tf_op jit(solution)/shard_map/pallas_call | solution.py:295
  394.5 6.1 fusion.57
  402.4 5.5 convolution_convert_fusion.4
  408.0 7.2 fusion.23
  415.3 9.6 multiply_convert_fusion.3
  424.9 7.4 fusion.6
  434.1 7.7 fusion.7
  441.8 13.9 %multiply_convert_fusion.2 = (bf16[864,1408]{1,0:T(8,128)(2,1)}, bf16[864,1408]{1,0:T(8,128)(2,1)}) fusion(f32[864,1408]{1,0:T(8,128)} %fusion.23, f32[864,1408]{1,0:T(8,128)} %get-tuple-element.171, bf16[864,2048]{1,0:T(8,128)(2,1)S(1)} %get-tuple-element.164, bf16[704,2048]{1,0:T(8,128)(2,1)S(1)} %copy-done.37, bf16[704,2048]{1,0:T(8,128)(2,1)S(1)} %copy-done.35), kind=kOutput, calls=%fused_computation.34 | convolution fusion | flops 5010182144 | bytes 23904256 | tf_op jit(solution)/shard_map/dot_general | solution.py:39
  455.7 10.8 %fusion.20 = f32[864,2048]{1,0:T(8,128)} fusion(bf16[864,1408]{1,0:T(8,128)(2,1)} %get-tuple-element.124, bf16[1024,1408]{1,0:T(8,128)(2,1)} %get-tuple-element.130, bf16[1024,1408]{1,0:T(8,128)(2,1)} %get-tuple-element.129), kind=kOutput, calls=%fused_computation.56 | convolution fusion | flops 4994367488 | bytes 15278080 | tf_op jit(solution)/shard_map/dot_general | solution.py:39
  466.5 10.0 %add_convert_fusion = bf16[864,2048]{1,0:T(8,128)(2,1)S(1)} fusion(f32[864,2048]{1,0:T(8,128)} %fusion.20, bf16[864,1408]{1,0:T(8,128)(2,1)} %get-tuple-element.123, bf16[1024,1408]{1,0:T(8,128)(2,1)} %get-tuple-element.128, bf16[1024,1408]{1,0:T(8,128)(2,1)S(1)} %copy-done.41), kind=kOutput, calls=%fused_computation.22 | convolution fusion | flops 4997906432 | bytes 18817024 | tf_op jit(solution)/shard_map/dot_general | solution.py:39
  476.5 8.3 fusion.109
  484.9 6.4 multiply_convert_fusion.7
  491.3 10.6 %fusion.1 = bf16[2048,2048]{1,0:T(8,128)(2,1)} fusion(f32[4,512,2048]{2,1,0:T(8,128)} %fusion.109, bf16[2048,16]{0,1:T(8,128)(2,1)S(1)} %multiply_convert_fusion.10, bf16[2048,176]{0,1:T(8,128)(2,1)} %get-tuple-element.134, bf16[2048,176]{0,1:T(8,128)(2,1)} %get-tuple-element.133, bf16[2048,16]{0,1:T(8,128)(2,1)S(1)} %copy-done.76, ...), kind=kOutput, calls=%fused_computation.2 | convolution fusion | flops 3104440320 | bytes 28180480 | tf_op jit(solution)/shard_map/dot_general | solution.py:39
  502.0 56.9 %shard_map.309 = f32[128,2048]{1,0:T(8,128)} custom-call(bf16[16,128,2048]{2,1,0:T(8,128)(2,1)} %bitcast.210), custom_call_target="tpu_custom_call" | custom-call | bytes 125829120 | tf_op jit(solution)/shard_map/pallas_call | solution.py:443
  570.3 6.0 fusion.56
  578.8 5.5 convolution_convert_fusion.7
  584.4 14.2 %shard_map.310 = bf16[2,1024,128]{2,1,0:T(8,128)(2,1)} custom-call(bf16[2,64,2048]{2,1,0:T(8,128)(2,1)} %bitcast.259), custom_call_target="tpu_custom_call" | custom-call | bytes 33554432 | tf_op jit(solution)/shard_map/pallas_call | solution.py:481
  606.3 5.3 fusion.113
  616.9 5.2 convolution_convert_fusion.5
  622.9 5.4 convolution_convert_fusion.1
  652.7 5.6 multiply_reduce_fusion.2
  665.7 8.3 fusion.108
  674.0 11.6 %fusion.2 = bf16[2048,2048]{1,0:T(8,128)(2,1)} fusion(f32[4,512,2048]{2,1,0:T(8,128)} %fusion.108, bf16[2048,176]{0,1:T(8,128)(2,1)S(1)} %copy-done.62, bf16[88,2048]{1,0:T(8,128)(2,1)S(1)} %copy-done.55, bf16[88,2048]{1,0:T(8,128)(2,1)S(1)} %copy-done.53), kind=kOutput, calls=%fused_computation.4 | convolution fusion | flops 1486225408 | bytes 26607616 | tf_op jit(solution)/shard_map/dot_general | solution.py:31
  688.0 12.4 %multiply_reduce_fusion.1 = (f32[2048]{0:T(1024)S(1)}, f32[2048,768]{0,1:T(8,128)}) fusion(bf16[1024,192]{0,1:T(8,128)(2,1)} %copy-done.72, bf16[1024,192]{0,1:T(8,128)(2,1)S(1)} %copy-done.71, bf16[2048,576]{0,1:T(8,128)(2,1)} %copy.302, bf16[2048,768]{0,1:T(8,128)(2,1)} %convert_dynamic-update-slice_fusion, bf16[2048,2048]{1,0:T(8,128)(2,1)} %fusion.4), kind=kOutput, calls=%fused_computation.23 | convolution fusion | flops 6469187584 | bytes 20979712 | tf_op jit(solution)/shard_map/dot_general | solution.py:35
  711.7 11.8 %convolution_convert_fusion = bf16[2048,2048]{1,0:T(8,128)(2,1)} fusion(bf16[2048,768]{0,1:T(8,128)(2,1)} %convert_dynamic-update-slice_fusion, bf16[1024,192]{0,1:T(8,128)(2,1)S(1)} %copy-done.73, bf16[1024,192]{0,1:T(8,128)(2,1)S(1)} %copy-done.71, bf16[2048,576]{0,1:T(8,128)(2,1)} %copy.302), kind=kOutput, calls=%fused_computation.18 | convolution fusion | flops 6470238208 | bytes 14680064 | tf_op jit(solution)/shard_map/dot_general | solution.py:39
  723.5 102.9 %shard_map.311 = (f32[2,64,576]{2,1,0:T(8,128)}, f32[2,64,128]{2,1,0:T(8,128)}, f32[128,2048]{1,0:T(8,128)}) custom-call(bf16[2,16,64,576]{3,2,1,0:T(8,128)(2,1)} %bitcast.224, bf16[2,16,64,128]{3,2,1,0:T(8,128)(2,1)} %bitcast.257, bf16[16,128,2048]{2,1,0:T(8,128)(2,1)} %bitcast.232), custom_call_target="tpu_custom_call" | custom-call | bytes 169082880 | tf_op jit(solution)/shard_map/pallas_call | solution.py:443
  832.6 4.9 convolution_convert_fusion.2
  853.0 6.9 all-to-all-start.2
  862.1 4.8 fusion.112
  870.2 8.4 all-to-all-done.2
  888.1 9.7 %add_bitcast_fusion.1 = f32[1,1024,1408]{2,1,0:T(8,128)} fusion(bf16[1024,1408]{1,0:T(8,128)(2,1)} %collective-permute-done.13, bf16[864,1408]{1,0:T(8,128)(2,1)} %get-tuple-element.124, pred[]{:T(512)S(6)} %eq.102, bf16[864,2048]{1,0:T(8,128)(2,1)} %bitcast.246), kind=kOutput, calls=%fused_computation.29 | convolution fusion | flops 2495184896 | bytes 14622721 | tf_op jit(solution)/shard_map/dot_general | solution.py:35
  897.9 29.5 %collective-permute-done.8 = bf16[1024,384]{0,1:T(8,128)(2,1)} collective-permute-done((bf16[1024,384]{0,1:T(8,128)(2,1)S(1)}, bf16[1024,384]{0,1:T(8,128)(2,1)}, u32[]{:S(2)}, u32[]{:S(2)}) %collective-permute-start.8) | collective-permute-done | bytes 786464 | tf_op jit(solution)/shard_map/ppermute | solution.py:88
  929.9 6.0 all-to-all-start.1
  935.9 9.7 %add_bitcast_fusion.2 = f32[1,1024,1408]{2,1,0:T(8,128)} fusion(bf16[1024,1408]{1,0:T(8,128)(2,1)} %collective-permute-done.12, bf16[864,1408]{1,0:T(8,128)(2,1)} %get-tuple-element.123, pred[]{:T(512)S(6)} %eq.102, bf16[864,2048]{1,0:T(8,128)(2,1)} %bitcast.247), kind=kOutput, calls=%fused_computation.30 | convolution fusion | flops 2495184896 | bytes 14622721 | tf_op jit(solution)/shard_map/dot_general | solution.py:35
  945.7 7.1 add_bitcast_fusion
  (434 shorter events, 195.2 us)
Async XLA Ops:
  7.2 312.5 %all-gather.6.cloned.1.call-start = ((), (), s32[]{:S(2)}) async-start(), calls=%async_computation.6 | async-start | bytes 8912896 | tf_op jit(solution)/shard_map/all_gather | solution.py:129
  12.0 26.5 %collective-permute-start = (bf16[64,640]{1,0:T(8,128)(2,1)S(1)}, bf16[64,640]{1,0:T(8,128)(2,1)S(1)}, u32[]{:S(2)}, u32[]{:S(2)}) collective-permute-start(bf16[64,640]{1,0:T(8,128)(2,1)S(1)} %concatenate.81), channel_id=1, source_target_pairs={{0,16},{16,0},{1,17},{17,1},{2,18},{18,2},{3,19},{19,3},{4,20},{20... | collective-permute-start | bytes 245768 | tf_op jit(solution)/shard_map/ppermute | solution.py:88
  15.0 233.2 %collective-permute-start.4 = (bf16[88,2048]{1,0:T(8,128)(2,1)}, bf16[88,2048]{1,0:T(8,128)(2,1)}, u32[]{:S(2)}, u32[]{:S(2)}) collective-permute-start(bf16[88,2048]{1,0:T(8,128)(2,1)} %param.33), channel_id=1, source_target_pairs={{0,16},{16,0},{1,17},{17,1},{2,18},{18,2},{3,19},{19,3},{4,20},{20... | collective-permute-start | bytes 1081352 | tf_op jit(solution)/shard_map/ppermute | solution.py:88
  18.2 13.7 %copy-start.92 = (s32[2,64,6]{1,0,2:T(2,128)S(1)}, s32[2,64,6]{1,0,2:T(2,128)}, u32[]{:S(2)}) copy-start(s32[2,64,6]{1,0,2:T(2,128)} %param.21) | copy-start | bytes 9220
  18.2 13.7 %copy-start.100 = (s32[2,64]{1,0:T(2,128)S(1)}, s32[2,64]{1,0:T(2,128)}, u32[]{:S(2)}) copy-start(s32[2,64]{1,0:T(2,128)} %param.22) | copy-start | bytes 1540
  18.2 14.1 %copy-start.82 = (bf16[16,4096]{1,0:T(8,128)(2,1)S(1)}, bf16[16,4096]{1,0:T(8,128)(2,1)}, u32[]{:S(2)}) copy-start(bf16[16,4096]{1,0:T(8,128)(2,1)} %param.26) | copy-start | bytes 393220
  19.5 14.6 %copy-start.69 = (bf16[64,3072]{1,0:T(8,128)(2,1)S(1)}, bf16[64,3072]{1,0:T(8,128)(2,1)}, u32[]{:S(2)}) copy-start(bf16[64,3072]{1,0:T(8,128)(2,1)} %param.24) | copy-start | bytes 1179652
  21.6 252.6 %all-to-all-start = ((bf16[16,64,352]{2,1,0:T(8,128)(2,1)}), bf16[16,64,352]{2,1,0:T(8,128)(2,1)}, u32[]{:S(2)}, u32[]{:S(2)}) async-start(bf16[16,64,352]{2,1,0:T(8,128)(2,1)} %pad_maximum_fusion.18), calls=%async_computation | async-start | bytes 1572864 | tf_op jit(solution)/shard_map/all_to_all | solution.py:125
  28.0 299.0 %all-gather.4.cloned.1.call-start = ((), (), s32[]{:S(2)}) async-start(), calls=%async_computation.4 | async-start | bytes 8650752 | tf_op jit(solution)/shard_map/all_gather | solution.py:129
  28.1 274.6 %collective-permute-start.7 = (bf16[704,2048]{1,0:T(8,128)(2,1)}, bf16[704,2048]{1,0:T(8,128)(2,1)}, u32[]{:S(2)}, u32[]{:S(2)}) collective-permute-start(bf16[704,2048]{1,0:T(8,128)(2,1)} %bitcast.36), channel_id=1, source_target_pairs={{0,16},{16,0},{1,17},{17,1},{2,18},{18,2},{3,19},{19,3},{4,20},{20... | collective-permute-start | bytes 8650760 | tf_op jit(solution)/shard_map/ppermute | solution.py:88
  29.6 278.6 %collective-permute-start.6 = (bf16[1024,1408]{1,0:T(8,128)(2,1)}, bf16[1024,1408]{1,0:T(8,128)(2,1)}, u32[]{:S(2)}, u32[]{:S(2)}) collective-permute-start(bf16[1024,1408]{1,0:T(8,128)(2,1)} %bitcast.35), channel_id=1, source_target_pairs={{0,16},{16,0},{1,17},{17,1},{2,18},{18,2},{3,19},{19,3},{4,20},{20... | collective-permute-start | bytes 8650760 | tf_op jit(solution)/shard_map/ppermute | solution.py:88
  30.2 283.7 %collective-permute-start.5 = (bf16[1024,1408]{1,0:T(8,128)(2,1)}, bf16[1024,1408]{1,0:T(8,128)(2,1)}, u32[]{:S(2)}, u32[]{:S(2)}) collective-permute-start(bf16[1024,1408]{1,0:T(8,128)(2,1)} %bitcast.34), channel_id=1, source_target_pairs={{0,16},{16,0},{1,17},{17,1},{2,18},{18,2},{3,19},{19,3},{4,20},{20... | collective-permute-start | bytes 8650760 | tf_op jit(solution)/shard_map/ppermute | solution.py:88
  31.7 830.4 %all-gather.8.cloned.1.call-start = ((), (), s32[]{:S(2)}) async-start(), calls=%async_computation.7 | async-start | bytes 8912896 | tf_op jit(solution)/shard_map/all_gather | solution.py:129
  180.8 22.7 %copy-start.7 = (bf16[16,2,64,640]{3,2,0,1:T(8,128)(2,1)}, bf16[16,2,64,640]{3,2,0,1:T(8,128)(2,1)S(1)}, u32[]{:S(2)}) copy-start(bf16[16,2,64,640]{3,2,0,1:T(8,128)(2,1)S(1)} %copy.241) | copy-start | bytes 7864324
  182.7 61.2 %collective-permute-start.2 = (bf16[256,256]{1,0:T(8,128)(2,1)}, bf16[256,256]{1,0:T(8,128)(2,1)}, u32[]{:S(2)}, u32[]{:S(2)}) collective-permute-start(bf16[256,256]{1,0:T(8,128)(2,1)} %bitcast.19), channel_id=1, source_target_pairs={{0,16},{16,0},{1,17},{17,1},{2,18},{18,2},{3,19},{19,3},{4,20},{20... | collective-permute-start | bytes 393224 | tf_op jit(solution)/shard_map/ppermute | solution.py:88
  189.1 371.3 %copy-start.78 = (f32[2048]{0:T(1024)}, f32[2048]{0:T(1024)S(1)}, u32[]{:S(2)}) copy-start(f32[2048]{0:T(1024)S(1)} %get-tuple-element.118) | copy-start | bytes 24580
  189.3 57.1 %copy-start.87 = (f32[512]{0:T(512)}, f32[512]{0:T(512)S(1)}, u32[]{:S(2)}) copy-start(f32[512]{0:T(512)S(1)} %mul.391) | copy-start | bytes 6148
  203.5 40.4 %copy-start.51 = (bf16[1024,192]{0,1:T(8,128)(2,1)S(1)}, bf16[1024,192]{0,1:T(8,128)(2,1)}, u32[]{:S(2)}) copy-start(bf16[1024,192]{0,1:T(8,128)(2,1)} %copy.243) | copy-start | bytes 1179652
  211.3 46.2 %copy-start.1 = (f32[2048,576]{0,1:T(8,128)}, f32[2048,576]{0,1:T(8,128)S(1)}, u32[]{:S(2)}) copy-start(f32[2048,576]{0,1:T(8,128)S(1)} %fusion.98) | copy-start | bytes 14155780
  211.3 43.2 %slice-start = ((s8[8388608]{0:T(1024)(128)(4,1)}), s8[4194304]{0:T(1024)(128)(4,1)S(1)}, s32[]{:S(2)}) async-start(s8[8388608]{0:T(1024)(128)(4,1)} %bitcast.225), calls=%async_computation.8 | async-start | bytes 8388608
  211.6 34.7 %copy-start.85 = (f32[2048]{0:T(1024)}, f32[2048]{0:T(1024)S(1)}, u32[]{:S(2)}) copy-start(f32[2048]{0:T(1024)S(1)} %add_rsqrt_fusion) | copy-start | bytes 24580
  243.9 10.5 %collective-permute-start.1 = (bf16[1024,192]{0,1:T(8,128)(2,1)S(1)}, bf16[1024,192]{0,1:T(8,128)(2,1)S(1)}, u32[]{:S(2)}, u32[]{:S(2)}) collective-permute-start(bf16[1024,192]{0,1:T(8,128)(2,1)S(1)} %copy-done.51), channel_id=1, source_target_pairs={{0,16},{16,0},{1,17},{17,1},{2,18},{18,2},{3,19},{19,3},{4,20},{20... | collective-permute-start | bytes 1179656 | tf_op jit(solution)/shard_map/ppermute | solution.py:88
  248.3 33.6 %copy-start.44 = (bf16[2,16,64,128]{3,2,1,0:T(8,128)(2,1)}, bf16[2,16,64,128]{3,2,1,0:T(8,128)(2,1)S(1)}, u32[]{:S(2)}) copy-start(bf16[2,16,64,128]{3,2,1,0:T(8,128)(2,1)S(1)} %copy.255) | copy-start | bytes 1572868
  275.6 26.1 %collective-permute-start.3 = (bf16[1024,352]{0,1:T(8,128)(2,1)S(1)}, bf16[1024,352]{0,1:T(8,128)(2,1)S(1)}, u32[]{:S(2)}, u32[]{:S(2)}) collective-permute-start(bf16[1024,352]{0,1:T(8,128)(2,1)S(1)} %copy.260), channel_id=1, source_target_pairs={{0,16},{16,0},{1,17},{17,1},{2,18},{18,2},{3,19},{19,3},{4,20},{20... | collective-permute-start | bytes 2162696 | tf_op jit(solution)/shard_map/ppermute | solution.py:88
  333.6 226.9 %copy-start.4 = (f32[128,2048]{1,0:T(8,128)}, f32[128,2048]{1,0:T(8,128)S(1)}, u32[]{:S(2)}) copy-start(f32[128,2048]{1,0:T(8,128)S(1)} %get-tuple-element.169) | copy-start | bytes 3145732
  333.6 226.9 %copy-start.90 = (f32[128]{0:T(128)}, f32[128]{0:T(128)S(1)}, u32[]{:S(2)}) copy-start(f32[128]{0:T(128)S(1)} %add_rsqrt_fusion.2) | copy-start | bytes 1540
  334.7 59.8 %copy-start.76 = (bf16[2048,16]{0,1:T(8,128)(2,1)S(1)}, bf16[2048,16]{0,1:T(8,128)(2,1)}, u32[]{:S(2)}) copy-start(bf16[2048,16]{0,1:T(8,128)(2,1)} %copy.262) | copy-start | bytes 196612
  441.8 13.9 %copy-start.9 = (bf16[864,2048]{1,0:T(8,128)(2,1)}, bf16[864,2048]{1,0:T(8,128)(2,1)S(1)}, u32[]{:S(2)}) copy-start(bf16[864,2048]{1,0:T(8,128)(2,1)S(1)} %get-tuple-element.164) | copy-start | bytes 10616836
  455.7 29.2 %slice-start.2 = ((s8[8388608]{0:T(1024)(128)(4,1)}), s8[4194304]{0:T(1024)(128)(4,1)S(1)}, s32[]{:S(2)}) async-start(s8[8388608]{0:T(1024)(128)(4,1)} %bitcast.230), calls=%async_computation.10 | async-start | bytes 8388608
  466.5 18.3 %slice-start.3 = ((s8[8388608]{0:T(1024)(128)(4,1)}), s8[4194304]{0:T(1024)(128)(4,1)S(1)}, s32[]{:S(2)}) async-start(s8[8388608]{0:T(1024)(128)(4,1)} %bitcast.230), calls=%async_computation.11 | async-start | bytes 8388608
  501.9 58.5 %copy-start.24 = (bf16[2,64,2048]{2,1,0:T(8,128)(2,1)S(1)}, bf16[2,64,2048]{2,1,0:T(8,128)(2,1)}, u32[]{:S(2)}) copy-start(bf16[2,64,2048]{2,1,0:T(8,128)(2,1)} %param.23) | copy-start | bytes 1572868
  562.9 389.9 %reduce-scatter.2.cloned.1.call-start = ((), (), s32[]{:S(2)}) async-start(), calls=%async_computation.5 | async-start | bytes 8912896 | tf_op jit(solution)/shard_map/reduce_scatter | solution.py:133
  578.8 21.1 %copy-start.45 = (bf16[2,16,64,128]{3,2,1,0:T(8,128)(2,1)S(1)}, bf16[2,16,64,128]{3,2,1,0:T(8,128)(2,1)}, u32[]{:S(2)}) copy-start(bf16[2,16,64,128]{3,2,1,0:T(8,128)(2,1)} %copy-done.44) | copy-start | bytes 1572868
  612.6 247.4 %collective-permute-start.11 = (bf16[88,2048]{1,0:T(8,128)(2,1)}, bf16[88,2048]{1,0:T(8,128)(2,1)}, u32[]{:S(2)}, u32[]{:S(2)}) collective-permute-start(bf16[88,2048]{1,0:T(8,128)(2,1)} %dynamic-slice_convert_fusion.2), channel_id=1, source_target_pairs={{0,16},{16,0},{1,17},{17,1},{2,18},{18,2},{3,19},{19,3},{4,20},{20... | collective-permute-start | bytes 1081352 | tf_op jit(solution)/shard_map/ppermute | solution.py:88
  615.7 234.4 %collective-permute-start.10 = (bf16[1024,352]{0,1:T(8,128)(2,1)}, bf16[1024,352]{0,1:T(8,128)(2,1)}, u32[]{:S(2)}, u32[]{:S(2)}) collective-permute-start(bf16[1024,352]{0,1:T(8,128)(2,1)} %dynamic-slice_convert_fusion.1), channel_id=1, source_target_pairs={{0,16},{16,0},{1,17},{17,1},{2,18},{18,2},{3,19},{19,3},{4,20},{20... | collective-permute-start | bytes 2162696 | tf_op jit(solution)/shard_map/ppermute | solution.py:88
  622.1 323.5 %collective-permute-start.14 = (bf16[704,2048]{1,0:T(8,128)(2,1)}, bf16[704,2048]{1,0:T(8,128)(2,1)}, u32[]{:S(2)}, u32[]{:S(2)}) collective-permute-start(bf16[704,2048]{1,0:T(8,128)(2,1)} %convolution_convert_fusion.5), channel_id=1, source_target_pairs={{0,16},{16,0},{1,17},{17,1},{2,18},{18,2},{3,19},{19,3},{4,20},{20... | collective-permute-start | bytes 8650760 | tf_op jit(solution)/shard_map/ppermute | solution.py:88
  628.4 259.8 %collective-permute-start.13 = (bf16[1024,1408]{1,0:T(8,128)(2,1)}, bf16[1024,1408]{1,0:T(8,128)(2,1)}, u32[]{:S(2)}, u32[]{:S(2)}) collective-permute-start(bf16[1024,1408]{1,0:T(8,128)(2,1)} %convolution_convert_fusion.1), channel_id=1, source_target_pairs={{0,16},{16,0},{1,17},{17,1},{2,18},{18,2},{3,19},{19,3},{4,20},{20... | collective-permute-start | bytes 8650760 | tf_op jit(solution)/shard_map/ppermute | solution.py:88
  687.9 13.2 %copy-start.96 = (pred[128]{0:T(512)(128)(4,1)S(1)}, pred[128]{0:T(512)(128)(4,1)}, u32[]{:S(2)}) copy-start(pred[128]{0:T(512)(128)(4,1)} %iota_compare_fusion.7) | copy-start | bytes 388
  687.9 13.2 %copy-start.97 = (pred[128]{0:T(512)(128)(4,1)S(1)}, pred[128]{0:T(512)(128)(4,1)}, u32[]{:S(2)}) copy-start(pred[128]{0:T(512)(128)(4,1)} %get-tuple-element.179) | copy-start | bytes 388
  723.5 104.0 %copy-start.81 = (f32[2048]{0:T(1024)S(1)}, f32[2048]{0:T(1024)}, u32[]{:S(2)}) copy-start(f32[2048]{0:T(1024)} %copy-done.80) | copy-start | bytes 24580
  723.5 104.0 %copy-start.95 = (f32[128]{0:T(128)S(1)}, f32[128]{0:T(128)}, u32[]{:S(2)}) copy-start(f32[128]{0:T(128)} %rsqrt.43) | copy-start | bytes 1540
  723.5 105.8 %copy-start.30 = (bf16[16,2,64,256]{3,2,1,0:T(8,128)(2,1)S(1)}, bf16[16,2,64,256]{3,2,1,0:T(8,128)(2,1)}, u32[]{:S(2)}) copy-start(bf16[16,2,64,256]{3,2,1,0:T(8,128)(2,1)} %copy.267) | copy-start | bytes 3145732
  838.3 6.9 collective-permute-start.9
  845.2 90.7 %collective-permute-start.12 = (bf16[1024,1408]{1,0:T(8,128)(2,1)}, bf16[1024,1408]{1,0:T(8,128)(2,1)}, u32[]{:S(2)}, u32[]{:S(2)}) collective-permute-start(bf16[1024,1408]{1,0:T(8,128)(2,1)} %convolution_convert_fusion.2), channel_id=1, source_target_pairs={{0,16},{16,0},{1,17},{17,1},{2,18},{18,2},{3,19},{19,3},{4,20},{20... | collective-permute-start | bytes 8650760 | tf_op jit(solution)/shard_map/ppermute | solution.py:88
  853.0 25.5 %all-to-all-start.2 = ((bf16[16,64,352]{2,1,0:T(8,128)(2,1)}), bf16[16,64,352]{2,1,0:T(8,128)(2,1)S(1)}, u32[]{:S(2)}, u32[]{:S(2)}) async-start(bf16[16,64,352]{2,1,0:T(8,128)(2,1)} %bitcast.73), calls=%async_computation.3 | async-start | bytes 1572864 | tf_op jit(solution)/shard_map/all_to_all | solution.py:125
  868.9 58.4 %collective-permute-start.8 = (bf16[1024,384]{0,1:T(8,128)(2,1)S(1)}, bf16[1024,384]{0,1:T(8,128)(2,1)}, u32[]{:S(2)}, u32[]{:S(2)}) collective-permute-start(bf16[1024,384]{0,1:T(8,128)(2,1)S(1)} %dynamic-slice_convert_fusion), channel_id=1, source_target_pairs={{0,16},{16,0},{1,17},{17,1},{2,18},{18,2},{3,19},{19,3},{4,20},{20... | collective-permute-start | bytes 2359304 | tf_op jit(solution)/shard_map/ppermute | solution.py:88
  888.1 39.2 %copy-start.16 = (f32[2048,384]{0,1:T(8,128)S(1)}, f32[2048,384]{0,1:T(8,128)}, u32[]{:S(2)}) copy-start(f32[2048,384]{0,1:T(8,128)} %copy-done.15) | copy-start | bytes 9437188
  929.9 26.0 %all-to-all-start.1 = ((bf16[16,64,384]{2,1,0:T(8,128)(2,1)}), bf16[16,64,384]{2,1,0:T(8,128)(2,1)S(1)}, u32[]{:S(2)}, u32[]{:S(2)}) async-start(bf16[16,64,384]{2,1,0:T(8,128)(2,1)} %bitcast.66), calls=%async_computation.2 | async-start | bytes 1572864 | tf_op jit(solution)/shard_map/all_to_all | solution.py:125
  (82 other events, 502.7 us)
Sparse Core Ops, SparseCore 0:
  10.2 121.7 all-gather.5
  134.9 99.1 all-gather.3
  563.0 75.6 all-gather.7
  685.8 141.4 reduce-scatter.1

commit v4 on v3

--- a/solution.py
+++ b/solution.py
@@ -57,26 +57,6 @@
     freqs = jnp.power(10000.0, -2.0 * jnp.arange(half, dtype=f32) / width)
     angles = positions.astype(f32)[:, None] * freqs[None, :]
     return (jnp.cos(angles), jnp.sin(angles))
-
-
-def rotate(values, tables):
-    half = values.shape[-1] // 2
-    cosine, sine = tables
-    first = values[..., :half]
-    second = values[..., half:]
-    return jnp.concatenate(
-        [first * cosine - second * sine, second * cosine + first * sine], axis=-1
-    )
-
-
-def unrotate(grads, tables):
-    half = grads.shape[-1] // 2
-    cosine, sine = tables
-    first = grads[..., :half]
-    second = grads[..., half:]
-    return jnp.concatenate(
-        [first * cosine + second * sine, second * cosine - first * sine], axis=-1
-    )
 
 
 def silu_slope(pre):
@@ -513,6 +493,297 @@
     return swap_call(
         head_columns(VD), block_rows(span), value, (seqs, span * HEADS, VD), collective
     )
+
+
+def matmul(left, right, dims):
+    return lax.dot_general(left, right, (dims, ((), ())), preferred_element_type=f32)
+
+
+ROWS_ROWS = ((0,), (0,))
+COLS_COLS = ((1,), (1,))
+COLS_ROWS = ((1,), (0,))
+
+
+def full(shape):
+    return pl.BlockSpec(shape, lambda *_: (0,) * len(shape), pipeline_mode=pl.Buffered(1))
+
+
+def tiled(rows, columns):
+    return pl.BlockSpec((rows, columns), lambda i: (i, 0))
+
+
+def estimate(flops, nbytes):
+    return pl.CostEstimate(
+        flops=int(flops), bytes_accessed=int(nbytes), transcendentals=0
+    )
+
+
+def combine_kernel(dims, select_ref, slot_ref, left_ref, right_ref, out_ref):
+    routed = matmul(select_ref[0], slot_ref[0], ROWS_ROWS)
+    out_ref[...] = (routed + matmul(left_ref[...], right_ref[...], dims)).astype(bf16)
+
+
+def combine(select, slot_rows, left, right, dims):
+    chunks, slots, chunk = select.shape
+    width = slot_rows.shape[-1]
+    tile = 256
+    per = chunk // tile
+    inner = left.shape[1]
+    return pl.pallas_call(
+        functools.partial(combine_kernel, dims),
+        grid=(chunks, per),
+        in_specs=[
+            pl.BlockSpec((1, slots, tile), lambda c, t: (c, 0, t)),
+            pl.BlockSpec((1, slots, width), lambda c, t: (c, 0, 0)),
+            pl.BlockSpec((tile, inner), lambda c, t: (c * per + t, 0)),
+            full(right.shape),
+        ],
+        out_specs=pl.BlockSpec((tile, width), lambda c, t: (c * per + t, 0)),
+        out_shape=jax.ShapeDtypeStruct((chunks * chunk, width), bf16),
+        cost_estimate=estimate(
+            2 * chunks * chunk * width * (slots + inner), 4 * chunks * chunk * width
+        ),
+    )(select, slot_rows.reshape(chunks, slots, width), left, right)
+
+
+def turn(values, cosine, sine):
+    lane = lax.broadcasted_iota(jnp.int32, values.shape, 1)
+    other = jnp.where(lane % 64 < 32, pltpu.roll(values, 96, 1), pltpu.roll(values, 32, 1))
+    return values * cosine + other * sine
+
+
+def project_kernel(
+    x_ref, weight_ref, lup_ref, gain_ref, gain_lat_ref, cos_ref, sin_ref,
+    h_ref, query_ref, key_ref, value_ref, latent_ref, normed_ref, factor_ref,
+):
+    x = x_ref[...].astype(f32)
+    factor = lax.rsqrt(jnp.mean(x * x, axis=-1, keepdims=True) + epsilon)
+    h = (x * factor * gain_ref[...]).astype(bf16)
+    h_ref[...] = h
+    raw = matmul(h, weight_ref[...], COLS_ROWS)
+    low = raw[:, :RANK]
+    factor = lax.rsqrt(jnp.mean(low * low, axis=-1, keepdims=True) + epsilon)
+    normed = low * factor
+    normed_ref[...] = normed
+    factor_ref[...] = factor
+    latent = (normed * gain_lat_ref[...]).astype(bf16)
+    latent_ref[...] = latent
+    expanded = matmul(latent, lup_ref[...], COLS_ROWS)
+    rope = turn(raw[:, RANK : RANK + 128], cos_ref[...], sin_ref[...])
+    lane = lax.broadcasted_iota(jnp.int32, rope.shape, 1)
+    query_ref[:, :HD] = raw[:, RANK + 128 :].astype(bf16)
+    query_ref[:, HD:] = jnp.where(lane < RD, pltpu.roll(rope, 64, 1), 0.0).astype(bf16)
+    key_ref[:, :HD] = expanded[:, :HD].astype(bf16)
+    key_ref[:, HD:] = jnp.where(lane < RD, rope, 0.0).astype(bf16)
+    value_ref[...] = expanded[:, HD:].astype(bf16)
+
+
+def project(x_all, weight, lup, gain, gain_lat, cosine, sine):
+    tokens, width = x_all.shape
+    tile = 256
+    outs = [
+        ((tokens, width), bf16),
+        ((tokens, HD + 128), bf16),
+        ((tokens, HD + 128), bf16),
+        ((tokens, VD), bf16),
+        ((tokens, RANK), bf16),
+        ((tokens, RANK), f32),
+        ((tokens, 1), f32),
+    ]
+    return pl.pallas_call(
+        project_kernel,
+        name="project",
+        grid=(tokens // tile,),
+        in_specs=[
+            tiled(tile, width),
+            full(weight.shape),
+            full(lup.shape),
+            full((1, width)),
+            full((1, RANK)),
+            tiled(tile, 128),
+            tiled(tile, 128),
+        ],
+        out_specs=[tiled(tile, s[1]) for s, _ in outs],
+        out_shape=[jax.ShapeDtypeStruct(s, d) for s, d in outs],
+        cost_estimate=estimate(2 * tokens * width * (weight.shape[1] + 64), 5 * tokens * width),
+    )(x_all, weight, lup, gain[None], gain_lat[None], cosine, sine)
+
+
+def attend_kernel(scale, query_ref, key_ref, value_ref, row_ref, col_ref, probs_ref, out_ref):
+    length = probs_ref.shape[1]
+    tile = 256
+    query = query_ref[...].reshape(length, -1)
+    key = key_ref[...].reshape(length, -1)
+    value = value_ref[...].reshape(length, -1)
+    for at in range(0, length, tile):
+        seen = at + tile
+        scores = matmul(query[at:seen], key[:seen], COLS_COLS) * scale
+        row = at + lax.broadcasted_iota(jnp.int32, scores.shape, 0)
+        col = lax.broadcasted_iota(jnp.int32, scores.shape, 1)
+        keep = (col <= row) & (row_ref[0, :, :seen] == col_ref[0, at:seen, :])
+        scores = jnp.where(keep, scores, masked_score)
+        weights = jnp.exp(scores - jnp.max(scores, axis=-1, keepdims=True))
+        probs = (weights / jnp.sum(weights, axis=-1, keepdims=True)).astype(bf16)
+        probs_ref[0, at:seen, :seen] = probs
+        if seen < length:
+            probs_ref[0, at:seen, seen:] = jnp.zeros((tile, length - seen), bf16)
+        out_ref[0, at:seen, :] = matmul(probs, value[:seen], COLS_ROWS).astype(bf16)
+
+
+def of_sequence(groups, span, columns):
+    return pl.BlockSpec((groups, 1, span, columns), lambda s: (0, s, 0, 0))
+
+
+def attend(query, key, value, segments, scale, groups, seqs, span):
+    length = groups * span
+    view = lambda v: v.reshape(groups, seqs, span, -1)
+    return pl.pallas_call(
+        functools.partial(attend_kernel, scale),
+        name="attend",
+        grid=(seqs,),
+        in_specs=[
+            of_sequence(groups, span, HD + 128),
+            of_sequence(groups, span, HD + 128),
+            of_sequence(groups, span, VD),
+            pl.BlockSpec((1, 1, length), lambda s: (s, 0, 0)),
+            pl.BlockSpec((1, length, 1), lambda s: (s, 0, 0)),
+        ],
+        out_specs=[
+            pl.BlockSpec((1, length, length), lambda s: (s, 0, 0)),
+            pl.BlockSpec((1, length, VD), lambda s: (s, 0, 0)),
+        ],
+        out_shape=[
+            jax.ShapeDtypeStruct((seqs, length, length), bf16),
+            jax.ShapeDtypeStruct((seqs, length, VD), bf16),
+        ],
+        cost_estimate=estimate(seqs * length * length * 500, seqs * length * length * 4),
+    )(view(query), view(key), view(value), segments[:, None, :], segments[:, :, None])
+
+
+def attend_back_kernel(
+    scale, probs_ref, grad_ref, out_ref, query_ref, key_ref, value_ref, dq_ref, dkv_ref, acc_ref
+):
+    length = probs_ref.shape[1]
+    tile = 256
+    _, _, span, _ = query_ref.shape
+    per = tile // span
+    query = query_ref[...].reshape(length, -1)
+    key = key_ref[...].reshape(length, -1)
+    value = value_ref[...].reshape(length, -1)
+    wide = query.shape[1]
+    for at in reversed(range(0, length, tile)):
+        seen = at + tile
+        grad = grad_ref[0, at:seen, :]
+        spread = jnp.sum(
+            grad.astype(f32) * out_ref[0, at:seen, :].astype(f32), axis=-1, keepdims=True
+        )
+        probs = probs_ref[0, at:seen, :seen]
+        back = matmul(grad, value[:seen], COLS_COLS) - spread
+        score_grad = (probs.astype(f32) * back * scale).astype(bf16)
+        dq = matmul(score_grad, key[:seen], COLS_ROWS)
+        dq_ref[at // span : seen // span, 0] = dq.reshape(per, span, wide)
+        dk = matmul(score_grad, query[at:seen], ROWS_ROWS)
+        dv = matmul(probs, grad, ROWS_ROWS)
+        if seen == length:
+            acc_ref[:, :wide] = dk
+            acc_ref[:, wide:] = dv
+        else:
+            acc_ref[:seen, :wide] += dk
+            acc_ref[:seen, wide:] += dv
+    dkv_ref[...] = acc_ref[...].reshape(dkv_ref.shape)
+
+
+def attend_back(probs, grad, out, query, key, value, scale, groups, span):
+    seqs, length, _ = probs.shape
+    wide = HD + 128
+    view = lambda v: v.reshape(groups, seqs, span, -1)
+    by_seq = lambda n: pl.BlockSpec((1, length, n), lambda s: (s, 0, 0))
+    dq, dkv = pl.pallas_call(
+        functools.partial(attend_back_kernel, scale),
+        name="attend_back",
+        grid=(seqs,),
+        in_specs=[
+            by_seq(length),
+            by_seq(VD),
+            by_seq(VD),
+            of_sequence(groups, span, wide),
+            of_sequence(groups, span, wide),
+            of_sequence(groups, span, VD),
+        ],
+        out_specs=[of_sequence(groups, span, wide), of_sequence(groups, span, wide + VD)],
+        out_shape=[
+            jax.ShapeDtypeStruct((groups, seqs, span, wide), f32),
+            jax.ShapeDtypeStruct((groups, seqs, span, wide + VD), f32),
+        ],
+        scratch_shapes=[pltpu.VMEM((length, wide + VD), f32)],
+        cost_estimate=estimate(seqs * length * length * 1000, seqs * length * length * 4),
+    )(probs, grad, out, view(query), view(key), view(value))
+    return dq.reshape(-1, wide), dkv.reshape(-1, wide + VD)
+
+
+def project_back_kernel(
+    dq_ref, dkv_ref, weight_ref, lup_ref, gain_lat_ref, cos_ref, sin_ref,
+    latent_ref, normed_ref, factor_ref, joint_ref, h_ref, lup_grad_ref, gain_grad_ref,
+):
+    dq = dq_ref[...]
+    dkv = dkv_ref[...]
+    lane = lax.broadcasted_iota(jnp.int32, (dq.shape[0], 128), 1)
+    rope = jnp.where(lane < RD, dkv[:, HD : HD + 128], pltpu.roll(dq[:, HD:], 64, 1))
+    rope = turn(rope, cos_ref[...], -sin_ref[...])
+    expanded = jnp.concatenate([dkv[:, :HD], dkv[:, HD + 128 :]], axis=1).astype(bf16)
+    latent_grad = matmul(expanded, lup_ref[...], COLS_COLS)
+    normed = normed_ref[...]
+
+    @pl.when(pl.program_id(0) == 0)
+    def _():
+        lup_grad_ref[...] = jnp.zeros_like(lup_grad_ref)
+        gain_grad_ref[...] = jnp.zeros_like(gain_grad_ref)
+
+    lup_grad_ref[...] += matmul(latent_ref[...], expanded, ROWS_ROWS)
+    gain_grad_ref[...] += jnp.sum(latent_grad * normed, axis=0, keepdims=True)
+    scaled = latent_grad * gain_lat_ref[...]
+    down = factor_ref[...] * (
+        scaled - normed * jnp.mean(scaled * normed, axis=-1, keepdims=True)
+    )
+    joint = jnp.concatenate([down, rope, dq[:, :HD]], axis=1).astype(bf16)
+    joint_ref[...] = joint
+    h_ref[...] = matmul(joint, weight_ref[...], COLS_COLS).astype(bf16)
+
+
+def project_back(dq, dkv, weight, lup, gain_lat, cosine, sine, latent, normed, factor):
+    tokens = dq.shape[0]
+    width, joint = weight.shape
+    tile = 256
+    return pl.pallas_call(
+        project_back_kernel,
+        name="project_back",
+        grid=(tokens // tile,),
+        in_specs=[
+            tiled(tile, dq.shape[1]),
+            tiled(tile, dkv.shape[1]),
+            full(weight.shape),
+            full(lup.shape),
+            full((1, RANK)),
+            tiled(tile, 128),
+            tiled(tile, 128),
+            tiled(tile, RANK),
+            tiled(tile, RANK),
+            tiled(tile, 1),
+        ],
+        out_specs=[
+            tiled(tile, joint),
+            tiled(tile, width),
+            pl.BlockSpec(lup.shape, lambda i: (0, 0)),
+            pl.BlockSpec((1, RANK), lambda i: (0, 0)),
+        ],
+        out_shape=[
+            jax.ShapeDtypeStruct((tokens, joint), bf16),
+            jax.ShapeDtypeStruct((tokens, width), bf16),
+            jax.ShapeDtypeStruct(lup.shape, f32),
+            jax.ShapeDtypeStruct((1, RANK), f32),
+        ],
+        cost_estimate=estimate(2 * tokens * width * joint * 1.2, 6 * tokens * width),
+    )(dq, dkv, weight, lup, gain_lat[None], cosine, sine, latent, normed, factor)
 
 
 def per_device(
@@ -540,7 +811,6 @@
     replicas = lax.axis_size(DP)
     place = lax.axis_index(EXPERT)
     seqs, span, width = inputs.shape
-    length = span * groups
     own = seqs * span
     tokens = own * groups
     experts = groups
@@ -551,11 +821,6 @@
     hidden_own = part * replicas
     QD = HD + RD
 
-    def by_sequence(value):
-        return value.reshape(groups, seqs, span, -1).transpose(1, 0, 2, 3).reshape(
-            seqs, length, -1
-        )
-
     def by_owner(value):
         return value.astype(bf16).reshape(groups, own, -1)
 
@@ -632,30 +897,14 @@
     positions = jnp.broadcast_to(
         at_block + jnp.arange(span, dtype=jnp.int32), (groups, seqs, span)
     ).reshape(tokens)
-    tables = lax.optimization_barrier(angle_tables(positions, RD))
-    normed_one, _ = norm_parts(x_all.astype(f32))
-    h_one = (normed_one * gain_attn).astype(bf16)
-    query_raw = product(h_one, wq)
-    query = jnp.concatenate(
-        [query_raw[:, :HD], rotate(query_raw[:, HD:], tables)], axis=-1
-    ).astype(bf16)
-    down = product(h_one, ldown_all)
-    normed_lat, factor_lat = norm_parts(down[:, :RANK])
-    latent = (normed_lat * gain_lat).astype(bf16)
-    key_rope = rotate(down[:, RANK:], tables).astype(bf16)
-    expanded = product(latent, lup).astype(bf16)
-    query_s = by_sequence(query)
-    key_s = by_sequence(jnp.concatenate([expanded[:, :HD], key_rope], axis=-1))
-    value_s = by_sequence(expanded[:, HD:])
-    at = jnp.arange(length, dtype=jnp.int32)
-    mask = (at[None, None, :] <= at[None, :, None]) & (
-        segments[:, None, :] == segments[:, :, None]
-    )
-    scores = jnp.where(mask, einsum("sqd,skd->sqk", query_s, key_s) * scale, masked_score)
-    top_score = jnp.max(scores, axis=-1, keepdims=True)
-    weights_exp = jnp.exp(scores - top_score)
-    probs_attn = (weights_exp / jnp.sum(weights_exp, axis=-1, keepdims=True)).astype(bf16)
-    heads_s = einsum("sqk,skd->sqd", probs_attn, value_s).astype(bf16)
+    cosine, sine = angle_tables(positions, RD)
+    cosine = jnp.concatenate([cosine] * 4, axis=1)
+    sine = jnp.concatenate([-sine, sine] * 2, axis=1)
+    joint_weight = jnp.concatenate([ldown_all, wq[:, HD:], wq[:, :HD]], axis=1)
+    h_one, query, key, value, latent, normed_lat, factor_lat = project(
+        x_all, joint_weight, lup, gain_attn, gain_lat, cosine, sine
+    )
+    probs_attn, heads_s = attend(query, key, value, segments, scale, groups, seqs, span)
     heads_own = heads_to_tokens(heads_s, span, 3).reshape(own, HEADS * VD)
 
     x_second = x_low.astype(f32) + right_product(heads_own, out_t)
@@ -683,9 +932,6 @@
         return einsum("cst,ctd->csd", select, values.reshape(chunks, chunk, -1)).astype(bf16).reshape(
             chunks * slots, -1
         )
-
-    def to_tokens(values):
-        return einsum("cst,csd->ctd", select, values.reshape(chunks, slots, -1)).reshape(tokens, -1)
 
     pre = product(h_two, gate_up_router)
     shared_a = pre[:, :hidden_own]
@@ -702,8 +948,9 @@
     up_pre = product(expert_in, up_w)
     expert_hidden = (jax.nn.silu(gate_pre) * up_pre).astype(bf16)
     expert_out = product(expert_hidden, down_w).astype(bf16).astype(f32)
-    partial = product(shared_hidden, sdown) + to_tokens((slot_prob * expert_out).astype(bf16))
-    partial = partial.astype(bf16)
+    partial = combine(
+        select, (slot_prob * expert_out).astype(bf16), shared_hidden, sdown, COLS_ROWS
+    )
     result = x_second + scatter_rows(partial, EXPERT).astype(f32)
     result = result.astype(bf16).reshape(seqs, span, width)
 
@@ -723,7 +970,7 @@
     expert_b_grad = (expert_hidden_grad * jax.nn.silu(gate_pre)).astype(bf16)
     in_grad = right_product(expert_a_grad, gate_w) + right_product(expert_b_grad, up_w)
     in_grad = in_grad.astype(bf16)
-    h_two_partial = right_product(pre_grad, gate_up_router) + to_tokens(in_grad)
+    h_two_partial = combine(select, in_grad, pre_grad, gate_up_router, COLS_COLS)
     routed_down_grad = dp_scatter_product(expert_hidden, slot_grad)
     routed_gate_grad = dp_scatter_product(expert_in, expert_a_grad)
     routed_up_grad = dp_scatter_product(expert_in, expert_b_grad)
@@ -752,30 +999,13 @@
 
     sgate_owned = owned_columns(gate_up_owned[:, :, :hidden_own])
     sup_owned = owned_columns(gate_up_owned[:, :, hidden_own:])
-    probs_grad = einsum("sqd,skd->sqk", grad_s, value_s)
-    spread = jnp.sum(grad_s.astype(f32) * heads_s.astype(f32), axis=-1, keepdims=True)
-    score_grad = (probs_attn.astype(f32) * (probs_grad - spread) * scale).astype(bf16)
-    value_grad = einsum("sqk,sqd->skd", probs_attn, grad_s)
-    key_grad = einsum("sqk,sqd->skd", score_grad, query_s)
-    query_grad = by_block(einsum("sqk,skd->sqd", score_grad, key_s))
-    expanded_grad = by_block(
-        jnp.concatenate([key_grad[..., :HD], value_grad], axis=-1).astype(bf16)
-    )
-    rope_grad = by_block(key_grad[..., HD:])
-    lup_grad = left_product(latent, expanded_grad)
-    latent_grad = right_product(expanded_grad, lup)
-    glat_grad = jnp.sum(latent_grad * normed_lat, axis=0)
-    joint_grad = jnp.concatenate(
-        [
-            norm_back(latent_grad * gain_lat, normed_lat, factor_lat),
-            unrotate(rope_grad, tables),
-            unrotate(query_grad[:, HD:], tables),
-            query_grad[:, :HD],
-        ],
-        axis=-1,
-    ).astype(bf16)
-    joint_weight = jnp.concatenate([ldown_all, wq[:, HD:], wq[:, :HD]], axis=1)
-    h_one_partial = right_product(joint_grad, joint_weight)
+    query_grad, pair_grad = attend_back(
+        probs_attn, grad_s, heads_s, query, key, value, scale, groups, span
+    )
+    joint_grad, h_one_partial, lup_grad, glat_grad = project_back(
+        query_grad, pair_grad, joint_weight, lup, gain_lat, cosine, sine,
+        latent, normed_lat, factor_lat,
+    )
     joint_weight_grad = left_product(h_one, joint_grad)
     gattn_grad = jnp.sum(joint_weight_grad * joint_weight.astype(f32), axis=1) / gain_attn
     out_grad = left_product(low_all, by_block(heads_s))

time: 975 us -> 1020 us (1.046)
  matrix products: 259 us -> 174 us
  waiting for transfers between devices: 76.1 us -> 161 us
  Pallas kernels: 389 us -> 458 us
  local copies, waits for them, and re-layouts: 99.6 us -> 75.3 us
    ppermute x15, waiting for transfers between devices: 67 us -> 152 us  [dp_swap(): return lax.ppermute(value, DP, [(0, 1), (1, 0)])]
    pallas_call x0 -> x6, Pallas kernels: none -> 73.9 us  [the longest x2 23.9 us: combine(): pl.pallas_call(functools.partial(combine_kernel, dims), grid=(chunks, per...]
    dot_general x10 -> x3, matrix products: 42.9 us -> 13 us  [einsum(): return jnp.einsum(spec, left, right, preferred_element_type=f32)]
    dot_general x8 -> x5, matrix products: 75.8 us -> 48.2 us  [right_product(): lax.dot_general(left, right, (((1,), (1,)), ((), ())), preferred_element_...]
    dot_general x9 -> x5, matrix products: 59.1 us -> 37.3 us  [product(): return jnp.dot(left, right, preferred_element_type=f32)]
    concatenate x1 -> x4, other arithmetic: 0.33 us -> 20.8 us  [the longest x1 13.2 us: per_device(): joint_weight = jnp.concatenate([ldown_all, wq[:, HD:], wq[:, :HD]], axis=1)]
    convert_element_type x2 -> x0, other arithmetic: 13.4 us -> none  [the longest x1 8.73 us: per_device(): h_one = (normed_one * gain_attn).astype(bf16)]
    unnamed x224 -> x106, local copies, waits for them, and re-layouts: 21.1 us -> 9.18 us
  transfers between devices with their start and end apart: 22 -> 22, of which waited for: 5 -> 5; matrix products, arithmetic and copies ran while one was open for 33% -> 22% of each run, Pallas kernels for 28% -> 33%
where the time goes in v4:
time: 1020 us; the launch traced here: 1010 us
  Pallas kernels  458 us (45%)
  matrix products  174 us (17%)
  waiting for transfers between devices  161 us (16%)
  other arithmetic  87.1 us (9%)
  local copies, waits for them, and re-layouts  75.3 us (7%)
  starting transfers between devices  38.1 us (4%)
  between operations  15.3 us (2%)
    pallas_call x2, Pallas kernels, ring_gather(): pl.pallas_call(functools.partial(gather_kernel, n, m), out_shape=[jax.Sha...  193 us
    pallas_call x2, Pallas kernels, ring_scatter(): pl.pallas_call(functools.partial(scatter_kernel, n), out_shape=[jax.Shape...  157 us
    ppermute x15, waiting for transfers between devices, dp_swap(): return lax.ppermute(value, DP, [(0, 1), (1, 0)])  152 us
    dot_general x10, matrix products, left_product(): lax.dot_general(left, right, (((0,), (0,)), ((), ())), preferred_element_...  75.3 us
    dot_general x5, matrix products, right_product(): lax.dot_general(left, right, (((1,), (1,)), ((), ())), preferred_element_...  48.2 us
    dot_general x5, matrix products, product(): return jnp.dot(left, right, preferred_element_type=f32)  37.3 us
    pallas_call x2, Pallas kernels, swap_call(): pl.pallas_call(functools.partial(swap_kernel, source, target), out_shape=...  33.2 us
    pallas_call x2, Pallas kernels, combine(): pl.pallas_call(functools.partial(combine_kernel, dims), grid=(chunks, per...  23.9 us
  transfers between devices with their start and end apart: 22, of which 5 were waited for; matrix products, arithmetic and copies ran while one was open for 22% of the time, Pallas kernels for 33%

profile of v4, /device:TPU:0, one launch (start us, length us, event | category | flops | bytes accessed | tf_op | source)
XLA Modules:
  0.0 1008.2 jit_solution(10051802128884258793)
XLA Ops:
  22.3 6.4 all-to-all-start
  44.8 133.4 %shard_map.306 = (bf16[16,128,640]{2,1,0:T(8,128)(2,1)}, bf16[16,128,2048]{2,1,0:T(8,128)(2,1)}, bf16[16,64,192]{2,1,0:T(8,128)(2,1)}, bf16[16,32,256]{2,1,0:T(8,128)(2,1)}) custom-call(bf16[128,640]{1,0:T(8,128)(2,1)} %pad_maximum_fusion.23.refs_0_, bf16[128,2048]{1,0:T(8,128)(2,1)} %bitcast.161, bf16[16,64,192]{2,1,0:T(8,128)(2,1)} %bitcast.181, ...), custom_call_target="tpu_custom_call" | custom-call | bytes 175636480 | tf_op jit(solution)/shard_map/pallas_call | solution.py:275
  191.7 52.8 %collective-permute-done.2 = bf16[256,256]{1,0:T(8,128)(2,1)S(1)} collective-permute-done((bf16[256,256]{1,0:T(8,128)(2,1)S(1)}, bf16[256,256]{1,0:T(8,128)(2,1)S(1)}, u32[]{:S(2)}, u32[]{:S(2)}) %collective-permute-start.2) | collective-permute-done | bytes 131104 | tf_op jit(solution)/shard_map/ppermute | solution.py:68
  248.8 9.1 collective-permute-done.1
  258.1 13.2 %fusion.11.weight_ref = bf16[2048,768]{1,0:T(8,128)(2,1)} fusion(bf16[1024,192]{1,0:T(8,128)(2,1)S(1)} %get-tuple-element.179, bf16[1024,192]{1,0:T(8,128)(2,1)S(1)} %get-tuple-element.178, bf16[2048,64]{1,0:T(8,128)(2,1)S(1)} %fusion.35, bf16[2048,576]{1,0:T(8,128)(2,1)} %bitcast.158), kind=kLoop, calls=%fused_computation.33 | loop fusion | flops 12582912 | bytes 6553600 | tf_op jit(solution)/shard_map/concatenate | solution.py:903
  273.1 17.4 %project.1 = (bf16[2048,2048]{1,0:T(8,128)(2,1)}, bf16[2048,256]{1,0:T(8,128)(2,1)}, bf16[2048,256]{1,0:T(8,128)(2,1)}, bf16[2048,128]{1,0:T(8,128)(2,1)}, bf16[...) custom-call(bf16[2048,2048]{1,0:T(8,128)(2,1)} %bitcast.214, bf16[2048,768]{1,0:T(8,128)(2,1)} %fusion.11.weight_ref, ...), custom_call_target="tpu_custom_call" | custom-call | flops 6979321856 | bytes 20971520 | tf_op jit(solution)/shard_map/project/pallas_call | solution.py:593
  290.5 7.7 attend.1
  298.2 15.2 %shard_map.307 = bf16[2,64,2048]{2,1,0:T(8,128)(2,1)} custom-call(bf16[2,1024,128]{2,1,0:T(8,128)(2,1)} %get-tuple-element.45.x_ref.out_ref), custom_call_target="tpu_custom_call" | custom-call | bytes 33554432 | tf_op jit(solution)/shard_map/pallas_call | solution.py:461
  316.6 4.8 broadcast_select_fusion.1
  321.4 4.9 broadcast_select_fusion.3
  326.4 4.9 broadcast_select_fusion.5
  331.3 7.2 convolution_convert_fusion.2
  338.5 6.4 multiply_reduce_fusion.5
  345.9 59.8 %shard_map.308 = bf16[16,128,2048]{2,1,0:T(8,128)(2,1)} custom-call(bf16[128,2048]{1,0:T(8,128)(2,1)} %multiply_convert_fusion.7.refs_0_), custom_call_target="tpu_custom_call" | custom-call | bytes 125829120 | tf_op jit(solution)/shard_map/pallas_call | solution.py:275
  405.7 7.8 fusion.63
  416.4 5.5 convolution_convert_fusion.3
  422.0 7.3 fusion.9
  429.3 9.6 multiply_convert_fusion.2
  439.0 7.2 fusion.2
  450.1 7.6 fusion.1
  457.7 15.9 %multiply_convert_fusion.1 = (bf16[864,1408]{1,0:T(8,128)(2,1)}, bf16[864,1408]{1,0:T(8,128)(2,1)}) fusion(f32[864,1408]{1,0:T(8,128)} %fusion.9, f32[864,1408]{1,0:T(8,128)} %get-tuple-element.200, bf16[864,2048]{1,0:T(8,128)(2,1)S(1)} %get-tuple-element.195, bf16[704,2048]{1,0:T(8,128)(2,1)} %get-tuple-element.166, bf16[704,2048]{1,0:T(8,128)(2,1)} %get-tuple-element.165), kind=kOutput, calls=%fused_computation.15 | convolution fusion | flops 5010182144 | bytes 23904256 | tf_op jit(solution)/shard_map/dot_general | solution.py:39
  473.7 10.8 %fusion.6 = f32[864,2048]{1,0:T(8,128)} fusion(bf16[864,1408]{1,0:T(8,128)(2,1)} %get-tuple-element.164, bf16[1024,1408]{1,0:T(8,128)(2,1)} %get-tuple-element.170, bf16[1024,1408]{1,0:T(8,128)(2,1)} %get-tuple-element.169), kind=kOutput, calls=%fused_computation.24 | convolution fusion | flops 4994367488 | bytes 15278080 | tf_op jit(solution)/shard_map/dot_general | solution.py:39
  484.5 10.8 %add_convert_fusion = bf16[864,2048]{1,0:T(8,128)(2,1)} fusion(f32[864,2048]{1,0:T(8,128)} %fusion.6, bf16[864,1408]{1,0:T(8,128)(2,1)} %get-tuple-element.163, bf16[1024,1408]{1,0:T(8,128)(2,1)} %get-tuple-element.168, bf16[1024,1408]{1,0:T(8,128)(2,1)S(1)} %copy-done.28), kind=kOutput, calls=%fused_computation.6 | convolution fusion | flops 4997906432 | bytes 18817024 | tf_op jit(solution)/shard_map/dot_general | solution.py:39
  501.6 12.7 %shard_map.310 = bf16[2048,2048]{1,0:T(8,128)(2,1)} custom-call(bf16[4,216,512]{2,1,0:T(8,128)(2,1)} %copy-done.2, bf16[4,216,2048]{2,1,0:T(8,128)(2,1)} %bitcast.217, bf16[2048,368]{1,0:T(8,128)(2,1)} %pad_maximum_fusion.16.left_ref, bf16[2048,368]{1,0:T(8,128)(2,1)} %pad_maximum_fusion.15.right_ref), custom_call_target="tpu_custom_call" | custom-call | flops 4898947072 | bytes 16777216 | tf_op jit(solution)/shard_map/pallas_call | solution.py:532
  514.3 57.0 %shard_map.311 = f32[128,2048]{1,0:T(8,128)} custom-call(bf16[16,128,2048]{2,1,0:T(8,128)(2,1)} %bitcast.164), custom_call_target="tpu_custom_call" | custom-call | bytes 125829120 | tf_op jit(solution)/shard_map/pallas_call | solution.py:423
  577.4 6.6 fusion.65
  586.0 5.4 convolution_convert_fusion.5
  591.5 18.0 %shard_map.312.grad_ref = bf16[2,1024,128]{2,1,0:T(8,128)(2,1)} custom-call(bf16[2,64,2048]{2,1,0:T(8,128)(2,1)} %bitcast.183), custom_call_target="tpu_custom_call" | custom-call | bytes 33554432 | tf_op jit(solution)/shard_map/pallas_call | solution.py:461
  609.5 7.1 attend_back.1
  616.7 11.2 %shard_map.309 = bf16[2048,2048]{1,0:T(8,128)(2,1)} custom-call(bf16[4,216,512]{2,1,0:T(8,128)(2,1)} %copy-done.2, bf16[4,216,2048]{2,1,0:T(8,128)(2,1)} %bitcast.159, bf16[2048,176]{1,0:T(8,128)(2,1)} %get-tuple-element.173.left_ref, bf16[176,2048]{1,0:T(8,128)(2,1)} %pad_maximum_fusion.20.right_ref), custom_call_target="tpu_custom_call" | custom-call | flops 3288334336 | bytes 16777216 | tf_op jit(solution)/shard_map/pallas_call | solution.py:532
  627.8 17.9 %project_back.1 = (bf16[2048,768]{1,0:T(8,128)(2,1)}, bf16[2048,2048]{1,0:T(8,128)(2,1)}, f32[512,256]{1,0:T(8,128)}, f32[1,512]{1,0:T(1,128)}) custom-call(f32[2048,256]{1,0:T(8,128)} %bitcast.216, f32[2048,384]{1,0:T(8,128)} %bitcast.215, bf16[2048,768]{1,0:T(8,128)(2,1)} %fusion.11.weight_ref, bf16[512,256]{1,0:T(8,128)(2,1)} %pad_maximum_fusion.22.lup_ref, ...), custom_call_target="tpu_custom_call" | custom-call | flops 7730940928 | bytes 25165824 | tf_op jit(solution)/shard_map/project_back/pallas_call | solution.py:757
  645.7 10.4 %fusion.64 = f32[2048,768]{0,1:T(8,128)S(1)} fusion(bf16[2048,2048]{1,0:T(8,128)(2,1)} %get-tuple-element.46, bf16[2048,768]{1,0:T(8,128)(2,1)} %get-tuple-element.53), kind=kOutput, calls=%fused_computation.186 | convolution fusion | flops 6442450944 | bytes 17825792 | tf_op jit(solution)/shard_map/dot_general | solution.py:35
  660.6 7.1 copy.217
  667.7 5.9 fusion.67
  685.8 4.5 multiply_reduce_fusion
  694.5 7.8 convolution_convert_fusion
  704.0 100.2 %shard_map.313 = (f32[2,64,576]{2,1,0:T(8,128)}, f32[2,64,128]{2,1,0:T(8,128)}, f32[128,2048]{1,0:T(8,128)}) custom-call(bf16[2,16,64,576]{3,2,1,0:T(8,128)(2,1)} %bitcast.163, bf16[2,16,64,128]{3,2,1,0:T(8,128)(2,1)} %bitcast.182, bf16[16,128,2048]{2,1,0:T(8,128)(2,1)} %bitcast.165), custom_call_target="tpu_custom_call" | custom-call | bytes 169082880 | tf_op jit(solution)/shard_map/pallas_call | solution.py:423
  806.9 8.0 convolution_convert_fusion.1
  814.8 5.2 convolution_convert_fusion.4
  823.7 4.8 collective-permute-done.9
  835.3 6.4 all-to-all-start.2
  843.8 4.9 fusion.66
  852.2 8.1 all-to-all-done.2
  874.3 9.7 add_bitcast_fusion.1
  884.1 84.9 %collective-permute-done.8 = bf16[1024,384]{0,1:T(8,128)(2,1)} collective-permute-done((bf16[1024,384]{0,1:T(8,128)(2,1)S(1)}, bf16[1024,384]{0,1:T(8,128)(2,1)}, u32[]{:S(2)}, u32[]{:S(2)}) %collective-permute-start.8) | collective-permute-done | bytes 786464 | tf_op jit(solution)/shard_map/ppermute | solution.py:68
  971.5 5.8 all-to-all-start.1
  977.3 9.7 add_bitcast_fusion.2
  987.1 7.1 add_bitcast_fusion
  (279 shorter events, 140.9 us)
Async XLA Ops:
  7.2 11.7 %copy-start.40 = (bf16[64,2816]{1,0:T(8,128)(2,1)S(1)}, bf16[64,2816]{1,0:T(8,128)(2,1)}, u32[]{:S(2)}) copy-start(bf16[64,2816]{1,0:T(8,128)(2,1)} %param.32) | copy-start | bytes 1081348
  7.2 324.1 %all-gather.6.cloned.1.call-start = ((), (), s32[]{:S(2)}) async-start(), calls=%async_computation.6 | async-start | bytes 8912896 | tf_op jit(solution)/shard_map/all_gather | solution.py:109
  7.9 330.6 %all-gather.4.cloned.1.call-start = ((), (), s32[]{:S(2)}) async-start(), calls=%async_computation.4 | async-start | bytes 8650752 | tf_op jit(solution)/shard_map/all_gather | solution.py:109
  12.8 31.4 %collective-permute-start = (bf16[64,640]{1,0:T(8,128)(2,1)S(1)}, bf16[64,640]{1,0:T(8,128)(2,1)S(1)}, u32[]{:S(2)}, u32[]{:S(2)}) collective-permute-start(bf16[64,640]{1,0:T(8,128)(2,1)S(1)} %concatenate.57), channel_id=1, source_target_pairs={{0,16},{16,0},{1,17},{17,1},{2,18},{18,2},{3,19},{19,3},{4,20},{20... | collective-permute-start | bytes 245768 | tf_op jit(solution)/shard_map/ppermute | solution.py:68
  15.8 231.0 %collective-permute-start.7 = (bf16[88,2048]{1,0:T(8,128)(2,1)}, bf16[88,2048]{1,0:T(8,128)(2,1)}, u32[]{:S(2)}, u32[]{:S(2)}) collective-permute-start(bf16[88,2048]{1,0:T(8,128)(2,1)} %param.33), channel_id=1, source_target_pairs={{0,16},{16,0},{1,17},{17,1},{2,18},{18,2},{3,19},{19,3},{4,20},{20... | collective-permute-start | bytes 1081352 | tf_op jit(solution)/shard_map/ppermute | solution.py:68
  18.9 13.6 %copy-start.45 = (s32[2,64,6]{1,0,2:T(2,128)S(1)}, s32[2,64,6]{1,0,2:T(2,128)}, u32[]{:S(2)}) copy-start(s32[2,64,6]{1,0,2:T(2,128)} %param.21) | copy-start | bytes 9220
  18.9 13.6 %copy-start.47 = (s32[2,64]{1,0:T(2,128)S(1)}, s32[2,64]{1,0:T(2,128)}, u32[]{:S(2)}) copy-start(s32[2,64]{1,0:T(2,128)} %param.22) | copy-start | bytes 1540
  19.0 13.9 %copy-start.44 = (s32[2,1024]{1,0:T(2,128)S(1)}, s32[2,1024]{1,0:T(2,128)}, u32[]{:S(2)}) copy-start(s32[2,1024]{1,0:T(2,128)} %param.20) | copy-start | bytes 24580
  19.0 14.5 %copy-start.41 = (bf16[16,4096]{1,0:T(8,128)(2,1)S(1)}, bf16[16,4096]{1,0:T(8,128)(2,1)}, u32[]{:S(2)}) copy-start(bf16[16,4096]{1,0:T(8,128)(2,1)} %param.26) | copy-start | bytes 393220
  20.3 13.3 %copy-start.39 = (bf16[64,3072]{1,0:T(8,128)(2,1)S(1)}, bf16[64,3072]{1,0:T(8,128)(2,1)}, u32[]{:S(2)}) copy-start(bf16[64,3072]{1,0:T(8,128)(2,1)} %param.24) | copy-start | bytes 1179652
  22.3 249.0 %all-to-all-start = ((bf16[16,64,352]{2,1,0:T(8,128)(2,1)}), bf16[16,64,352]{2,1,0:T(8,128)(2,1)S(1)}, u32[]{:S(2)}, u32[]{:S(2)}) async-start(bf16[16,64,352]{2,1,0:T(8,128)(2,1)} %pad_maximum_fusion.19), calls=%async_computation | async-start | bytes 1572864 | tf_op jit(solution)/shard_map/all_to_all | solution.py:105
  28.7 815.0 %all-gather.8.cloned.1.call-start = ((), (), s32[]{:S(2)}) async-start(), calls=%async_computation.7 | async-start | bytes 8912896 | tf_op jit(solution)/shard_map/all_gather | solution.py:109
  28.8 287.8 %collective-permute-start.6 = (bf16[704,2048]{1,0:T(8,128)(2,1)}, bf16[704,2048]{1,0:T(8,128)(2,1)}, u32[]{:S(2)}, u32[]{:S(2)}) collective-permute-start(bf16[704,2048]{1,0:T(8,128)(2,1)} %bitcast.177), channel_id=1, source_target_pairs={{0,16},{16,0},{1,17},{17,1},{2,18},{18,2},{3,19},{19,3},{4,20},{20... | collective-permute-start | bytes 8650760 | tf_op jit(solution)/shard_map/ppermute | solution.py:68
  30.4 291.1 %collective-permute-start.5 = (bf16[1024,1408]{1,0:T(8,128)(2,1)}, bf16[1024,1408]{1,0:T(8,128)(2,1)}, u32[]{:S(2)}, u32[]{:S(2)}) collective-permute-start(bf16[1024,1408]{1,0:T(8,128)(2,1)} %bitcast.178), channel_id=1, source_target_pairs={{0,16},{16,0},{1,17},{17,1},{2,18},{18,2},{3,19},{19,3},{4,20},{20... | collective-permute-start | bytes 8650760 | tf_op jit(solution)/shard_map/ppermute | solution.py:68
  30.9 295.5 %collective-permute-start.4 = (bf16[1024,1408]{1,0:T(8,128)(2,1)}, bf16[1024,1408]{1,0:T(8,128)(2,1)}, u32[]{:S(2)}, u32[]{:S(2)}) collective-permute-start(bf16[1024,1408]{1,0:T(8,128)(2,1)} %bitcast.179), channel_id=1, source_target_pairs={{0,16},{16,0},{1,17},{17,1},{2,18},{18,2},{3,19},{19,3},{4,20},{20... | collective-permute-start | bytes 8650760 | tf_op jit(solution)/shard_map/ppermute | solution.py:68
  181.9 62.7 %collective-permute-start.2 = (bf16[256,256]{1,0:T(8,128)(2,1)S(1)}, bf16[256,256]{1,0:T(8,128)(2,1)S(1)}, u32[]{:S(2)}, u32[]{:S(2)}) collective-permute-start(bf16[256,256]{1,0:T(8,128)(2,1)S(1)} %bitcast.195), channel_id=1, source_target_pairs={{0,16},{16,0},{1,17},{17,1},{2,18},{18,2},{3,19},{19,3},{4,20},{20... | collective-permute-start | bytes 393224 | tf_op jit(solution)/shard_map/ppermute | solution.py:68
  184.3 262.0 %copy-start.2 = (bf16[4,216,512]{2,1,0:T(8,128)(2,1)}, bf16[4,216,512]{2,1,0:T(8,128)(2,1)S(1)}, u32[]{:S(2)}) copy-start(bf16[4,216,512]{2,1,0:T(8,128)(2,1)S(1)} %and_convert_fusion.select_ref) | copy-start | bytes 2654212
  184.3 60.2 %copy-start.38 = (bf16[16,64,192]{2,1,0:T(8,128)(2,1)S(1)}, bf16[16,64,192]{2,1,0:T(8,128)(2,1)}, u32[]{:S(2)}) copy-start(bf16[16,64,192]{2,1,0:T(8,128)(2,1)} %get-tuple-element.40) | copy-start | bytes 1179652
  244.5 13.4 %collective-permute-start.1 = (bf16[1024,192]{1,0:T(8,128)(2,1)S(1)}, bf16[1024,192]{1,0:T(8,128)(2,1)S(1)}, u32[]{:S(2)}, u32[]{:S(2)}) collective-permute-start(bf16[1024,192]{1,0:T(8,128)(2,1)S(1)} %bitcast.194), channel_id=1, source_target_pairs={{0,16},{16,0},{1,17},{17,1},{2,18},{18,2},{3,19},{19,3},{4,20},{20... | collective-permute-start | bytes 1179656 | tf_op jit(solution)/shard_map/ppermute | solution.py:68
  271.6 41.8 %collective-permute-start.3 = (bf16[1024,352]{0,1:T(8,128)(2,1)S(1)}, bf16[1024,352]{0,1:T(8,128)(2,1)S(1)}, u32[]{:S(2)}, u32[]{:S(2)}) collective-permute-start(bf16[1024,352]{0,1:T(8,128)(2,1)S(1)} %copy.208), channel_id=1, source_target_pairs={{0,16},{16,0},{1,17},{17,1},{2,18},{18,2},{3,19},{19,3},{4,20},{20... | collective-permute-start | bytes 2162696 | tf_op jit(solution)/shard_map/ppermute | solution.py:68
  429.3 9.7 copy-start.5
  429.3 9.7 copy-start.23
  429.3 9.7 copy-start.24
  457.7 16.0 %copy-start.6 = (bf16[864,2048]{1,0:T(8,128)(2,1)}, bf16[864,2048]{1,0:T(8,128)(2,1)S(1)}, u32[]{:S(2)}) copy-start(bf16[864,2048]{1,0:T(8,128)(2,1)S(1)} %get-tuple-element.195) | copy-start | bytes 10616836
  457.7 37.7 %slice-start = ((s8[8388608]{0:T(1024)(128)(4,1)}), s8[4194304]{0:T(1024)(128)(4,1)S(1)}, s32[]{:S(2)}) async-start(s8[8388608]{0:T(1024)(128)(4,1)} %bitcast.151), calls=%async_computation.8 | async-start | bytes 8388608
  473.7 10.9 %copy-start.28 = (bf16[1024,1408]{1,0:T(8,128)(2,1)S(1)}, bf16[1024,1408]{1,0:T(8,128)(2,1)}, u32[]{:S(2)}) copy-start(bf16[1024,1408]{1,0:T(8,128)(2,1)} %get-tuple-element.167) | copy-start | bytes 8650756
  473.7 21.7 %slice-start.1 = ((s8[8388608]{0:T(1024)(128)(4,1)}), s8[4194304]{0:T(1024)(128)(4,1)S(1)}, s32[]{:S(2)}) async-start(s8[8388608]{0:T(1024)(128)(4,1)} %bitcast.151), calls=%async_computation.9 | async-start | bytes 8388608
  484.5 10.9 %copy-start.15 = (f32[2048,368]{1,0:T(8,128)S(1)}, f32[2048,368]{1,0:T(8,128)}, u32[]{:S(2)}) copy-start(f32[2048,368]{1,0:T(8,128)} %copy-done.14) | copy-start | bytes 9043972
  484.5 10.9 %copy-start.31 = (bf16[88,2048]{1,0:T(8,128)(2,1)S(1)}, bf16[88,2048]{1,0:T(8,128)(2,1)}, u32[]{:S(2)}) copy-start(bf16[88,2048]{1,0:T(8,128)(2,1)} %get-tuple-element.184) | copy-start | bytes 1081348
  484.5 10.9 %copy-start.32 = (bf16[88,2048]{1,0:T(8,128)(2,1)S(1)}, bf16[88,2048]{1,0:T(8,128)(2,1)}, u32[]{:S(2)}) copy-start(bf16[88,2048]{1,0:T(8,128)(2,1)} %get-tuple-element.185) | copy-start | bytes 1081348
  514.3 58.6 %copy-start.16 = (bf16[2,64,2048]{2,1,0:T(8,128)(2,1)S(1)}, bf16[2,64,2048]{2,1,0:T(8,128)(2,1)}, u32[]{:S(2)}) copy-start(bf16[2,64,2048]{2,1,0:T(8,128)(2,1)} %param.23) | copy-start | bytes 1572868
  575.3 418.8 %reduce-scatter.2.cloned.1.call-start = ((), (), s32[]{:S(2)}) async-start(), calls=%async_computation.5 | async-start | bytes 8912896 | tf_op jit(solution)/shard_map/reduce_scatter | solution.py:113
  667.7 12.8 %copy-start.46 = (f32[1,512]{1,0:T(1,128)S(1)}, f32[1,512]{1,0:T(1,128)}, u32[]{:S(2)}) copy-start(f32[1,512]{1,0:T(1,128)} %get-tuple-element.54) | copy-start | bytes 6148
  675.5 166.1 %collective-permute-start.11 = (bf16[88,2048]{1,0:T(8,128)(2,1)}, bf16[88,2048]{1,0:T(8,128)(2,1)}, u32[]{:S(2)}, u32[]{:S(2)}) collective-permute-start(bf16[88,2048]{1,0:T(8,128)(2,1)} %dynamic-slice_convert_fusion.2), channel_id=1, source_target_pairs={{0,16},{16,0},{1,17},{17,1},{2,18},{18,2},{3,19},{19,3},{4,20},{20... | collective-permute-start | bytes 1081352 | tf_op jit(solution)/shard_map/ppermute | solution.py:68
  679.6 152.7 %collective-permute-start.10 = (bf16[1024,352]{0,1:T(8,128)(2,1)}, bf16[1024,352]{0,1:T(8,128)(2,1)}, u32[]{:S(2)}, u32[]{:S(2)}) collective-permute-start(bf16[1024,352]{0,1:T(8,128)(2,1)} %dynamic-slice_convert_fusion.1), channel_id=1, source_target_pairs={{0,16},{16,0},{1,17},{17,1},{2,18},{18,2},{3,19},{19,3},{4,20},{20... | collective-permute-start | bytes 2162696 | tf_op jit(solution)/shard_map/ppermute | solution.py:68
  702.4 172.0 %collective-permute-start.13 = (bf16[1024,1408]{1,0:T(8,128)(2,1)}, bf16[1024,1408]{1,0:T(8,128)(2,1)}, u32[]{:S(2)}, u32[]{:S(2)}) collective-permute-start(bf16[1024,1408]{1,0:T(8,128)(2,1)} %convolution_convert_fusion), channel_id=1, source_target_pairs={{0,16},{16,0},{1,17},{17,1},{2,18},{18,2},{3,19},{19,3},{4,20},{20... | collective-permute-start | bytes 8650760 | tf_op jit(solution)/shard_map/ppermute | solution.py:68
  704.0 101.3 %copy-start.43 = (f32[2048]{0:T(1024)S(1)}, f32[2048]{0:T(1024)}, u32[]{:S(2)}) copy-start(f32[2048]{0:T(1024)} %get-tuple-element.160) | copy-start | bytes 24580
  806.9 8.0 copy-start.7
  806.9 8.0 copy-start.35
  820.9 7.6 collective-permute-start.9
  821.9 165.1 %collective-permute-start.14 = (bf16[704,2048]{1,0:T(8,128)(2,1)}, bf16[704,2048]{1,0:T(8,128)(2,1)}, u32[]{:S(2)}, u32[]{:S(2)}) collective-permute-start(bf16[704,2048]{1,0:T(8,128)(2,1)} %convolution_convert_fusion.4), channel_id=1, source_target_pairs={{0,16},{16,0},{1,17},{17,1},{2,18},{18,2},{3,19},{19,3},{4,20},{20... | collective-permute-start | bytes 8650760 | tf_op jit(solution)/shard_map/ppermute | solution.py:68
  828.5 148.8 %collective-permute-start.12 = (bf16[1024,1408]{1,0:T(8,128)(2,1)}, bf16[1024,1408]{1,0:T(8,128)(2,1)}, u32[]{:S(2)}, u32[]{:S(2)}) collective-permute-start(bf16[1024,1408]{1,0:T(8,128)(2,1)} %convolution_convert_fusion.1), channel_id=1, source_target_pairs={{0,16},{16,0},{1,17},{17,1},{2,18},{18,2},{3,19},{19,3},{4,20},{20... | collective-permute-start | bytes 8650760 | tf_op jit(solution)/shard_map/ppermute | solution.py:68
  835.3 25.0 %all-to-all-start.2 = ((bf16[16,64,352]{2,1,0:T(8,128)(2,1)}), bf16[16,64,352]{2,1,0:T(8,128)(2,1)S(1)}, u32[]{:S(2)}, u32[]{:S(2)}) async-start(bf16[16,64,352]{2,1,0:T(8,128)(2,1)} %bitcast.56), calls=%async_computation.3 | async-start | bytes 1572864 | tf_op jit(solution)/shard_map/all_to_all | solution.py:105
  850.7 118.3 %collective-permute-start.8 = (bf16[1024,384]{0,1:T(8,128)(2,1)S(1)}, bf16[1024,384]{0,1:T(8,128)(2,1)}, u32[]{:S(2)}, u32[]{:S(2)}) collective-permute-start(bf16[1024,384]{0,1:T(8,128)(2,1)S(1)} %dynamic-slice_convert_fusion), channel_id=1, source_target_pairs={{0,16},{16,0},{1,17},{17,1},{2,18},{18,2},{3,19},{19,3},{4,20},{20... | collective-permute-start | bytes 2359304 | tf_op jit(solution)/shard_map/ppermute | solution.py:68
  874.3 94.6 %copy-start.11 = (f32[2048,384]{0,1:T(8,128)S(1)}, f32[2048,384]{0,1:T(8,128)}, u32[]{:S(2)}) copy-start(f32[2048,384]{0,1:T(8,128)} %copy-done.10) | copy-start | bytes 9437188
  971.5 25.6 %all-to-all-start.1 = ((bf16[16,64,384]{2,1,0:T(8,128)(2,1)}), bf16[16,64,384]{2,1,0:T(8,128)(2,1)S(1)}, u32[]{:S(2)}, u32[]{:S(2)}) async-start(bf16[16,64,384]{2,1,0:T(8,128)(2,1)} %bitcast.49), calls=%async_computation.2 | async-start | bytes 1572864 | tf_op jit(solution)/shard_map/all_to_all | solution.py:105
  977.3 9.8 copy-start.8
  977.3 9.8 copy-start.36
  (26 other events, 125.4 us)
Sparse Core Ops, SparseCore 0:
  10.2 119.7 all-gather.5
  132.9 102.6 all-gather.3
  575.5 81.6 all-gather.7
  661.0 127.0 reduce-scatter.1

commit v5 on v4

--- a/solution.py
+++ b/solution.py
@@ -68,13 +68,16 @@
     return lax.ppermute(value, DP, [(0, 1), (1, 0)])
 
 
+def ordered(value, other):
+    first = lax.axis_index(DP) == 0
+    return jnp.concatenate(
+        [jnp.where(first, value, other), jnp.where(first, other, value)], axis=0
+    )
+
+
 def dp_gather(value):
     if lax.axis_size(DP) == 2:
-        other = dp_swap(value)
-        first = lax.axis_index(DP) == 0
-        return jnp.concatenate(
-            [jnp.where(first, value, other), jnp.where(first, other, value)], axis=0
-        )
+        return ordered(value, dp_swap(value))
     return lax.all_gather(value, DP, axis=0, tiled=True)
 
 
@@ -144,29 +147,53 @@
     return partner, mate
 
 
-def greet_all(me):
+def greet_all(me, mirrored=False):
     barrier = pltpu.get_barrier_semaphore()
+    if mirrored:
+        other = 1 - lax.axis_index(DP)
+        pl.semaphore_signal(barrier, inc=1, device_id={DP: other}, device_id_type=MESH)
     for step in range(1, 16):
         pl.semaphore_signal(
             barrier, inc=1, device_id=at_expert((me + step) % 16), device_id_type=MESH
         )
-    pl.semaphore_wait(barrier, 15)
-
-
-def gather_kernel(n, m, *refs):
-    x_refs, swap_refs = refs[:n], refs[n : n + m]
-    outs, swap_outs = refs[n + m : 2 * n + m], refs[2 * n + m : 2 * (n + m)]
-    own_sem, send_sem, recv_sem, swap_send, swap_recv = refs[2 * (n + m) :]
+    pl.semaphore_wait(barrier, 15 + mirrored)
+
+
+def halves(rows):
+    return (pl.ds(0, rows // 2), pl.ds(rows // 2, rows // 2)) if rows % 32 == 0 else (pl.ds(0, rows),)
+
+
+def gather_kernel(k, m, mirrored, *refs):
+    x_refs, swap_refs = refs[:k], refs[k : k + m]
+    outs, swap_outs = refs[k + m : 2 * k + m], refs[2 * k + m : 2 * (k + m)]
+    mirrors = refs[2 * (k + m) : 2 * (k + m) + m * mirrored]
+    own_sem, send_sem, recv_sem, swap_send, swap_recv, mirror_sem = refs[
+        2 * (k + m) + m * mirrored :
+    ]
+    pieces = [
+        (a, at)
+        for a in range(k)
+        for at in (halves(x_refs[a].shape[0]) if len(x_refs[a].shape) == 2 else (None,))
+    ]
+    n = len(pieces)
     me, line, pair, core = grid_place()
     if m:
-        greet_all(me)
+        greet_all(me, mirrored)
         partner, mate = me + 1 - 2 * core, me + 2 - 4 * pair
     else:
         partner, mate = greet_neighbours(me, line, pair, core)
 
+    def held(i):
+        a, at = pieces[i]
+        return x_refs[a] if at is None else x_refs[a].at[at, :]
+
+    def slot(i, origin):
+        a, at = pieces[i]
+        return outs[a].at[:, origin] if at is None else outs[a].at[origin, at, :]
+
     def own_copy(i):
         if i < n:
-            return pltpu.make_async_copy(x_refs[i], outs[i].at[me], own_sem.at[i])
+            return pltpu.make_async_copy(held(i), slot(i, me), own_sem.at[i])
         i -= n
         return pltpu.make_async_copy(
             swap_refs[i].at[me], swap_outs[i].at[me], own_sem.at[n + i]
@@ -175,7 +202,7 @@
     def copy(i, source, origin, way, to):
         return pltpu.make_async_remote_copy(
             src_ref=source,
-            dst_ref=outs[i].at[origin],
+            dst_ref=slot(i, origin),
             send_sem=send_sem.at[i, origin, way],
             recv_sem=recv_sem.at[i, origin],
             device_id=at_expert(to),
@@ -194,7 +221,25 @@
         )
 
     def arrived(i, origin):
-        copy(i, outs[i].at[origin], origin, 0, partner).wait_recv()
+        copy(i, slot(i, origin), origin, 0, partner).wait_recv()
+
+    def mirror_copy(i):
+        return pltpu.make_async_remote_copy(
+            src_ref=swap_outs[i],
+            dst_ref=mirrors[i],
+            send_sem=mirror_sem.at[i, 0],
+            recv_sem=mirror_sem.at[i, 1],
+            device_id={DP: 1 - lax.axis_index(DP)},
+            device_id_type=MESH,
+        )
+
+    def swaps_done():
+        for i in range(m):
+            for step in range(1, 16):
+                swap_copy(i, step).wait_recv()
+            own_copy(n + i).wait()
+            if mirrored:
+                mirror_copy(i).start()
 
     def along(i, origin, source, upward, downward, act):
         if upward:
@@ -212,8 +257,10 @@
         act(copy(i, source, origin, 2, mate))
         act(copy(i, source, origin, 3, partner))
 
-    def walk(act, wait):
+    def walk(act, wait, between):
         for far in range(1, 5):
+            if far == 3:
+                between()
             if far < 4:
 
                 @pl.when(line >= far)
@@ -221,14 +268,14 @@
                     origin = me - 4 * far
                     for i in range(n):
                         wait(i, origin)
-                        along(i, origin, outs[i].at[origin], True, False, act)
+                        along(i, origin, slot(i, origin), True, False, act)
 
                 @pl.when(line + far <= 3)
                 def _():
                     origin = me + 4 * far
                     for i in range(n):
                         wait(i, origin)
-                        along(i, origin, outs[i].at[origin], False, True, act)
+                        along(i, origin, slot(i, origin), False, True, act)
 
             for sign in (-1, 1) if far > 1 else (1,):
                 step = sign * (far - 1)
@@ -238,7 +285,7 @@
                     origin = mate + 4 * step
                     for i in range(n):
                         wait(i, origin)
-                        act(copy(i, outs[i].at[origin], origin, 3, partner))
+                        act(copy(i, slot(i, origin), origin, 3, partner))
 
     def start(c):
         c.start()
@@ -247,61 +294,80 @@
         c.wait_send()
 
     for i in range(n):
-        along(i, me, x_refs[i], True, True, start)
+        along(i, me, held(i), True, True, start)
     for i in range(m):
         for step in range(1, 16):
             swap_copy(i, step).start()
     for i in range(n + m):
         own_copy(i).start()
-    walk(start, arrived)
+    walk(start, arrived, swaps_done)
     for i in range(n):
         for index in range(8):
             arrived(i, 2 * index + 1 - core)
     for i in range(n):
-        along(i, me, x_refs[i], True, True, sent)
-    walk(sent, lambda i, origin: None)
+        along(i, me, held(i), True, True, sent)
+    walk(sent, lambda i, origin: None, lambda: None)
     for i in range(m):
         for step in range(1, 16):
-            swap_copy(i, step).wait()
-    for i in range(n + m):
+            swap_copy(i, step).wait_send()
+        if mirrored:
+            mirror_copy(i).wait()
+    for i in range(n):
         own_copy(i).wait()
 
 
-def ring_gather(values, swaps, collective):
-    n, m = len(values), len(swaps)
+def ring_gather(values, swaps, collective, mirrored=False):
+    k, m = len(values), len(swaps)
+    n = sum(len(halves(v.shape[0])) if v.ndim == 2 else 1 for v in values)
     sent = 2 * (15 * sum(v.size for v in values) + sum(v.size for v in swaps))
     sems = pltpu.SemaphoreType.DMA
     anywhere = pl.BlockSpec(memory_space=pl.ANY)
+    shapes = [(16,) + v.shape if v.ndim == 2 else v.shape[:1] + (16,) + v.shape[1:] for v in values]
+    shapes += [v.shape for v in swaps] * (1 + mirrored)
     outs = pl.pallas_call(
-        functools.partial(gather_kernel, n, m),
-        out_shape=[jax.ShapeDtypeStruct((16,) + v.shape, v.dtype) for v in values]
-        + [jax.ShapeDtypeStruct(v.shape, v.dtype) for v in swaps],
-        in_specs=[pl.BlockSpec(memory_space=pltpu.VMEM)] * (n + m),
-        out_specs=[anywhere] * (n + m),
+        functools.partial(gather_kernel, k, m, mirrored),
+        out_shape=[jax.ShapeDtypeStruct(shape, bf16) for shape in shapes],
+        in_specs=[pl.BlockSpec(memory_space=pltpu.VMEM)] * (k + m),
+        out_specs=[anywhere] * len(shapes),
         scratch_shapes=[
             sems((n + m,)),
             sems((n, 16, 4)),
             sems((n, 16)),
             sems((max(m, 1), 16)),
             sems((max(m, 1), 16)),
+            sems((max(m, 1), 2)),
         ],
         compiler_params=pltpu.CompilerParams(collective_id=collective, has_side_effects=True),
         cost_estimate=pl.CostEstimate(flops=0, bytes_accessed=16 * sent, transcendentals=0),
     )(*values, *swaps)
-    return [o.reshape(-1, o.shape[-1]) for o in outs[:n]] + list(outs[n:])
-
-
-def scatter_kernel(n, *refs):
-    parts = [(refs[i], refs[n + i]) + refs[2 * n + 5 * i : 2 * n + 5 * i + 5] for i in range(n)]
+    return [o.reshape(-1, o.shape[-1]) for o in outs[:k]] + list(outs[k:])
+
+
+def scatter_pieces(shapes):
+    return [
+        (a, at)
+        for a, shape in enumerate(shapes)
+        for at in (halves(shape[0]) if len(shape) == 2 else (None,))
+    ]
+
+
+def scatter_kernel(k, *refs):
+    pieces = scatter_pieces([ref.shape for ref in refs[k : 2 * k]])
+    n = len(pieces)
+    parts = [
+        (refs[a], refs[k + a] if at is None else refs[k + a].at[at, :])
+        + refs[2 * k + 5 * i : 2 * k + 5 * i + 5]
+        for i, (a, at) in enumerate(pieces)
+    ]
     (
         core_send, core_recv, mate_send, mate_recv, up_send, up_recv, down_send, down_recv,
-    ) = refs[7 * n :]
+    ) = refs[2 * k + 5 * n :]
     me, line, pair, core = grid_place()
     partner, mate = greet_neighbours(me, line, pair, core)
 
     def block(i, dest):
-        ref = parts[i][0]
-        return ref.at[dest] if len(ref.shape) == 3 else ref.at[:, dest]
+        ref, at = parts[i][0], pieces[i][1]
+        return ref.at[:, dest] if at is None else ref.at[dest, at, :]
 
     def remote(source, target, send, recv, to):
         return pltpu.make_async_remote_copy(
@@ -415,16 +481,21 @@
 
 
 def ring_scatter(values, collective):
-    n = len(values)
+    count = len(values)
     shapes = [v.shape[1:] if len(v.shape) == 3 else v.shape[:1] + v.shape[2:] for v in values]
-    buffers = [pltpu.VMEM((k,) + s, bf16) for s in shapes for k in (8, 4, 4, 4, 8)]
+    pieces = scatter_pieces(shapes)
+    n = len(pieces)
+    parts = [
+        shapes[a] if at is None else (at.size,) + shapes[a][1:] for a, at in pieces
+    ]
+    buffers = [pltpu.VMEM((k,) + s, bf16) for s in parts for k in (8, 4, 4, 4, 8)]
     sent = 30 * sum(math.prod(s) for s in shapes)
     vmem = pl.BlockSpec(memory_space=pltpu.VMEM)
     return pl.pallas_call(
-        functools.partial(scatter_kernel, n),
+        functools.partial(scatter_kernel, count),
         out_shape=[jax.ShapeDtypeStruct(s, f32) for s in shapes],
-        in_specs=[vmem] * n,
-        out_specs=[vmem] * n,
+        in_specs=[vmem] * count,
+        out_specs=[vmem] * count,
         scratch_shapes=buffers
         + [pltpu.SemaphoreType.DMA((n, k)) for k in (8, 8, 4, 4, 4, 4, 4, 4)],
         compiler_params=pltpu.CompilerParams(collective_id=collective, has_side_effects=True),
@@ -849,7 +920,7 @@
         ],
         axis=1,
     )
-    small = dp_gather(small)
+    small = dp_gather(small).reshape(replicas, rows, -1)
     query_parts = query_weight.reshape(rows, HEADS, QD).transpose(1, 0, 2)
     lup_rows = latent_up.shape[0]
     code_rows = -(lup_rows + 1) % 16 + 1
@@ -859,11 +930,8 @@
     lup_parts = jnp.concatenate(
         [latent_up.reshape(lup_rows, HEADS, HD + VD).transpose(1, 0, 2), code_part], axis=1
     )
-    small_all, x_all, query_swap, lup_swap = ring_gather(
-        [small, x_low], [query_parts, lup_parts], 1
-    )
-    small_all = (
-        small_all.reshape(groups, replicas, rows, -1).transpose(1, 0, 2, 3).reshape(width, -1)
+    small_all, x_all, *swapped = ring_gather(
+        [small, x_low], [query_parts, lup_parts], 1, replicas == 2
     )
     ldown_all = small_all[:, : RANK + RD]
     router_all = small_all[:, RANK + RD : RANK + RD + experts]
@@ -872,9 +940,15 @@
     gain_moe = gains[:, 1]
     gain_lat = gains[:, 2].reshape(-1, rows)[:, : latent_gain.shape[0]].reshape(-1)
 
-    wq = dp_gather(query_swap.reshape(groups * rows, QD))
-    lup = dp_gather(lup_swap[:, :lup_rows].reshape(groups * lup_rows, HD + VD))
-    code = lup_swap[:, lup_rows, :own].astype(f32).reshape(tokens)
+    def all_rows(at, cut):
+        value = swapped[at][:, :cut].reshape(groups * cut, -1)
+        if replicas != 2:
+            return dp_gather(value)
+        return ordered(value, swapped[at + 2][:, :cut].reshape(groups * cut, -1))
+
+    wq = all_rows(0, rows)
+    lup = all_rows(1, lup_rows)
+    code = swapped[1][:, lup_rows, :own].astype(f32).reshape(tokens)
 
     def columns_of(weight):
         return (
@@ -988,7 +1062,7 @@
     low_all = gather_rows(attn_low, EXPERT)
     gate_up_owned = expert_swap(
         gate_up_owned.reshape(groups, rows, 2 * hidden_own)
-    ).astype(f32)
+    )
 
     def owned_columns(value):
         return (
@@ -997,8 +1071,8 @@
             .reshape(rows, replicas * groups * part)
         )
 
-    sgate_owned = owned_columns(gate_up_owned[:, :, :hidden_own])
-    sup_owned = owned_columns(gate_up_owned[:, :, hidden_own:])
+    sgate_owned = owned_columns(gate_up_owned[:, :, :hidden_own]).astype(f32)
+    sup_owned = owned_columns(gate_up_owned[:, :, hidden_own:]).astype(f32)
     query_grad, pair_grad = attend_back(
         probs_attn, grad_s, heads_s, query, key, value, scale, groups, span
     )

time: 1020 us -> 1020 us (level)
  Pallas kernels: 458 us -> 531 us
  waiting for transfers between devices: 161 us -> 98.3 us
    pallas_call x4, Pallas kernels: 350 us -> 423 us  [the longest x2 272 us: ring_gather(): pl.pallas_call(functools.partial(gather_kernel, k, m, mirrored), out_shap...]
    ppermute x15 -> x13, waiting for transfers between devices: 152 us -> 88.6 us  [dp_swap(): return lax.ppermute(value, DP, [(0, 1), (1, 0)])]
    convert_element_type x1 -> x7, local copies, waits for them, and re-layouts: 0.01 us -> 13.5 us  [the longest x3 8.5 us: per_device(): sup_owned = owned_columns(gate_up_owned[:, :, hidden_own:]).astype(f32)]
  transfers between devices with their start and end apart: 22 -> 20, of which waited for: 5 -> 3; matrix products, arithmetic and copies ran while one was open for 22% -> 22% of each run, Pallas kernels for 33% -> 40%
where the time goes in v5:
time: 1020 us; the launch traced here: 1010 us
  Pallas kernels  531 us (52%)
  matrix products  174 us (17%)
  waiting for transfers between devices  98.3 us (10%)
  other arithmetic  92.2 us (9%)
  local copies, waits for them, and re-layouts  71.3 us (7%)
  starting transfers between devices  33.5 us (3%)
  between operations  15 us (1%)
    pallas_call x2, Pallas kernels, ring_gather(): pl.pallas_call(functools.partial(gather_kernel, k, m, mirrored), out_shap...  272 us
    pallas_call x2, Pallas kernels, ring_scatter(): pl.pallas_call(functools.partial(scatter_kernel, count), out_shape=[jax.S...  152 us
    ppermute x13, waiting for transfers between devices, dp_swap(): return lax.ppermute(value, DP, [(0, 1), (1, 0)])  88.6 us
    dot_general x10, matrix products, left_product(): lax.dot_general(left, right, (((0,), (0,)), ((), ())), preferred_element_...  75.3 us
    dot_general x5, matrix products, right_product(): lax.dot_general(left, right, (((1,), (1,)), ((), ())), preferred_element_...  48.2 us
    dot_general x5, matrix products, product(): return jnp.dot(left, right, preferred_element_type=f32)  37.3 us
    pallas_call x2, Pallas kernels, swap_call(): pl.pallas_call(functools.partial(swap_kernel, source, target), out_shape=...  33.8 us
    pallas_call x2, Pallas kernels, combine(): pl.pallas_call(functools.partial(combine_kernel, dims), grid=(chunks, per...  23.9 us
  transfers between devices with their start and end apart: 20, of which 3 were waited for; matrix products, arithmetic and copies ran while one was open for 22% of the time, Pallas kernels for 40%

profile of v5, /device:TPU:0, one launch (start us, length us, event | category | flops | bytes accessed | tf_op | source)
XLA Modules:
  0.0 1015.0 jit_solution(11791128213012813800)
XLA Ops:
  22.3 6.4 all-to-all-start
  45.8 216.2 %shard_map.306 = (bf16[2,16,64,640]{3,2,1,0:T(8,128)(2,1)}, bf16[16,128,2048]{2,1,0:T(8,128)(2,1)}, bf16[16,64,192]{2,1,0:T(8,128)(2,1)}, bf16[16,32,256]{2,1,0:...) custom-call(bf16[2,64,640]{2,1,0:T(8,128)(2,1)} %bitcast.193, bf16[128,2048]{1,0:T(8,128)(2,1)} %bitcast.154, ...), custom_call_target="tpu_custom_call" | custom-call | bytes 175636480 | tf_op jit(solution)/shard_map/pallas_call | solution.py:327
  270.2 13.3 %fusion.11.weight_ref = bf16[2048,768]{1,0:T(8,128)(2,1)} fusion(bf16[1024,192]{1,0:T(8,128)(2,1)S(1)} %bitcast.166, bf16[1024,192]{1,0:T(8,128)(2,1)S(1)} %bitcast.164, bf16[2048,64]{1,0:T(8,128)(2,1)S(1)} %fusion.35, bf16[2048,576]{1,0:T(8,128)(2,1)} %bitcast.161), kind=kLoop, calls=%fused_computation.33 | loop fusion | flops 12582912 | bytes 6553600 | tf_op jit(solution)/shard_map/concatenate | solution.py:977
  283.5 17.4 %project.1 = (bf16[2048,2048]{1,0:T(8,128)(2,1)}, bf16[2048,256]{1,0:T(8,128)(2,1)}, bf16[2048,256]{1,0:T(8,128)(2,1)}, bf16[2048,128]{1,0:T(8,128)(2,1)}, bf16[...) custom-call(bf16[2048,2048]{1,0:T(8,128)(2,1)} %bitcast.214, bf16[2048,768]{1,0:T(8,128)(2,1)} %fusion.11.weight_ref, ...), custom_call_target="tpu_custom_call" | custom-call | flops 6979321856 | bytes 20971520 | tf_op jit(solution)/shard_map/project/pallas_call | solution.py:664
  306.2 7.6 attend.1
  313.9 15.5 %shard_map.307 = bf16[2,64,2048]{2,1,0:T(8,128)(2,1)} custom-call(bf16[2,1024,128]{2,1,0:T(8,128)(2,1)} %get-tuple-element.49.x_ref.out_ref), custom_call_target="tpu_custom_call" | custom-call | bytes 33554432 | tf_op jit(solution)/shard_map/pallas_call | solution.py:532
  334.7 4.8 broadcast_select_fusion.1
  339.5 4.9 broadcast_select_fusion.3
  344.4 4.9 broadcast_select_fusion.5
  349.3 7.2 convolution_convert_fusion.2
  356.5 6.4 multiply_reduce_fusion.5
  363.9 55.6 %shard_map.308 = bf16[16,128,2048]{2,1,0:T(8,128)(2,1)} custom-call(bf16[128,2048]{1,0:T(8,128)(2,1)} %multiply_convert_fusion.7.refs_0_), custom_call_target="tpu_custom_call" | custom-call | bytes 125829120 | tf_op jit(solution)/shard_map/pallas_call | solution.py:327
  419.5 7.8 fusion.62
  430.2 5.5 convolution_convert_fusion.3
  435.8 7.3 fusion.9
  443.1 9.6 multiply_convert_fusion.2
  452.8 7.2 fusion.2
  463.9 7.6 fusion.1
  471.5 16.0 %multiply_convert_fusion.1 = (bf16[864,1408]{1,0:T(8,128)(2,1)}, bf16[864,1408]{1,0:T(8,128)(2,1)}) fusion(f32[864,1408]{1,0:T(8,128)} %fusion.9, f32[864,1408]{1,0:T(8,128)} %get-tuple-element.204, bf16[864,2048]{1,0:T(8,128)(2,1)S(1)} %get-tuple-element.199, bf16[704,2048]{1,0:T(8,128)(2,1)} %get-tuple-element.170, bf16[704,2048]{1,0:T(8,128)(2,1)} %get-tuple-element.169), kind=kOutput, calls=%fused_computation.15 | convolution fusion | flops 5010182144 | bytes 23904256 | tf_op jit(solution)/shard_map/dot_general | solution.py:39
  487.5 10.9 %fusion.6 = f32[864,2048]{1,0:T(8,128)} fusion(bf16[864,1408]{1,0:T(8,128)(2,1)} %get-tuple-element.168, bf16[1024,1408]{1,0:T(8,128)(2,1)} %get-tuple-element.174, bf16[1024,1408]{1,0:T(8,128)(2,1)} %get-tuple-element.173), kind=kOutput, calls=%fused_computation.24 | convolution fusion | flops 4994367488 | bytes 15278080 | tf_op jit(solution)/shard_map/dot_general | solution.py:39
  498.4 10.8 %add_convert_fusion = bf16[864,2048]{1,0:T(8,128)(2,1)} fusion(f32[864,2048]{1,0:T(8,128)} %fusion.6, bf16[864,1408]{1,0:T(8,128)(2,1)} %get-tuple-element.167, bf16[1024,1408]{1,0:T(8,128)(2,1)} %get-tuple-element.172, bf16[1024,1408]{1,0:T(8,128)(2,1)S(1)} %copy-done.29), kind=kOutput, calls=%fused_computation.6 | convolution fusion | flops 4997906432 | bytes 18817024 | tf_op jit(solution)/shard_map/dot_general | solution.py:39
  509.2 4.2 multiply_convert_fusion.4
  515.4 12.7 %shard_map.310 = bf16[2048,2048]{1,0:T(8,128)(2,1)} custom-call(bf16[4,216,512]{2,1,0:T(8,128)(2,1)} %copy-done.2, bf16[4,216,2048]{2,1,0:T(8,128)(2,1)} %bitcast.217, bf16[2048,368]{1,0:T(8,128)(2,1)} %pad_maximum_fusion.16.left_ref, bf16[2048,368]{1,0:T(8,128)(2,1)} %pad_maximum_fusion.15.right_ref), custom_call_target="tpu_custom_call" | custom-call | flops 4898947072 | bytes 16777216 | tf_op jit(solution)/shard_map/pallas_call | solution.py:603
  528.1 54.8 %shard_map.311 = f32[128,2048]{1,0:T(8,128)} custom-call(bf16[16,128,2048]{2,1,0:T(8,128)(2,1)} %bitcast.157), custom_call_target="tpu_custom_call" | custom-call | bytes 125829120 | tf_op jit(solution)/shard_map/pallas_call | solution.py:494
  589.1 6.6 fusion.64
  597.6 5.4 convolution_convert_fusion.5
  603.1 18.3 %shard_map.312.grad_ref = bf16[2,1024,128]{2,1,0:T(8,128)(2,1)} custom-call(bf16[2,64,2048]{2,1,0:T(8,128)(2,1)} %bitcast.182), custom_call_target="tpu_custom_call" | custom-call | bytes 33554432 | tf_op jit(solution)/shard_map/pallas_call | solution.py:532
  621.4 7.1 attend_back.1
  628.5 11.2 %shard_map.309 = bf16[2048,2048]{1,0:T(8,128)(2,1)} custom-call(bf16[4,216,512]{2,1,0:T(8,128)(2,1)} %copy-done.2, bf16[4,216,2048]{2,1,0:T(8,128)(2,1)} %bitcast.152, bf16[2048,176]{1,0:T(8,128)(2,1)} %get-tuple-element.177.left_ref, bf16[176,2048]{1,0:T(8,128)(2,1)} %pad_maximum_fusion.20.right_ref), custom_call_target="tpu_custom_call" | custom-call | flops 3288334336 | bytes 16777216 | tf_op jit(solution)/shard_map/pallas_call | solution.py:603
  639.7 17.8 %project_back.1 = (bf16[2048,768]{1,0:T(8,128)(2,1)}, bf16[2048,2048]{1,0:T(8,128)(2,1)}, f32[512,256]{1,0:T(8,128)}, f32[1,512]{1,0:T(1,128)}) custom-call(f32[2048,256]{1,0:T(8,128)} %bitcast.216, f32[2048,384]{1,0:T(8,128)} %bitcast.215, bf16[2048,768]{1,0:T(8,128)(2,1)} %fusion.11.weight_ref, bf16[512,256]{1,0:T(8,128)(2,1)} %pad_maximum_fusion.22.lup_ref, ...), custom_call_target="tpu_custom_call" | custom-call | flops 7730940928 | bytes 25165824 | tf_op jit(solution)/shard_map/project_back/pallas_call | solution.py:828
  657.5 10.4 %fusion.63 = f32[2048,768]{0,1:T(8,128)S(1)} fusion(bf16[2048,2048]{1,0:T(8,128)(2,1)} %get-tuple-element.50, bf16[2048,768]{1,0:T(8,128)(2,1)} %get-tuple-element.57), kind=kOutput, calls=%fused_computation.187 | convolution fusion | flops 6442450944 | bytes 17825792 | tf_op jit(solution)/shard_map/dot_general | solution.py:35
  672.4 6.8 copy.211
  679.2 5.9 fusion.66
  692.9 4.4 copy.210
  697.3 4.5 multiply_reduce_fusion
  706.2 7.8 convolution_convert_fusion
  716.0 96.8 %shard_map.313 = (f32[2,64,576]{2,1,0:T(8,128)}, f32[2,64,128]{2,1,0:T(8,128)}, f32[128,2048]{1,0:T(8,128)}) custom-call(bf16[2,16,64,576]{3,2,1,0:T(8,128)(2,1)} %bitcast.156, bf16[2,16,64,128]{3,2,1,0:T(8,128)(2,1)} %bitcast.181, bf16[16,128,2048]{2,1,0:T(8,128)(2,1)} %bitcast.158), custom_call_target="tpu_custom_call" | custom-call | bytes 169082880 | tf_op jit(solution)/shard_map/pallas_call | solution.py:494
  815.5 8.0 convolution_convert_fusion.1
  823.4 5.2 convolution_convert_fusion.4
  832.3 4.9 collective-permute-done.7
  844.8 4.7 all-to-all-start.2
  851.7 4.9 fusion.65
  859.9 8.2 all-to-all-done.2
  883.3 9.7 add_bitcast_fusion.1
  893.0 83.6 %collective-permute-done.6 = bf16[1024,384]{0,1:T(8,128)(2,1)} collective-permute-done((bf16[1024,384]{0,1:T(8,128)(2,1)S(1)}, bf16[1024,384]{0,1:T(8,128)(2,1)}, u32[]{:S(2)}, u32[]{:S(2)}) %collective-permute-start.6) | collective-permute-done | bytes 786464 | tf_op jit(solution)/shard_map/ppermute | solution.py:68
  979.2 5.1 all-to-all-start.1
  984.4 9.7 add_bitcast_fusion.2
  994.1 7.1 add_bitcast_fusion
  (275 shorter events, 131.3 us)
Async XLA Ops:
  7.2 11.7 %copy-start.40 = (bf16[64,2816]{1,0:T(8,128)(2,1)S(1)}, bf16[64,2816]{1,0:T(8,128)(2,1)}, u32[]{:S(2)}) copy-start(bf16[64,2816]{1,0:T(8,128)(2,1)} %param.32) | copy-start | bytes 1081348
  7.2 342.1 %all-gather.6.cloned.1.call-start = ((), (), s32[]{:S(2)}) async-start(), calls=%async_computation.6 | async-start | bytes 8912896 | tf_op jit(solution)/shard_map/all_gather | solution.py:112
  7.9 348.6 %all-gather.4.cloned.1.call-start = ((), (), s32[]{:S(2)}) async-start(), calls=%async_computation.4 | async-start | bytes 8650752 | tf_op jit(solution)/shard_map/all_gather | solution.py:112
  12.8 32.4 %collective-permute-start = (bf16[64,640]{1,0:T(8,128)(2,1)S(1)}, bf16[64,640]{1,0:T(8,128)(2,1)S(1)}, u32[]{:S(2)}, u32[]{:S(2)}) collective-permute-start(bf16[64,640]{1,0:T(8,128)(2,1)S(1)} %concatenate.57), channel_id=1, source_target_pairs={{0,16},{16,0},{1,17},{17,1},{2,18},{18,2},{3,19},{19,3},{4,20},{20... | collective-permute-start | bytes 245768 | tf_op jit(solution)/shard_map/ppermute | solution.py:68
  15.8 313.6 %collective-permute-start.5 = (bf16[88,2048]{1,0:T(8,128)(2,1)}, bf16[88,2048]{1,0:T(8,128)(2,1)}, u32[]{:S(2)}, u32[]{:S(2)}) collective-permute-start(bf16[88,2048]{1,0:T(8,128)(2,1)} %param.33), channel_id=1, source_target_pairs={{0,16},{16,0},{1,17},{17,1},{2,18},{18,2},{3,19},{19,3},{4,20},{20... | collective-permute-start | bytes 1081352 | tf_op jit(solution)/shard_map/ppermute | solution.py:68
  18.9 14.1 %copy-start.45 = (s32[2,64,6]{1,0,2:T(2,128)S(1)}, s32[2,64,6]{1,0,2:T(2,128)}, u32[]{:S(2)}) copy-start(s32[2,64,6]{1,0,2:T(2,128)} %param.21) | copy-start | bytes 9220
  18.9 14.2 %copy-start.48 = (s32[2,64]{1,0:T(2,128)S(1)}, s32[2,64]{1,0:T(2,128)}, u32[]{:S(2)}) copy-start(s32[2,64]{1,0:T(2,128)} %param.22) | copy-start | bytes 1540
  19.0 14.5 %copy-start.44 = (s32[2,1024]{1,0:T(2,128)S(1)}, s32[2,1024]{1,0:T(2,128)}, u32[]{:S(2)}) copy-start(s32[2,1024]{1,0:T(2,128)} %param.20) | copy-start | bytes 24580
  19.0 15.1 %copy-start.42 = (bf16[16,4096]{1,0:T(8,128)(2,1)S(1)}, bf16[16,4096]{1,0:T(8,128)(2,1)}, u32[]{:S(2)}) copy-start(bf16[16,4096]{1,0:T(8,128)(2,1)} %param.26) | copy-start | bytes 393220
  20.3 13.8 %copy-start.39 = (bf16[64,3072]{1,0:T(8,128)(2,1)S(1)}, bf16[64,3072]{1,0:T(8,128)(2,1)}, u32[]{:S(2)}) copy-start(bf16[64,3072]{1,0:T(8,128)(2,1)} %param.24) | copy-start | bytes 1179652
  22.3 279.3 %all-to-all-start = ((bf16[16,64,352]{2,1,0:T(8,128)(2,1)}), bf16[16,64,352]{2,1,0:T(8,128)(2,1)S(1)}, u32[]{:S(2)}, u32[]{:S(2)}) async-start(bf16[16,64,352]{2,1,0:T(8,128)(2,1)} %pad_maximum_fusion.19), calls=%async_computation | async-start | bytes 1572864 | tf_op jit(solution)/shard_map/all_to_all | solution.py:108
  28.7 822.9 %all-gather.8.cloned.1.call-start = ((), (), s32[]{:S(2)}) async-start(), calls=%async_computation.7 | async-start | bytes 8912896 | tf_op jit(solution)/shard_map/all_gather | solution.py:112
  29.3 305.3 %collective-permute-start.4 = (bf16[704,2048]{1,0:T(8,128)(2,1)}, bf16[704,2048]{1,0:T(8,128)(2,1)}, u32[]{:S(2)}, u32[]{:S(2)}) collective-permute-start(bf16[704,2048]{1,0:T(8,128)(2,1)} %bitcast.177), channel_id=1, source_target_pairs={{0,16},{16,0},{1,17},{17,1},{2,18},{18,2},{3,19},{19,3},{4,20},{20... | collective-permute-start | bytes 8650760 | tf_op jit(solution)/shard_map/ppermute | solution.py:68
  30.9 308.6 %collective-permute-start.3 = (bf16[1024,1408]{1,0:T(8,128)(2,1)}, bf16[1024,1408]{1,0:T(8,128)(2,1)}, u32[]{:S(2)}, u32[]{:S(2)}) collective-permute-start(bf16[1024,1408]{1,0:T(8,128)(2,1)} %bitcast.178), channel_id=1, source_target_pairs={{0,16},{16,0},{1,17},{17,1},{2,18},{18,2},{3,19},{19,3},{4,20},{20... | collective-permute-start | bytes 8650760 | tf_op jit(solution)/shard_map/ppermute | solution.py:68
  31.4 313.0 %collective-permute-start.2 = (bf16[1024,1408]{1,0:T(8,128)(2,1)}, bf16[1024,1408]{1,0:T(8,128)(2,1)}, u32[]{:S(2)}, u32[]{:S(2)}) collective-permute-start(bf16[1024,1408]{1,0:T(8,128)(2,1)} %bitcast.179), channel_id=1, source_target_pairs={{0,16},{16,0},{1,17},{17,1},{2,18},{18,2},{3,19},{19,3},{4,20},{20... | collective-permute-start | bytes 8650760 | tf_op jit(solution)/shard_map/ppermute | solution.py:68
  302.0 29.4 %collective-permute-start.1 = (bf16[1024,352]{0,1:T(8,128)(2,1)S(1)}, bf16[1024,352]{0,1:T(8,128)(2,1)S(1)}, u32[]{:S(2)}, u32[]{:S(2)}) collective-permute-start(bf16[1024,352]{0,1:T(8,128)(2,1)S(1)} %copy.202), channel_id=1, source_target_pairs={{0,16},{16,0},{1,17},{17,1},{2,18},{18,2},{3,19},{19,3},{4,20},{20... | collective-permute-start | bytes 2162696 | tf_op jit(solution)/shard_map/ppermute | solution.py:68
  303.9 156.2 %copy-start.2 = (bf16[4,216,512]{2,1,0:T(8,128)(2,1)}, bf16[4,216,512]{2,1,0:T(8,128)(2,1)S(1)}, u32[]{:S(2)}) copy-start(bf16[4,216,512]{2,1,0:T(8,128)(2,1)S(1)} %and_convert_fusion.select_ref) | copy-start | bytes 2654212
  419.5 9.4 copy-start.46
  435.8 7.3 copy-start.20
  443.1 9.7 copy-start.5
  443.1 9.7 copy-start.24
  443.1 9.7 copy-start.25
  471.5 16.0 %copy-start.6 = (bf16[864,2048]{1,0:T(8,128)(2,1)}, bf16[864,2048]{1,0:T(8,128)(2,1)S(1)}, u32[]{:S(2)}) copy-start(bf16[864,2048]{1,0:T(8,128)(2,1)S(1)} %get-tuple-element.199) | copy-start | bytes 10616836
  471.5 37.7 %slice-start = ((s8[8388608]{0:T(1024)(128)(4,1)}), s8[4194304]{0:T(1024)(128)(4,1)S(1)}, s32[]{:S(2)}) async-start(s8[8388608]{0:T(1024)(128)(4,1)} %bitcast.147), calls=%async_computation.8 | async-start | bytes 8388608
  487.5 10.9 %copy-start.29 = (bf16[1024,1408]{1,0:T(8,128)(2,1)S(1)}, bf16[1024,1408]{1,0:T(8,128)(2,1)}, u32[]{:S(2)}) copy-start(bf16[1024,1408]{1,0:T(8,128)(2,1)} %get-tuple-element.171) | copy-start | bytes 8650756
  487.5 21.7 %slice-start.1 = ((s8[8388608]{0:T(1024)(128)(4,1)}), s8[4194304]{0:T(1024)(128)(4,1)S(1)}, s32[]{:S(2)}) async-start(s8[8388608]{0:T(1024)(128)(4,1)} %bitcast.147), calls=%async_computation.9 | async-start | bytes 8388608
  498.3 10.9 %copy-start.15 = (f32[2048,368]{1,0:T(8,128)S(1)}, f32[2048,368]{1,0:T(8,128)}, u32[]{:S(2)}) copy-start(f32[2048,368]{1,0:T(8,128)} %copy-done.14) | copy-start | bytes 9043972
  498.3 10.9 %copy-start.32 = (bf16[88,2048]{1,0:T(8,128)(2,1)S(1)}, bf16[88,2048]{1,0:T(8,128)(2,1)}, u32[]{:S(2)}) copy-start(bf16[88,2048]{1,0:T(8,128)(2,1)} %get-tuple-element.188) | copy-start | bytes 1081348
  498.3 10.9 %copy-start.33 = (bf16[88,2048]{1,0:T(8,128)(2,1)S(1)}, bf16[88,2048]{1,0:T(8,128)(2,1)}, u32[]{:S(2)}) copy-start(bf16[88,2048]{1,0:T(8,128)(2,1)} %get-tuple-element.189) | copy-start | bytes 1081348
  528.1 56.4 %copy-start.16 = (bf16[2,64,2048]{2,1,0:T(8,128)(2,1)S(1)}, bf16[2,64,2048]{2,1,0:T(8,128)(2,1)}, u32[]{:S(2)}) copy-start(bf16[2,64,2048]{2,1,0:T(8,128)(2,1)} %param.23) | copy-start | bytes 1572868
  586.9 414.2 %reduce-scatter.2.cloned.1.call-start = ((), (), s32[]{:S(2)}) async-start(), calls=%async_computation.5 | async-start | bytes 8912896 | tf_op jit(solution)/shard_map/reduce_scatter | solution.py:116
  679.2 12.9 %copy-start.47 = (f32[1,512]{1,0:T(1,128)S(1)}, f32[1,512]{1,0:T(1,128)}, u32[]{:S(2)}) copy-start(f32[1,512]{1,0:T(1,128)} %get-tuple-element.58) | copy-start | bytes 6148
  687.0 162.5 %collective-permute-start.9 = (bf16[88,2048]{1,0:T(8,128)(2,1)}, bf16[88,2048]{1,0:T(8,128)(2,1)}, u32[]{:S(2)}, u32[]{:S(2)}) collective-permute-start(bf16[88,2048]{1,0:T(8,128)(2,1)} %dynamic-slice_convert_fusion.2), channel_id=1, source_target_pairs={{0,16},{16,0},{1,17},{17,1},{2,18},{18,2},{3,19},{19,3},{4,20},{20... | collective-permute-start | bytes 1081352 | tf_op jit(solution)/shard_map/ppermute | solution.py:68
  691.5 150.3 %collective-permute-start.8 = (bf16[1024,352]{0,1:T(8,128)(2,1)}, bf16[1024,352]{0,1:T(8,128)(2,1)}, u32[]{:S(2)}, u32[]{:S(2)}) collective-permute-start(bf16[1024,352]{0,1:T(8,128)(2,1)} %dynamic-slice_convert_fusion.1), channel_id=1, source_target_pairs={{0,16},{16,0},{1,17},{17,1},{2,18},{18,2},{3,19},{19,3},{4,20},{20... | collective-permute-start | bytes 2162696 | tf_op jit(solution)/shard_map/ppermute | solution.py:68
  714.1 169.3 %collective-permute-start.11 = (bf16[1024,1408]{1,0:T(8,128)(2,1)}, bf16[1024,1408]{1,0:T(8,128)(2,1)}, u32[]{:S(2)}, u32[]{:S(2)}) collective-permute-start(bf16[1024,1408]{1,0:T(8,128)(2,1)} %convolution_convert_fusion), channel_id=1, source_target_pairs={{0,16},{16,0},{1,17},{17,1},{2,18},{18,2},{3,19},{19,3},{4,20},{20... | collective-permute-start | bytes 8650760 | tf_op jit(solution)/shard_map/ppermute | solution.py:68
  716.0 98.0 %copy-start.43 = (f32[2048]{0:T(1024)S(1)}, f32[2048]{0:T(1024)}, u32[]{:S(2)}) copy-start(f32[2048]{0:T(1024)} %get-tuple-element.164) | copy-start | bytes 24580
  815.4 8.0 copy-start.7
  815.5 8.0 copy-start.36
  829.5 7.7 collective-permute-start.7
  831.3 162.8 %collective-permute-start.12 = (bf16[704,2048]{1,0:T(8,128)(2,1)}, bf16[704,2048]{1,0:T(8,128)(2,1)}, u32[]{:S(2)}, u32[]{:S(2)}) collective-permute-start(bf16[704,2048]{1,0:T(8,128)(2,1)} %convolution_convert_fusion.4), channel_id=1, source_target_pairs={{0,16},{16,0},{1,17},{17,1},{2,18},{18,2},{3,19},{19,3},{4,20},{20... | collective-permute-start | bytes 8650760 | tf_op jit(solution)/shard_map/ppermute | solution.py:68
  837.2 147.1 %collective-permute-start.10 = (bf16[1024,1408]{1,0:T(8,128)(2,1)}, bf16[1024,1408]{1,0:T(8,128)(2,1)}, u32[]{:S(2)}, u32[]{:S(2)}) collective-permute-start(bf16[1024,1408]{1,0:T(8,128)(2,1)} %convolution_convert_fusion.1), channel_id=1, source_target_pairs={{0,16},{16,0},{1,17},{17,1},{2,18},{18,2},{3,19},{19,3},{4,20},{20... | collective-permute-start | bytes 8650760 | tf_op jit(solution)/shard_map/ppermute | solution.py:68
  844.8 23.4 %all-to-all-start.2 = ((bf16[16,64,352]{2,1,0:T(8,128)(2,1)}), bf16[16,64,352]{2,1,0:T(8,128)(2,1)S(1)}, u32[]{:S(2)}, u32[]{:S(2)}) async-start(bf16[16,64,352]{2,1,0:T(8,128)(2,1)} %bitcast.56), calls=%async_computation.3 | async-start | bytes 1572864 | tf_op jit(solution)/shard_map/all_to_all | solution.py:108
  858.7 118.0 %collective-permute-start.6 = (bf16[1024,384]{0,1:T(8,128)(2,1)S(1)}, bf16[1024,384]{0,1:T(8,128)(2,1)}, u32[]{:S(2)}, u32[]{:S(2)}) collective-permute-start(bf16[1024,384]{0,1:T(8,128)(2,1)S(1)} %dynamic-slice_convert_fusion), channel_id=1, source_target_pairs={{0,16},{16,0},{1,17},{17,1},{2,18},{18,2},{3,19},{19,3},{4,20},{20... | collective-permute-start | bytes 2359304 | tf_op jit(solution)/shard_map/ppermute | solution.py:68
  869.9 8.5 copy-start.19
  883.3 93.4 %copy-start.11 = (f32[2048,384]{0,1:T(8,128)S(1)}, f32[2048,384]{0,1:T(8,128)}, u32[]{:S(2)}) copy-start(f32[2048,384]{0,1:T(8,128)} %copy-done.10) | copy-start | bytes 9437188
  979.2 24.9 %all-to-all-start.1 = ((bf16[16,64,384]{2,1,0:T(8,128)(2,1)}), bf16[16,64,384]{2,1,0:T(8,128)(2,1)S(1)}, u32[]{:S(2)}, u32[]{:S(2)}) async-start(bf16[16,64,384]{2,1,0:T(8,128)(2,1)} %bitcast.49), calls=%async_computation.2 | async-start | bytes 1572864 | tf_op jit(solution)/shard_map/all_to_all | solution.py:108
  984.3 9.8 copy-start.8
  984.4 9.8 copy-start.37
  (25 other events, 121.4 us)
Sparse Core Ops, SparseCore 0:
  10.2 125.0 all-gather.5
  138.1 99.4 all-gather.3
  587.1 82.2 all-gather.7
  673.3 127.6 reduce-scatter.1

commit v6 on v5

--- a/solution.py
+++ b/solution.py
@@ -624,14 +624,14 @@
 
 
 def project_kernel(
-    x_ref, weight_ref, lup_ref, gain_ref, gain_lat_ref, cos_ref, sin_ref,
+    x_ref, down_ref, weight_ref, lup_ref, gain_ref, gain_lat_ref, cos_ref, sin_ref,
     h_ref, query_ref, key_ref, value_ref, latent_ref, normed_ref, factor_ref,
 ):
     x = x_ref[...].astype(f32)
     factor = lax.rsqrt(jnp.mean(x * x, axis=-1, keepdims=True) + epsilon)
     h = (x * factor * gain_ref[...]).astype(bf16)
     h_ref[...] = h
-    raw = matmul(h, weight_ref[...], COLS_ROWS)
+    raw = matmul(h, down_ref[...], COLS_ROWS)
     low = raw[:, :RANK]
     factor = lax.rsqrt(jnp.mean(low * low, axis=-1, keepdims=True) + epsilon)
     normed = low * factor
@@ -642,14 +642,15 @@
     expanded = matmul(latent, lup_ref[...], COLS_ROWS)
     rope = turn(raw[:, RANK : RANK + 128], cos_ref[...], sin_ref[...])
     lane = lax.broadcasted_iota(jnp.int32, rope.shape, 1)
-    query_ref[:, :HD] = raw[:, RANK + 128 :].astype(bf16)
-    query_ref[:, HD:] = jnp.where(lane < RD, pltpu.roll(rope, 64, 1), 0.0).astype(bf16)
+    raw = matmul(h, weight_ref[...], COLS_ROWS)
+    query_ref[:, :HD] = raw[:, :HD].astype(bf16)
+    query_ref[:, HD:] = turn(raw[:, HD:], cos_ref[...], sin_ref[...]).astype(bf16)
     key_ref[:, :HD] = expanded[:, :HD].astype(bf16)
     key_ref[:, HD:] = jnp.where(lane < RD, rope, 0.0).astype(bf16)
     value_ref[...] = expanded[:, HD:].astype(bf16)
 
 
-def project(x_all, weight, lup, gain, gain_lat, cosine, sine):
+def project(x_all, down, weight, lup, gain, gain_lat, cosine, sine):
     tokens, width = x_all.shape
     tile = 256
     outs = [
@@ -667,6 +668,7 @@
         grid=(tokens // tile,),
         in_specs=[
             tiled(tile, width),
+            full(down.shape),
             full(weight.shape),
             full(lup.shape),
             full((1, width)),
@@ -676,8 +678,8 @@
         ],
         out_specs=[tiled(tile, s[1]) for s, _ in outs],
         out_shape=[jax.ShapeDtypeStruct(s, d) for s, d in outs],
-        cost_estimate=estimate(2 * tokens * width * (weight.shape[1] + 64), 5 * tokens * width),
-    )(x_all, weight, lup, gain[None], gain_lat[None], cosine, sine)
+        cost_estimate=estimate(2 * tokens * width * 1000, 5 * tokens * width),
+    )(x_all, down, weight, lup, gain[None], gain_lat[None], cosine, sine)
 
 
 def attend_kernel(scale, query_ref, key_ref, value_ref, row_ref, col_ref, probs_ref, out_ref):
@@ -793,14 +795,13 @@
 
 
 def project_back_kernel(
-    dq_ref, dkv_ref, weight_ref, lup_ref, gain_lat_ref, cos_ref, sin_ref,
-    latent_ref, normed_ref, factor_ref, joint_ref, h_ref, lup_grad_ref, gain_grad_ref,
+    dq_ref, dkv_ref, down_ref, weight_ref, lup_ref, gain_lat_ref, cos_ref, sin_ref,
+    latent_ref, normed_ref, factor_ref, down_grad_ref, query_grad_ref, h_ref, lup_grad_ref, gain_grad_ref,
 ):
     dq = dq_ref[...]
     dkv = dkv_ref[...]
-    lane = lax.broadcasted_iota(jnp.int32, (dq.shape[0], 128), 1)
-    rope = jnp.where(lane < RD, dkv[:, HD : HD + 128], pltpu.roll(dq[:, HD:], 64, 1))
-    rope = turn(rope, cos_ref[...], -sin_ref[...])
+    key_rope = turn(dkv[:, HD : HD + 128], cos_ref[...], -sin_ref[...])
+    query_rope = turn(dq[:, HD:], cos_ref[...], -sin_ref[...])
     expanded = jnp.concatenate([dkv[:, :HD], dkv[:, HD + 128 :]], axis=1).astype(bf16)
     latent_grad = matmul(expanded, lup_ref[...], COLS_COLS)
     normed = normed_ref[...]
@@ -816,14 +817,17 @@
     down = factor_ref[...] * (
         scaled - normed * jnp.mean(scaled * normed, axis=-1, keepdims=True)
     )
-    joint = jnp.concatenate([down, rope, dq[:, :HD]], axis=1).astype(bf16)
-    joint_ref[...] = joint
-    h_ref[...] = matmul(joint, weight_ref[...], COLS_COLS).astype(bf16)
-
-
-def project_back(dq, dkv, weight, lup, gain_lat, cosine, sine, latent, normed, factor):
+    down = jnp.concatenate([down, key_rope], axis=1).astype(bf16)
+    query = jnp.concatenate([dq[:, :HD], query_rope], axis=1).astype(bf16)
+    down_grad_ref[...] = down
+    query_grad_ref[...] = query
+    back = matmul(down, down_ref[...], COLS_COLS) + matmul(query, weight_ref[...], COLS_COLS)
+    h_ref[...] = back.astype(bf16)
+
+
+def project_back(dq, dkv, down, weight, lup, gain_lat, cosine, sine, latent, normed, factor):
     tokens = dq.shape[0]
-    width, joint = weight.shape
+    width = weight.shape[0]
     tile = 256
     return pl.pallas_call(
         project_back_kernel,
@@ -832,6 +836,7 @@
         in_specs=[
             tiled(tile, dq.shape[1]),
             tiled(tile, dkv.shape[1]),
+            full(down.shape),
             full(weight.shape),
             full(lup.shape),
             full((1, RANK)),
@@ -842,19 +847,21 @@
             tiled(tile, 1),
         ],
         out_specs=[
-            tiled(tile, joint),
+            tiled(tile, down.shape[1]),
+            tiled(tile, weight.shape[1]),
             tiled(tile, width),
             pl.BlockSpec(lup.shape, lambda i: (0, 0)),
             pl.BlockSpec((1, RANK), lambda i: (0, 0)),
         ],
         out_shape=[
-            jax.ShapeDtypeStruct((tokens, joint), bf16),
+            jax.ShapeDtypeStruct((tokens, down.shape[1]), bf16),
+            jax.ShapeDtypeStruct((tokens, weight.shape[1]), bf16),
             jax.ShapeDtypeStruct((tokens, width), bf16),
             jax.ShapeDtypeStruct(lup.shape, f32),
             jax.ShapeDtypeStruct((1, RANK), f32),
         ],
-        cost_estimate=estimate(2 * tokens * width * joint * 1.2, 6 * tokens * width),
-    )(dq, dkv, weight, lup, gain_lat[None], cosine, sine, latent, normed, factor)
+        cost_estimate=estimate(2 * tokens * width * 1000, 6 * tokens * width),
+    )(dq, dkv, down, weight, lup, gain_lat[None], cosine, sine, latent, normed, factor)
 
 
 def per_device(
@@ -933,7 +940,6 @@
     small_all, x_all, *swapped = ring_gather(
         [small, x_low], [query_parts, lup_parts], 1, replicas == 2
     )
-    ldown_all = small_all[:, : RANK + RD]
     router_all = small_all[:, RANK + RD : RANK + RD + experts]
     gains = small_all[:, RANK + RD + experts :].astype(f32)
     gain_attn = gains[:, 0]
@@ -946,7 +952,7 @@
             return dp_gather(value)
         return ordered(value, swapped[at + 2][:, :cut].reshape(groups * cut, -1))
 
-    wq = all_rows(0, rows)
+    wq = jnp.pad(all_rows(0, rows), ((0, 0), (0, 128 - RD)))
     lup = all_rows(1, lup_rows)
     code = swapped[1][:, lup_rows, :own].astype(f32).reshape(tokens)
 
@@ -965,7 +971,8 @@
     gate_w = dp_gather(expert_gate[0])
     up_w = dp_gather(expert_up[0])
     down_w = dp_gather(expert_down[0])
-    out_t = gather_rows(output_weight.T, BOTH)
+    out_rows = dp_gather(output_weight.T)
+    out_t = gather_rows(out_rows, EXPERT)
 
     at_block = jnp.arange(groups, dtype=jnp.int32)[:, None, None] * span
     positions = jnp.broadcast_to(
@@ -974,14 +981,15 @@
     cosine, sine = angle_tables(positions, RD)
     cosine = jnp.concatenate([cosine] * 4, axis=1)
     sine = jnp.concatenate([-sine, sine] * 2, axis=1)
-    joint_weight = jnp.concatenate([ldown_all, wq[:, HD:], wq[:, :HD]], axis=1)
     h_one, query, key, value, latent, normed_lat, factor_lat = project(
-        x_all, joint_weight, lup, gain_attn, gain_lat, cosine, sine
+        x_all, small_all, wq, lup, gain_attn, gain_lat, cosine, sine
     )
     probs_attn, heads_s = attend(query, key, value, segments, scale, groups, seqs, span)
     heads_own = heads_to_tokens(heads_s, span, 3).reshape(own, HEADS * VD)
 
-    x_second = x_low.astype(f32) + right_product(heads_own, out_t)
+    x_second = x_low.astype(f32) + right_product(heads_own, out_t).reshape(
+        own, groups, replicas, rows
+    ).transpose(0, 2, 1, 3).reshape(own, width)
     normed_two, factor_two = norm_parts(x_second)
     (h_two,) = ring_gather([(normed_two * gain_moe).astype(bf16)], [], 2)
 
@@ -1021,7 +1029,8 @@
     gate_pre = product(expert_in, gate_w)
     up_pre = product(expert_in, up_w)
     expert_hidden = (jax.nn.silu(gate_pre) * up_pre).astype(bf16)
-    expert_out = product(expert_hidden, down_w).astype(bf16).astype(f32)
+    expert_out = product(expert_hidden, down_w).astype(bf16)
+    expert_out = lax.optimization_barrier(expert_out).astype(f32)
     partial = combine(
         select, (slot_prob * expert_out).astype(bf16), shared_hidden, sdown, COLS_ROWS
     )
@@ -1057,7 +1066,8 @@
     gmoe_grad = jnp.sum(h_two_grad * normed_two, axis=0)
     x_second_grad = cot_own.astype(f32) + norm_back(h_two_grad * gain_moe, normed_two, factor_two)
     attn_low = x_second_grad.astype(bf16)
-    heads_grad = product(attn_low, out_t).astype(bf16)
+    low_parts = attn_low.reshape(own, replicas, groups, rows).transpose(0, 2, 1, 3)
+    heads_grad = product(low_parts.reshape(own, width), out_t).astype(bf16)
     grad_s = tokens_to_heads(heads_grad.reshape(seqs, span, HEADS * VD), 5)
     low_all = gather_rows(attn_low, EXPERT)
     gate_up_owned = expert_swap(
@@ -1076,19 +1086,21 @@
     query_grad, pair_grad = attend_back(
         probs_attn, grad_s, heads_s, query, key, value, scale, groups, span
     )
-    joint_grad, h_one_partial, lup_grad, glat_grad = project_back(
-        query_grad, pair_grad, joint_weight, lup, gain_lat, cosine, sine,
+    down_grad, head_grad, h_one_partial, lup_grad, glat_grad = project_back(
+        query_grad, pair_grad, small_all, wq, lup, gain_lat, cosine, sine,
         latent, normed_lat, factor_lat,
     )
-    joint_weight_grad = left_product(h_one, joint_grad)
-    gattn_grad = jnp.sum(joint_weight_grad * joint_weight.astype(f32), axis=1) / gain_attn
+    small_grad = left_product(h_one, down_grad)
+    head_grad = left_product(h_one, head_grad)
+    gattn_grad = jnp.sum(small_grad * small_all.astype(f32), axis=1)
+    gattn_grad = (gattn_grad + jnp.sum(head_grad * wq.astype(f32), axis=1)) / gain_attn
     out_grad = left_product(low_all, by_block(heads_s))
     down_at = RANK + RD
     back_grad = jnp.concatenate(
         [
-            joint_weight_grad[:, down_at + RD :],
+            head_grad[:, :HD],
             out_grad,
-            joint_weight_grad[:, down_at : down_at + RD],
+            head_grad[:, HD : HD + RD],
             lup_grad.reshape(width, -1),
         ],
         axis=1,
@@ -1105,28 +1117,21 @@
     glat_column = jnp.pad(
         glat_grad.reshape(-1, latent_gain.shape[0]), ((0, 0), (0, pad))
     ).reshape(-1)
-    lane = jnp.arange(128, dtype=jnp.int32)
-    small_grad = jnp.pad(router_grad, ((0, 0), (0, 128 - experts)))
+    lane = jnp.arange(small_grad.shape[1], dtype=jnp.int32)
+    small_grad = small_grad + jnp.pad(
+        router_grad, ((0, 0), (down_at, small_grad.shape[1] - down_at - experts))
+    )
     for at_lane, column in enumerate((gattn_grad, gmoe_grad, glat_column)):
-        small_grad = jnp.where(lane == experts + at_lane, column[:, None], small_grad)
+        small_grad = jnp.where(lane == down_at + experts + at_lane, column[:, None], small_grad)
 
     def by_row_owner(value):
         return value.astype(bf16).reshape(replicas, groups, rows, -1)
 
-    ldown_owned, small_owned, h_one_grad = ring_scatter(
-        [
-            by_row_owner(joint_weight_grad[:, :down_at]),
-            by_row_owner(small_grad),
-            by_owner(h_one_partial),
-        ],
-        6,
-    )
+    small_owned, h_one_grad = ring_scatter([by_row_owner(small_grad), by_owner(h_one_partial)], 6)
     normed_own, factor_own = norm_parts(x_low.astype(f32))
     input_grad = x_second_grad + norm_back(h_one_grad * gain_attn, normed_own, factor_own)
     input_grad = input_grad.astype(bf16).reshape(seqs, span, width)
-    small_owned = dp_scatter(
-        jnp.concatenate([ldown_owned, small_owned], axis=2).reshape(replicas * rows, -1)
-    )
+    small_owned = dp_scatter(small_owned.reshape(replicas * rows, -1))
     ldown_owned = small_owned[:, :down_at]
     router_owned = small_owned[:, down_at : down_at + experts]
     gain_owned = small_owned[:, down_at + experts :]

time: 1020 us -> 989 us (0.970)
  Pallas kernels: 531 us -> 498 us
  other arithmetic: 92.2 us -> 79.7 us
    pallas_call x2, Pallas kernels: 272 us -> 243 us  [ring_gather(): pl.pallas_call(functools.partial(gather_kernel, k, m, mirrored), out_shap...]
    concatenate x3 -> x1, other arithmetic: 14.8 us -> 0.34 us  [per_device(): jnp.concatenate([head_grad[:, :HD], out_grad, head_grad[:, HD:HD + RD], l...]
    dot_general x10 -> x11, matrix products: 75.3 us -> 83.3 us  [left_product(): lax.dot_general(left, right, (((0,), (0,)), ((), ())), preferred_element_...]
    ppermute x13 -> x14, waiting for transfers between devices: 88.6 us -> 90.1 us  [dp_swap(): return lax.ppermute(value, DP, [(0, 1), (1, 0)])]
  transfers between devices with their start and end apart: 20 -> 21, of which waited for: 3 -> 4; matrix products, arithmetic and copies ran while one was open for 22% -> 22% of each run, Pallas kernels for 40% -> 38%
where the time goes in v6:
time: 989 us; the launch traced here: 983 us
  Pallas kernels  498 us (50%)
  matrix products  181 us (18%)
  waiting for transfers between devices  97.9 us (10%)
  other arithmetic  79.7 us (8%)
  local copies, waits for them, and re-layouts  76.8 us (8%)
  starting transfers between devices  34.7 us (4%)
  between operations  15.1 us (2%)
    pallas_call x2, Pallas kernels, ring_gather(): pl.pallas_call(functools.partial(gather_kernel, k, m, mirrored), out_shap...  243 us
    pallas_call x2, Pallas kernels, ring_scatter(): pl.pallas_call(functools.partial(scatter_kernel, count), out_shape=[jax.S...  148 us
    ppermute x14, waiting for transfers between devices, dp_swap(): return lax.ppermute(value, DP, [(0, 1), (1, 0)])  90.1 us
    dot_general x11, matrix products, left_product(): lax.dot_general(left, right, (((0,), (0,)), ((), ())), preferred_element_...  83.3 us
    dot_general x5, matrix products, right_product(): lax.dot_general(left, right, (((1,), (1,)), ((), ())), preferred_element_...  48.4 us
    dot_general x5, matrix products, product(): return jnp.dot(left, right, preferred_element_type=f32)  36.2 us
    pallas_call x2, Pallas kernels, swap_call(): pl.pallas_call(functools.partial(swap_kernel, source, target), out_shape=...  29.6 us
    pallas_call x2, Pallas kernels, combine(): pl.pallas_call(functools.partial(combine_kernel, dims), grid=(chunks, per...  23.6 us
  transfers between devices with their start and end apart: 21, of which 4 were waited for; matrix products, arithmetic and copies ran while one was open for 22% of the time, Pallas kernels for 38%

profile of v6, /device:TPU:0, one launch (start us, length us, event | category | flops | bytes accessed | tf_op | source)
XLA Modules:
  0.0 982.7 jit_solution(10020971726932126627)
XLA Ops:
  11.1 6.5 collective-permute-done.1
  28.2 6.2 all-to-all-start
  47.4 3.7 fusion.38
  55.7 187.7 %shard_map.306 = (bf16[2,16,64,640]{3,2,1,0:T(8,128)(2,1)}, bf16[16,128,2048]{2,1,0:T(8,128)(2,1)}, bf16[16,64,192]{2,1,0:T(8,128)(2,1)}, bf16[16,32,256]{2,1,0:...) custom-call(bf16[2,64,640]{2,1,0:T(8,128)(2,1)} %bitcast.222, bf16[128,2048]{1,0:T(8,128)(2,1)} %bitcast.183, ...), custom_call_target="tpu_custom_call" | custom-call | bytes 175636480 | tf_op jit(solution)/shard_map/pallas_call | solution.py:327
  251.6 18.6 %project.1 = (bf16[2048,2048]{1,0:T(8,128)(2,1)}, bf16[2048,256]{1,0:T(8,128)(2,1)}, bf16[2048,256]{1,0:T(8,128)(2,1)}, bf16[2048,128]{1,0:T(8,128)(2,1)}, bf16[...) custom-call(bf16[2048,2048]{1,0:T(8,128)(2,1)} %bitcast.249, bf16[2048,640]{1,0:T(8,128)(2,1)} %bitcast.232, ...), custom_call_target="tpu_custom_call" | custom-call | flops 8388608000 | bytes 20971520 | tf_op jit(solution)/shard_map/project/pallas_call | solution.py:665
  274.1 7.7 attend.1
  281.7 15.5 %shard_map.307 = bf16[2,64,2048]{2,1,0:T(8,128)(2,1)} custom-call(bf16[2,1024,128]{2,1,0:T(8,128)(2,1)} %get-tuple-element.49.x_ref.out_ref), custom_call_target="tpu_custom_call" | custom-call | bytes 33554432 | tf_op jit(solution)/shard_map/pallas_call | solution.py:532
  303.1 4.9 broadcast_select_fusion.1
  308.0 4.9 broadcast_select_fusion.3
  312.9 4.7 broadcast_select_fusion.5
  317.7 7.3 convolution_convert_fusion.2
  325.0 5.8 multiply_reduce_fusion.6
  332.9 55.6 %shard_map.308 = bf16[16,128,2048]{2,1,0:T(8,128)(2,1)} custom-call(bf16[128,2048]{1,0:T(8,128)(2,1)} %multiply_convert_fusion.7.refs_0_), custom_call_target="tpu_custom_call" | custom-call | bytes 125829120 | tf_op jit(solution)/shard_map/pallas_call | solution.py:327
  388.5 7.8 fusion.63
  399.2 5.6 convolution_convert_fusion.3
  404.8 7.3 fusion.9
  412.1 9.6 multiply_convert_fusion.2
  421.8 6.0 fusion.10
  434.4 7.5 fusion.1
  442.0 16.0 %multiply_convert_fusion.1 = (bf16[864,1408]{1,0:T(8,128)(2,1)}, bf16[864,1408]{1,0:T(8,128)(2,1)}) fusion(f32[864,1408]{1,0:T(8,128)} %fusion.9, f32[864,1408]{1,0:T(8,128)} %get-tuple-element.206, bf16[864,2048]{1,0:T(8,128)(2,1)S(1)} %get-tuple-element.201, bf16[704,2048]{1,0:T(8,128)(2,1)} %get-tuple-element.170, bf16[704,2048]{1,0:T(8,128)(2,1)} %get-tuple-element.169), kind=kOutput, calls=%fused_computation.16 | convolution fusion | flops 5010182144 | bytes 23904256 | tf_op jit(solution)/shard_map/dot_general | solution.py:39
  458.0 10.8 %fusion.6 = f32[864,2048]{1,0:T(8,128)} fusion(bf16[864,1408]{1,0:T(8,128)(2,1)} %get-tuple-element.168, bf16[1024,1408]{1,0:T(8,128)(2,1)} %get-tuple-element.174, bf16[1024,1408]{1,0:T(8,128)(2,1)} %get-tuple-element.173), kind=kOutput, calls=%fused_computation.24 | convolution fusion | flops 4994367488 | bytes 15278080 | tf_op jit(solution)/shard_map/dot_general | solution.py:39
  468.8 11.6 %add_convert_fusion = bf16[864,2048]{1,0:T(8,128)(2,1)} fusion(f32[864,2048]{1,0:T(8,128)} %fusion.6, bf16[864,1408]{1,0:T(8,128)(2,1)} %get-tuple-element.167, bf16[1024,1408]{1,0:T(8,128)(2,1)} %get-tuple-element.172, bf16[1024,1408]{1,0:T(8,128)(2,1)} %get-tuple-element.171), kind=kOutput, calls=%fused_computation.6 | convolution fusion | flops 4997906432 | bytes 18817024 | tf_op jit(solution)/shard_map/dot_general | solution.py:39
  480.4 4.3 multiply_convert_fusion.4
  486.6 12.7 %shard_map.310 = bf16[2048,2048]{1,0:T(8,128)(2,1)} custom-call(bf16[4,216,512]{2,1,0:T(8,128)(2,1)} %copy-done.5, bf16[4,216,2048]{2,1,0:T(8,128)(2,1)} %bitcast.252, bf16[2048,368]{1,0:T(8,128)(2,1)} %pad_maximum_fusion.15.left_ref, bf16[2048,368]{1,0:T(8,128)(2,1)} %pad_maximum_fusion.14.right_ref), custom_call_target="tpu_custom_call" | custom-call | flops 4898947072 | bytes 16777216 | tf_op jit(solution)/shard_map/pallas_call | solution.py:603
  499.3 54.8 %shard_map.311 = f32[128,2048]{1,0:T(8,128)} custom-call(bf16[16,128,2048]{2,1,0:T(8,128)(2,1)} %bitcast.187), custom_call_target="tpu_custom_call" | custom-call | bytes 125829120 | tf_op jit(solution)/shard_map/pallas_call | solution.py:494
  561.2 6.9 fusion.65
  572.1 5.5 convolution_convert_fusion.5
  577.6 14.1 %shard_map.312.grad_ref = bf16[2,1024,128]{2,1,0:T(8,128)(2,1)} custom-call(bf16[2,64,2048]{2,1,0:T(8,128)(2,1)} %bitcast.212), custom_call_target="tpu_custom_call" | custom-call | bytes 33554432 | tf_op jit(solution)/shard_map/pallas_call | solution.py:532
  591.7 7.1 attend_back.1
  598.9 10.9 %shard_map.309 = bf16[2048,2048]{1,0:T(8,128)(2,1)} custom-call(bf16[4,216,512]{2,1,0:T(8,128)(2,1)} %copy-done.5, bf16[4,216,2048]{2,1,0:T(8,128)(2,1)} %bitcast.185, bf16[2048,176]{1,0:T(8,128)(2,1)} %get-tuple-element.177.left_ref, bf16[176,2048]{1,0:T(8,128)(2,1)} %pad_maximum_fusion.19.right_ref), custom_call_target="tpu_custom_call" | custom-call | flops 3288334336 | bytes 16777216 | tf_op jit(solution)/shard_map/pallas_call | solution.py:603
  609.8 19.4 %project_back.1 = (bf16[2048,640]{1,0:T(8,128)(2,1)}, bf16[2048,256]{1,0:T(8,128)(2,1)}, bf16[2048,2048]{1,0:T(8,128)(2,1)}, f32[512,256]{1,0:T(8,128)}, f32[1,512]{1,0:T(1,128)}) custom-call(f32[2048,256]{1,0:T(8,128)} %bitcast.251, f32[2048,384]{1,0:T(8,128)} %bitcast.250, bf16[2048,640]{1,0:T(8,128)(2,1)} %bitcast.234, ...), custom_call_target="tpu_custom_call" | custom-call | flops 8388608000 | bytes 25165824 | tf_op jit(solution)/shard_map/project_back/pallas_call | solution.py:832
  629.2 6.1 fusion.64
  639.7 5.4 fusion.67
  657.2 12.2 %multiply_reduce_fusion = (f32[2048]{0:T(1024)S(1)}, f32[2048,640]{1,0:T(8,128)}) fusion(bf16[2,16,64,640]{3,2,1,0:T(8,128)(2,1)S(1)} %copy-done.44, bf16[2048,2048]{1,0:T(8,128)(2,1)} %get-tuple-element.57, bf16[2048,640]{1,0:T(8,128)(2,1)} %get-tuple-element.58), kind=kOutput, calls=%fused_computation.14 | convolution fusion | flops 5372639232 | bytes 18882560 | tf_op jit(solution)/shard_map/dot_general | solution.py:35
  670.9 8.2 convolution_convert_fusion
  681.2 5.3 select_convert_fusion
  686.5 93.4 %shard_map.313 = (f32[2,64,640]{2,1,0:T(8,128)}, f32[128,2048]{1,0:T(8,128)}) custom-call(bf16[2,16,64,640]{3,2,1,0:T(8,128)(2,1)} %bitcast.186, bf16[16,128,2048]{2,1,0:T(8,128)(2,1)} %bitcast.188), custom_call_target="tpu_custom_call" | custom-call | bytes 165150720 | tf_op jit(solution)/shard_map/pallas_call | solution.py:494
  781.5 8.0 convolution_convert_fusion.1
  789.5 5.2 convolution_convert_fusion.4
  809.6 5.3 all-to-all-start.2
  817.0 4.9 fusion.66
  826.4 7.1 all-to-all-done.2
  851.8 9.7 add_bitcast_fusion.1
  861.6 83.1 %collective-permute-done.7 = bf16[1024,384]{0,1:T(8,128)(2,1)} collective-permute-done((bf16[1024,384]{0,1:T(8,128)(2,1)}, bf16[1024,384]{0,1:T(8,128)(2,1)}, u32[]{:S(2)}, u32[]{:S(2)}) %collective-permute-start.7) | collective-permute-done | bytes 786464 | tf_op jit(solution)/shard_map/ppermute | solution.py:68
  947.2 4.7 all-to-all-start.1
  951.9 9.7 add_bitcast_fusion.2
  961.6 7.0 add_bitcast_fusion
  968.6 3.3 fusion.33
  (312 shorter events, 142.1 us)
Async XLA Ops:
  7.2 12.3 %copy-start.62 = (bf16[16]{0:T(256)(128)(2,1)S(1)}, bf16[16]{0:T(256)(128)(2,1)}, u32[]{:S(2)}) copy-start(bf16[16]{0:T(256)(128)(2,1)} %param.29) | copy-start | bytes 100
  7.2 12.4 %copy-start.59 = (bf16[64]{0:T(256)(128)(2,1)S(1)}, bf16[64]{0:T(256)(128)(2,1)}, u32[]{:S(2)}) copy-start(bf16[64]{0:T(256)(128)(2,1)} %param.28) | copy-start | bytes 388
  7.2 12.5 %copy-start.57 = (bf16[64,16]{0,1:T(8,128)(2,1)S(1)}, bf16[64,16]{0,1:T(8,128)(2,1)}, u32[]{:S(2)}) copy-start(bf16[64,16]{0,1:T(8,128)(2,1)} %param.30) | copy-start | bytes 6148
  7.2 12.6 %copy-start.60 = (bf16[64]{0:T(256)(128)(2,1)S(1)}, bf16[64]{0:T(256)(128)(2,1)}, u32[]{:S(2)}) copy-start(bf16[64]{0:T(256)(128)(2,1)} %param.34) | copy-start | bytes 388
  7.2 12.7 %copy-start.50 = (bf16[64,576]{1,0:T(8,128)(2,1)S(1)}, bf16[64,576]{1,0:T(8,128)(2,1)}, u32[]{:S(2)}) copy-start(bf16[64,576]{1,0:T(8,128)(2,1)} %param.25) | copy-start | bytes 221188
  7.2 15.5 %copy-start.46 = (bf16[64,2816]{1,0:T(8,128)(2,1)S(1)}, bf16[64,2816]{1,0:T(8,128)(2,1)}, u32[]{:S(2)}) copy-start(bf16[64,2816]{1,0:T(8,128)(2,1)} %param.31) | copy-start | bytes 1081348
  7.2 310.4 %all-gather.6.cloned.1.call-start = ((), (), s32[]{:S(2)}) async-start(), calls=%async_computation.6 | async-start | bytes 8912896 | tf_op jit(solution)/shard_map/all_gather | solution.py:112
  8.0 16.8 %copy-start.47 = (bf16[64,2816]{1,0:T(8,128)(2,1)S(1)}, bf16[64,2816]{1,0:T(8,128)(2,1)}, u32[]{:S(2)}) copy-start(bf16[64,2816]{1,0:T(8,128)(2,1)} %param.32) | copy-start | bytes 1081348
  8.0 317.0 %all-gather.4.cloned.1.call-start = ((), (), s32[]{:S(2)}) async-start(), calls=%async_computation.4 | async-start | bytes 8912896 | tf_op jit(solution)/shard_map/all_gather | solution.py:112
  8.0 9.5 collective-permute-start.1
  20.7 33.4 %collective-permute-start = (bf16[64,640]{1,0:T(8,128)(2,1)}, bf16[64,640]{1,0:T(8,128)(2,1)}, u32[]{:S(2)}, u32[]{:S(2)}) collective-permute-start(bf16[64,640]{1,0:T(8,128)(2,1)} %concatenate.54), channel_id=1, source_target_pairs={{0,16},{16,0},{1,17},{17,1},{2,18},{18,2},{3,19},{19,3},{4,20},{20... | collective-permute-start | bytes 245768 | tf_op jit(solution)/shard_map/ppermute | solution.py:68
  22.4 274.8 %collective-permute-start.6 = (bf16[88,2048]{1,0:T(8,128)(2,1)}, bf16[88,2048]{1,0:T(8,128)(2,1)}, u32[]{:S(2)}, u32[]{:S(2)}) collective-permute-start(bf16[88,2048]{1,0:T(8,128)(2,1)} %param.33), channel_id=1, source_target_pairs={{0,16},{16,0},{1,17},{17,1},{2,18},{18,2},{3,19},{19,3},{4,20},{20... | collective-permute-start | bytes 1081352 | tf_op jit(solution)/shard_map/ppermute | solution.py:68
  24.8 13.9 %copy-start.56 = (s32[2,64,6]{1,0,2:T(2,128)S(1)}, s32[2,64,6]{1,0,2:T(2,128)}, u32[]{:S(2)}) copy-start(s32[2,64,6]{1,0,2:T(2,128)} %param.21) | copy-start | bytes 9220
  26.1 12.7 %copy-start.61 = (s32[2,64]{1,0:T(2,128)S(1)}, s32[2,64]{1,0:T(2,128)}, u32[]{:S(2)}) copy-start(s32[2,64]{1,0:T(2,128)} %param.22) | copy-start | bytes 1540
  26.1 13.6 %copy-start.54 = (s32[2,1024]{1,0:T(2,128)S(1)}, s32[2,1024]{1,0:T(2,128)}, u32[]{:S(2)}) copy-start(s32[2,1024]{1,0:T(2,128)} %param.20) | copy-start | bytes 24580
  26.1 14.2 %copy-start.49 = (bf16[16,4096]{1,0:T(8,128)(2,1)S(1)}, bf16[16,4096]{1,0:T(8,128)(2,1)}, u32[]{:S(2)}) copy-start(bf16[16,4096]{1,0:T(8,128)(2,1)} %param.26) | copy-start | bytes 393220
  26.2 14.2 %copy-start.45 = (bf16[64,3072]{1,0:T(8,128)(2,1)S(1)}, bf16[64,3072]{1,0:T(8,128)(2,1)}, u32[]{:S(2)}) copy-start(bf16[64,3072]{1,0:T(8,128)(2,1)} %param.24) | copy-start | bytes 1179652
  27.0 16.3 %copy-start = (bf16[2,64,2048]{2,1,0:T(8,128)(2,1)S(1)}, bf16[2,64,2048]{2,1,0:T(8,128)(2,1)}, u32[]{:S(2)}) copy-start(bf16[2,64,2048]{2,1,0:T(8,128)(2,1)} %param.19) | copy-start | bytes 1572868
  28.2 242.0 %all-to-all-start = ((bf16[16,64,352]{2,1,0:T(8,128)(2,1)}), bf16[16,64,352]{2,1,0:T(8,128)(2,1)S(1)}, u32[]{:S(2)}, u32[]{:S(2)}) async-start(bf16[16,64,352]{2,1,0:T(8,128)(2,1)} %pad_maximum_fusion.18), calls=%async_computation | async-start | bytes 1572864 | tf_op jit(solution)/shard_map/all_to_all | solution.py:108
  34.4 782.6 %all-gather.8.cloned.1.call-start = ((), (), s32[]{:S(2)}) async-start(), calls=%async_computation.7 | async-start | bytes 8912896 | tf_op jit(solution)/shard_map/all_gather | solution.py:112
  35.0 267.5 %collective-permute-start.5 = (bf16[704,2048]{1,0:T(8,128)(2,1)}, bf16[704,2048]{1,0:T(8,128)(2,1)}, u32[]{:S(2)}, u32[]{:S(2)}) collective-permute-start(bf16[704,2048]{1,0:T(8,128)(2,1)} %bitcast.208), channel_id=1, source_target_pairs={{0,16},{16,0},{1,17},{17,1},{2,18},{18,2},{3,19},{19,3},{4,20},{20... | collective-permute-start | bytes 8650760 | tf_op jit(solution)/shard_map/ppermute | solution.py:68
  36.6 271.4 %collective-permute-start.4 = (bf16[1024,1408]{1,0:T(8,128)(2,1)}, bf16[1024,1408]{1,0:T(8,128)(2,1)}, u32[]{:S(2)}, u32[]{:S(2)}) collective-permute-start(bf16[1024,1408]{1,0:T(8,128)(2,1)} %bitcast.209), channel_id=1, source_target_pairs={{0,16},{16,0},{1,17},{17,1},{2,18},{18,2},{3,19},{19,3},{4,20},{20... | collective-permute-start | bytes 8650760 | tf_op jit(solution)/shard_map/ppermute | solution.py:68
  37.1 275.8 %collective-permute-start.3 = (bf16[1024,1408]{1,0:T(8,128)(2,1)}, bf16[1024,1408]{1,0:T(8,128)(2,1)}, u32[]{:S(2)}, u32[]{:S(2)}) collective-permute-start(bf16[1024,1408]{1,0:T(8,128)(2,1)} %bitcast.210), channel_id=1, source_target_pairs={{0,16},{16,0},{1,17},{17,1},{2,18},{18,2},{3,19},{19,3},{4,20},{20... | collective-permute-start | bytes 8650760 | tf_op jit(solution)/shard_map/ppermute | solution.py:68
  270.6 28.7 %collective-permute-start.2 = (bf16[1024,352]{0,1:T(8,128)(2,1)S(1)}, bf16[1024,352]{0,1:T(8,128)(2,1)}, u32[]{:S(2)}, u32[]{:S(2)}) collective-permute-start(bf16[1024,352]{0,1:T(8,128)(2,1)S(1)} %copy.221), channel_id=1, source_target_pairs={{0,16},{16,0},{1,17},{17,1},{2,18},{18,2},{3,19},{19,3},{4,20},{20... | collective-permute-start | bytes 2162696 | tf_op jit(solution)/shard_map/ppermute | solution.py:68
  272.5 158.2 %copy-start.5 = (bf16[4,216,512]{2,1,0:T(8,128)(2,1)}, bf16[4,216,512]{2,1,0:T(8,128)(2,1)S(1)}, u32[]{:S(2)}) copy-start(bf16[4,216,512]{2,1,0:T(8,128)(2,1)S(1)} %and_convert_fusion.select_ref) | copy-start | bytes 2654212
  442.0 16.0 %copy-start.8 = (bf16[864,2048]{1,0:T(8,128)(2,1)}, bf16[864,2048]{1,0:T(8,128)(2,1)S(1)}, u32[]{:S(2)}) copy-start(bf16[864,2048]{1,0:T(8,128)(2,1)S(1)} %get-tuple-element.201) | copy-start | bytes 10616836
  442.0 38.4 %slice-start = ((s8[8388608]{0:T(1024)(128)(4,1)}), s8[4194304]{0:T(1024)(128)(4,1)S(1)}, s32[]{:S(2)}) async-start(s8[8388608]{0:T(1024)(128)(4,1)} %bitcast.178), calls=%async_computation.8 | async-start | bytes 8388608
  458.0 22.4 %slice-start.1 = ((s8[8388608]{0:T(1024)(128)(4,1)}), s8[4194304]{0:T(1024)(128)(4,1)S(1)}, s32[]{:S(2)}) async-start(s8[8388608]{0:T(1024)(128)(4,1)} %bitcast.178), calls=%async_computation.9 | async-start | bytes 8388608
  468.8 11.6 %copy-start.15 = (f32[2048,368]{1,0:T(8,128)S(1)}, f32[2048,368]{1,0:T(8,128)}, u32[]{:S(2)}) copy-start(f32[2048,368]{1,0:T(8,128)} %copy-done.14) | copy-start | bytes 9043972
  468.8 11.6 %copy-start.37 = (bf16[88,2048]{1,0:T(8,128)(2,1)S(1)}, bf16[88,2048]{1,0:T(8,128)(2,1)}, u32[]{:S(2)}) copy-start(bf16[88,2048]{1,0:T(8,128)(2,1)} %get-tuple-element.188) | copy-start | bytes 1081348
  468.8 11.6 %copy-start.38 = (bf16[88,2048]{1,0:T(8,128)(2,1)S(1)}, bf16[88,2048]{1,0:T(8,128)(2,1)}, u32[]{:S(2)}) copy-start(bf16[88,2048]{1,0:T(8,128)(2,1)} %get-tuple-element.189) | copy-start | bytes 1081348
  499.3 56.5 %copy-start.21 = (bf16[2,64,2048]{2,1,0:T(8,128)(2,1)S(1)}, bf16[2,64,2048]{2,1,0:T(8,128)(2,1)}, u32[]{:S(2)}) copy-start(bf16[2,64,2048]{2,1,0:T(8,128)(2,1)} %param.23) | copy-start | bytes 1572868
  557.1 411.5 %reduce-scatter.2.cloned.1.call-start = ((), (), s32[]{:S(2)}) async-start(), calls=%async_computation.5 | async-start | bytes 8912896 | tf_op jit(solution)/shard_map/reduce_scatter | solution.py:116
  647.0 167.9 %collective-permute-start.10 = (bf16[88,2048]{1,0:T(8,128)(2,1)}, bf16[88,2048]{1,0:T(8,128)(2,1)}, u32[]{:S(2)}, u32[]{:S(2)}) collective-permute-start(bf16[88,2048]{1,0:T(8,128)(2,1)} %dynamic-slice_convert_fusion.2), channel_id=1, source_target_pairs={{0,16},{16,0},{1,17},{17,1},{2,18},{18,2},{3,19},{19,3},{4,20},{20... | collective-permute-start | bytes 1081352 | tf_op jit(solution)/shard_map/ppermute | solution.py:68
  650.9 155.6 %collective-permute-start.9 = (bf16[1024,352]{0,1:T(8,128)(2,1)}, bf16[1024,352]{0,1:T(8,128)(2,1)}, u32[]{:S(2)}, u32[]{:S(2)}) collective-permute-start(bf16[1024,352]{0,1:T(8,128)(2,1)} %dynamic-slice_convert_fusion.1), channel_id=1, source_target_pairs={{0,16},{16,0},{1,17},{17,1},{2,18},{18,2},{3,19},{19,3},{4,20},{20... | collective-permute-start | bytes 2162696 | tf_op jit(solution)/shard_map/ppermute | solution.py:68
  670.9 10.0 %copy-start.4 = (f32[2048,48]{1,0:T(8,128)S(1)}, f32[2048,48]{1,0:T(8,128)}, u32[]{:S(2)}) copy-start(f32[2048,48]{1,0:T(8,128)} %copy-done.3) | copy-start | bytes 1179652
  670.9 10.0 %copy-start.23 = (f32[2048,1]{1,0:T(8,128)S(1)}, f32[2048,1]{1,0:T(8,128)}, u32[]{:S(2)}) copy-start(f32[2048,1]{1,0:T(8,128)} %copy.232) | copy-start | bytes 24580
  670.9 10.3 %copy-start.24 = (f32[2048,16]{1,0:T(8,128)S(1)}, f32[2048,16]{1,0:T(8,128)}, u32[]{:S(2)}) copy-start(f32[2048,16]{1,0:T(8,128)} %copy.249) | copy-start | bytes 393220
  679.0 172.8 %collective-permute-start.12 = (bf16[1024,1408]{1,0:T(8,128)(2,1)}, bf16[1024,1408]{1,0:T(8,128)(2,1)}, u32[]{:S(2)}, u32[]{:S(2)}) collective-permute-start(bf16[1024,1408]{1,0:T(8,128)(2,1)} %convolution_convert_fusion), channel_id=1, source_target_pairs={{0,16},{16,0},{1,17},{17,1},{2,18},{18,2},{3,19},{19,3},{4,20},{20... | collective-permute-start | bytes 8650760 | tf_op jit(solution)/shard_map/ppermute | solution.py:68
  686.5 93.4 %copy-start.52 = (f32[2048]{0:T(1024)S(1)}, f32[2048]{0:T(1024)}, u32[]{:S(2)}) copy-start(f32[2048]{0:T(1024)} %get-tuple-element.164) | copy-start | bytes 24580
  795.5 7.3 collective-permute-start.8
  800.9 160.8 %collective-permute-start.13 = (bf16[704,2048]{1,0:T(8,128)(2,1)}, bf16[704,2048]{1,0:T(8,128)(2,1)}, u32[]{:S(2)}, u32[]{:S(2)}) collective-permute-start(bf16[704,2048]{1,0:T(8,128)(2,1)} %convolution_convert_fusion.4), channel_id=1, source_target_pairs={{0,16},{16,0},{1,17},{17,1},{2,18},{18,2},{3,19},{19,3},{4,20},{20... | collective-permute-start | bytes 8650760 | tf_op jit(solution)/shard_map/ppermute | solution.py:68
  802.9 149.0 %collective-permute-start.11 = (bf16[1024,1408]{1,0:T(8,128)(2,1)}, bf16[1024,1408]{1,0:T(8,128)(2,1)}, u32[]{:S(2)}, u32[]{:S(2)}) collective-permute-start(bf16[1024,1408]{1,0:T(8,128)(2,1)} %convolution_convert_fusion.1), channel_id=1, source_target_pairs={{0,16},{16,0},{1,17},{17,1},{2,18},{18,2},{3,19},{19,3},{4,20},{20... | collective-permute-start | bytes 8650760 | tf_op jit(solution)/shard_map/ppermute | solution.py:68
  809.6 23.9 %all-to-all-start.2 = ((bf16[16,64,352]{2,1,0:T(8,128)(2,1)}), bf16[16,64,352]{2,1,0:T(8,128)(2,1)S(1)}, u32[]{:S(2)}, u32[]{:S(2)}) async-start(bf16[16,64,352]{2,1,0:T(8,128)(2,1)} %bitcast.207), calls=%async_computation.3 | async-start | bytes 1572864 | tf_op jit(solution)/shard_map/all_to_all | solution.py:108
  825.0 119.7 %collective-permute-start.7 = (bf16[1024,384]{0,1:T(8,128)(2,1)}, bf16[1024,384]{0,1:T(8,128)(2,1)}, u32[]{:S(2)}, u32[]{:S(2)}) collective-permute-start(bf16[1024,384]{0,1:T(8,128)(2,1)} %dynamic-slice_convert_fusion), channel_id=1, source_target_pairs={{0,16},{16,0},{1,17},{17,1},{2,18},{18,2},{3,19},{19,3},{4,20},{20... | collective-permute-start | bytes 2359304 | tf_op jit(solution)/shard_map/ppermute | solution.py:68
  851.8 92.8 %copy-start.12 = (f32[2048,384]{0,1:T(8,128)S(1)}, f32[2048,384]{0,1:T(8,128)}, u32[]{:S(2)}) copy-start(f32[2048,384]{0,1:T(8,128)} %copy-done.11) | copy-start | bytes 9437188
  947.2 24.7 %all-to-all-start.1 = ((bf16[16,64,384]{2,1,0:T(8,128)(2,1)}), bf16[16,64,384]{2,1,0:T(8,128)(2,1)S(1)}, u32[]{:S(2)}, u32[]{:S(2)}) async-start(bf16[16,64,384]{2,1,0:T(8,128)(2,1)} %bitcast.206), calls=%async_computation.2 | async-start | bytes 1572864 | tf_op jit(solution)/shard_map/all_to_all | solution.py:108
  951.9 9.8 copy-start.10
  (40 other events, 198.0 us)
Sparse Core Ops, SparseCore 0:
  10.2 110.4 all-gather.5
  123.4 83.6 all-gather.3
  557.2 79.9 all-gather.7
  641.1 127.7 reduce-scatter.1
